TPU v7x, 32 devices: a whole 2x2x4 slice. The times are simulated.
32 devices in a mesh: seg: 16 (over z, y, x), slab: 2 (over core).
Axes of the slice: x: 2, y: 2, z: 4, core: 2. Of those that a mesh axis runs over, the one named last changes fastest.
Arguments:
- block: float32 [16, 4, 16, 4096], P('seg', None, 'slab'), may hold values from -6 to 6
- base_velocity: bfloat16 [16, 8, 2, 16, 4096], P('seg', None, None, 'slab'), may hold values from -6 to 6
Outputs:
- new_block: float32 [16, 4, 16, 4096], P('seg', None, 'slab')
All inputs are finite; a program needn't handle non-finite values.
Results may differ from a plain program's by a relative error of at most 0.0003.
Values may be sent and summed in bfloat16 or wider, within the bound.
No kernel may reach another device: no remote copies, remote signals or barrier semaphores. Data moves between devices by JAX's collectives and lax.ppermute only.
A program may use at most 64 MiB of HBM per device.

v0:
```python
import jax
import jax.numpy as jnp
from jax import lax
from jax.sharding import PartitionSpec as P

HOPS = 4


def with_halo(shard, sides, width):
    for axis, dim in sides:
        size, length = (lax.axis_size(axis), shard.shape[dim])
        up = [(i, (i + 1) % size) for i in range(size)]
        down = [(j, i) for i, j in up]
        last = lax.slice_in_dim(shard, length - width, length, axis=dim)
        first = lax.slice_in_dim(shard, 0, width, axis=dim)
        before = lax.ppermute(last, axis, up)
        after = lax.ppermute(first, axis, down)
        shard = jnp.concatenate([before, shard, after], axis=dim)
    return shard


def shifted(block, axis, distance):
    devices = range(lax.axis_size(axis))
    route = [((i - distance) % len(devices), i) for i in devices]
    return lax.ppermute(block, axis, route)


def advance(padded, velocity):
    centre = padded[:, 1:-1]
    up = padded[:, 2:]
    down = padded[:, :-2]
    east = jnp.roll(centre, -1, 2)
    west = jnp.roll(centre, 1, 2)
    speed_x = velocity[0].astype(jnp.float32)
    speed_y = velocity[1].astype(jnp.float32)
    return (
        centre
        + 0.2 * (up + down + east + west - 4.0 * centre)
        - 0.05 * (speed_x * (east - west) + speed_y * (up - down))
        - 0.02 * centre
    )


def lower_inverse(lower):
    count = lower.shape[0]
    rows = []
    for i in range(count):
        entries = []
        for j in range(count):
            if j > i:
                entries.append(jnp.zeros((), jnp.float32))
            elif j == i:
                entries.append(1.0 / lower[i, i])
            else:
                total = jnp.zeros((), jnp.float32)
                for k in range(j, i):
                    total = total + lower[i, k] * rows[k][j]
                entries.append(-total / lower[i, i])
        rows.append(entries)
    return jnp.stack([jnp.stack(r) for r in rows])


def shards(block, base_velocity):
    vectors = block[0]
    velocity = base_velocity[0]
    depth = velocity.shape[0]
    velocity_wide = with_halo(velocity, (("slab", 2),), depth)
    for hop in range(HOPS):
        moved = with_halo(vectors, (("slab", 1),), depth)
        for j in range(depth):
            height = velocity_wide.shape[2]
            moved = advance(moved, velocity_wide[j][:, j + 1 : height - j - 1])
        arrived = shifted(moved, "seg", 1)
        residual = arrived - vectors
        local_gram = jnp.einsum("ayx,byx->ab", residual, residual, precision=lax.Precision.HIGHEST)
        gram = lax.psum(local_gram, ("seg", "slab"))
        inverse = lower_inverse(jnp.linalg.cholesky(gram))
        vectors = jnp.einsum("ab,byx->ayx", inverse, residual, precision=lax.Precision.HIGHEST)
    return vectors[None]


def solution(mesh):
    placed = (P("seg", None, "slab", None), P("seg", None, None, "slab", None))
    return jax.shard_map(
        shards, mesh=mesh, in_specs=placed, out_specs=P("seg", None, "slab", None), check_vma=False
    )
```

profile of v0, /device:TPU:0, one launch (start us, length us, event | category | flops | bytes accessed | tf_op | source)
XLA Modules:
  0.0 402.6 jit_solution(13128962922173816920)
XLA Ops:
  8.0 3.8 multiply_subtract_fusion.3
  26.7 3.5 collective-permute-start.4
  30.2 16.2 %collective-permute-done.4 = f32[4,8,4096]{2,0,1:T(4,128)S(1)} collective-permute-done((f32[4,8,4096]{2,0,1:T(4,128)S(1)}, f32[4,8,4096]{2,0,1:T(4,128)S(1)}, u32[]{:S(2)}, u32[]{:S(2)}) %collective-permute-start.4) | collective-permute-done | bytes 524320 | tf_op jit(solution)/shard_map/ppermute | solution.py:25
  47.2 2.3 convolution_bitcast_fusion.4
  49.6 37.5 %psum.28 = f32[4,4]{0,1:T(4,128)S(1)} all-reduce(f32[4,4]{0,1:T(4,128)S(1)} %convolution_bitcast_fusion.4), channel_id=1, replica_groups=mesh['seg'=16,'slab'=2] {'seg','slab'}, use_global_device_ids=true, to_apply=%region_0.1 | all-reduce | flops 16 | bytes 128 | tf_op jit(solution)/shard_map/psum | solution.py:76
  102.4 2.5 fusion.24
  109.0 3.5 multiply_subtract_fusion.2
  113.5 2.1 multiply_subtract_fusion.6
  128.5 2.3 collective-permute-start.7
  130.8 15.3 %collective-permute-done.7 = f32[4,8,4096]{2,0,1:T(4,128)S(1)} collective-permute-done((f32[4,8,4096]{2,0,1:T(4,128)S(1)}, f32[4,8,4096]{2,0,1:T(4,128)S(1)}, u32[]{:S(2)}, u32[]{:S(2)}) %collective-permute-start.7) | collective-permute-done | bytes 524320 | tf_op jit(solution)/shard_map/ppermute | solution.py:25
  146.2 2.3 convolution_bitcast_fusion.3
  148.6 38.1 %psum.29 = f32[4,4]{0,1:T(4,128)S(1)} all-reduce(f32[4,4]{0,1:T(4,128)S(1)} %convolution_bitcast_fusion.3), channel_id=1, replica_groups=mesh['seg'=16,'slab'=2] {'seg','slab'}, use_global_device_ids=true, to_apply=%region_3.5 | all-reduce | flops 16 | bytes 128 | tf_op jit(solution)/shard_map/psum | solution.py:76
  207.9 3.5 multiply_subtract_fusion.1
  212.3 2.1 multiply_subtract_fusion.5
  228.1 2.3 collective-permute-start.10
  230.5 15.3 %collective-permute-done.10 = f32[4,8,4096]{2,0,1:T(4,128)S(1)} collective-permute-done((f32[4,8,4096]{2,0,1:T(4,128)S(1)}, f32[4,8,4096]{2,0,1:T(4,128)S(1)}, u32[]{:S(2)}, u32[]{:S(2)}) %collective-permute-start.10) | collective-permute-done | bytes 524320 | tf_op jit(solution)/shard_map/ppermute | solution.py:25
  245.9 2.3 convolution_bitcast_fusion.2
  248.2 37.4 %psum.30 = f32[4,4]{0,1:T(4,128)S(1)} all-reduce(f32[4,4]{0,1:T(4,128)S(1)} %convolution_bitcast_fusion.2), channel_id=1, replica_groups=mesh['seg'=16,'slab'=2] {'seg','slab'}, use_global_device_ids=true, to_apply=%region_4.6 | all-reduce | flops 16 | bytes 128 | tf_op jit(solution)/shard_map/psum | solution.py:76
  306.8 3.5 multiply_subtract_fusion
  311.3 2.1 multiply_subtract_fusion.4
  326.8 2.3 collective-permute-start.13
  329.1 15.3 %collective-permute-done.13 = f32[4,8,4096]{2,0,1:T(4,128)S(1)} collective-permute-done((f32[4,8,4096]{2,0,1:T(4,128)S(1)}, f32[4,8,4096]{2,0,1:T(4,128)S(1)}, u32[]{:S(2)}, u32[]{:S(2)}) %collective-permute-start.13) | collective-permute-done | bytes 524320 | tf_op jit(solution)/shard_map/ppermute | solution.py:25
  344.6 2.3 convolution_bitcast_fusion.1
  346.9 38.2 %psum.31 = f32[4,4]{0,1:T(4,128)S(1)} all-reduce(f32[4,4]{0,1:T(4,128)S(1)} %convolution_bitcast_fusion.1), channel_id=1, replica_groups=mesh['seg'=16,'slab'=2] {'seg','slab'}, use_global_device_ids=true, to_apply=%region_5.7 | all-reduce | flops 16 | bytes 128 | tf_op jit(solution)/shard_map/psum | solution.py:76
  (225 shorter events, 93.8 us)
Async XLA Ops:
  1.4 2.1 collective-permute-start.1
  1.9 2.3 collective-permute-start
  2.0 3.7 collective-permute-start.3
  2.5 4.8 %collective-permute-start.2 = (bf16[8,2,8,4096]{3,2,1,0:T(8,128)(2,1)}, bf16[8,2,8,4096]{3,2,1,0:T(8,128)(2,1)S(1)}, u32[]{:S(2)}, u32[]{:S(2)}) collective-permute-start(bf16[8,2,8,4096]{3,2,1,0:T(8,128)(2,1)} %bitcast.228), channel_id=1, source_target_pairs={{0,1},{1,0},{2,3},{3,2},{4,5},{5,4},{6,7},{7,6},{8,9},{9,8},{10,11... | collective-permute-start | bytes 3145736 | tf_op jit(solution)/shard_map/ppermute | solution.py:16
  4.8 2.4 copy-start.28
  18.5 1.6 copy-start.14
  18.5 1.6 copy-start.18
  23.0 100.8 %copy-start = (f32[12,4096]{1,0:T(8,128)}, f32[12,4096]{1,0:T(8,128)S(1)}, u32[]{:S(2)}) copy-start(f32[12,4096]{1,0:T(8,128)S(1)} %get-tuple-element.138) | copy-start | bytes 589828
  23.0 100.8 %copy-start.3 = (f32[12,4096]{1,0:T(8,128)}, f32[12,4096]{1,0:T(8,128)S(1)}, u32[]{:S(2)}) copy-start(f32[12,4096]{1,0:T(8,128)S(1)} %get-tuple-element.139) | copy-start | bytes 589828
  26.0 21.2 %copy-start.22 = (f32[1,4,8,4096]{3,2,1,0:T(8,128)S(1)}, f32[1,4,8,4096]{3,2,1,0:T(8,128)}, u32[]{:S(2)}) copy-start(f32[1,4,8,4096]{3,2,1,0:T(8,128)} %param.3) | copy-start | bytes 1572868
  26.7 19.7 %collective-permute-start.4 = (f32[4,8,4096]{2,0,1:T(4,128)S(1)}, f32[4,8,4096]{2,0,1:T(4,128)S(1)}, u32[]{:S(2)}, u32[]{:S(2)}) collective-permute-start(f32[4,8,4096]{2,0,1:T(4,128)S(1)} %multiply_subtract_fusion.31), channel_id=1, source_target_pairs={{30,0},{0,2},{2,4},{4,6},{6,8},{8,10},{10,12},{12,14},{14,16},{16,... | collective-permute-start | bytes 1572872 | tf_op jit(solution)/shard_map/ppermute | solution.py:25
  104.8 2.0 collective-permute-start.6
  104.9 2.6 collective-permute-start.5
  118.3 1.0 copy-start.19
  128.5 17.6 %collective-permute-start.7 = (f32[4,8,4096]{2,0,1:T(4,128)S(1)}, f32[4,8,4096]{2,0,1:T(4,128)S(1)}, u32[]{:S(2)}, u32[]{:S(2)}) collective-permute-start(f32[4,8,4096]{2,0,1:T(4,128)S(1)} %multiply_subtract_fusion.30), channel_id=1, source_target_pairs={{30,0},{0,2},{2,4},{4,6},{6,8},{8,10},{10,12},{12,14},{14,16},{16,... | collective-permute-start | bytes 1572872 | tf_op jit(solution)/shard_map/ppermute | solution.py:25
  203.7 2.0 collective-permute-start.9
  203.8 2.6 collective-permute-start.8
  217.2 1.0 copy-start.20
  222.5 1.0 copy-start.4
  228.1 17.6 %collective-permute-start.10 = (f32[4,8,4096]{2,0,1:T(4,128)S(1)}, f32[4,8,4096]{2,0,1:T(4,128)S(1)}, u32[]{:S(2)}, u32[]{:S(2)}) collective-permute-start(f32[4,8,4096]{2,0,1:T(4,128)S(1)} %multiply_subtract_fusion.29), channel_id=1, source_target_pairs={{30,0},{0,2},{2,4},{4,6},{6,8},{8,10},{10,12},{12,14},{14,16},{16,... | collective-permute-start | bytes 1572872 | tf_op jit(solution)/shard_map/ppermute | solution.py:25
  302.6 2.0 collective-permute-start.12
  302.7 2.6 collective-permute-start.11
  316.1 1.0 copy-start.21
  326.8 17.6 %collective-permute-start.13 = (f32[4,8,4096]{2,0,1:T(4,128)S(1)}, f32[4,8,4096]{2,0,1:T(4,128)S(1)}, u32[]{:S(2)}, u32[]{:S(2)}) collective-permute-start(f32[4,8,4096]{2,0,1:T(4,128)S(1)} %multiply_subtract_fusion.28), channel_id=1, source_target_pairs={{30,0},{0,2},{2,4},{4,6},{6,8},{8,10},{10,12},{12,14},{14,16},{16,... | collective-permute-start | bytes 1572872 | tf_op jit(solution)/shard_map/ppermute | solution.py:25
  (19 other events, 17.8 us)
where the time goes:
time: 407 us; the launch traced here: 403 us
  blocking collectives  151 us (37%)
  waiting for transfers between devices  71.7 us (18%)
  other arithmetic  65.1 us (16%)
  between operations  52.8 us (13%)
  local copies, waits for them, and re-layouts  33.8 us (8%)
  matrix products  14.7 us (4%)
  starting transfers between devices  13.3 us (3%)
    psum x4, blocking collectives, shards(): gram = lax.psum(local_gram, ('seg', 'slab'))  151 us
    ppermute x4, waiting for transfers between devices, shifted(): return lax.ppermute(block, axis, route)  62.1 us
    sub x32, other arithmetic, advance(): centre + 0.2 * (up + down + east + west - 4.0 * centre)  53.8 us
    slice x60, local copies, waits for them, and re-layouts, advance(): east = jnp.roll(centre, -1, 2)  21.5 us
    ppermute x4, starting transfers between devices, shifted(): return lax.ppermute(block, axis, route)  10.5 us
    dot_general x4, matrix products, shards(): jnp.einsum('ayx,byx->ab', residual, residual, precision=lax.Precision.HIG...  9.32 us
  transfers between devices with their start and end apart: 14, of which 13 were waited for; matrix products, arithmetic and copies ran while one was open for 0% of the time, Pallas kernels for 0%

commit v1 on v0

v1 whole, which is shorter than its diff:
```python
import functools

import jax
import jax.numpy as jnp
from jax import lax
from jax.experimental import pallas as pl
from jax.experimental.pallas import tpu as pltpu
from jax.sharding import PartitionSpec as P

HOPS = 4
SUB = 8
LANE = 128
VMEM = pl.BlockSpec(memory_space=pltpu.VMEM)


def tiled(rows):
    lead, (height, width) = rows.shape[:-2], rows.shape[-2:]
    cut = rows.reshape(lead + (height, width // LANE, LANE))
    return jnp.swapaxes(cut, -3, -2)


def untiled(tiles):
    lead, (count, height, lane) = tiles.shape[:-3], tiles.shape[-3:]
    return jnp.swapaxes(tiles, -3, -2).reshape(lead + (height, count * lane))


def propagate_kernel(pieces, index, subtract, keep, apart, *refs):
    def take(count):
        nonlocal refs
        taken, refs = refs[:count], refs[count:]
        return taken

    def pick(group, piece):
        return group[piece].at[0] if len(group) > 1 or pieces == 1 else group[0].at[piece]

    velocity = take(pieces)
    if subtract:
        previous, arrived = take(1), take(1)
        start_out = take(pieces if apart else 1)
    else:
        previous = take(pieces)
    moved = take(keep if apart else 1)
    ping, pong = refs
    depth, _, columns, height, _ = velocity[0].shape
    rows = pieces * height
    lane = lax.broadcasted_iota(jnp.int32, (SUB, LANE), 1)
    first, last = lane == 0, lane == LANE - 1
    blocks = range(rows // SUB)

    def place(ref, j, b, value):
        ref[j, pl.ds(SUB + SUB * b, SUB), :] = value
        if b == blocks[0]:
            ref[j, pl.ds(SUB + rows, 1), :] = value[:1]
        if b == blocks[-1]:
            ref[j, pl.ds(SUB - 1, 1), :] = value[SUB - 1 :]

    for j in range(columns):
        for b in blocks:
            piece, at = divmod(SUB * b, height)
            at = pl.ds(at, SUB)
            if subtract:
                value = pick(arrived, piece)[j, at, :] - pick(previous, piece)[j, at, :]
                pick(start_out, piece)[j, at, :] = value
            else:
                value = previous[piece][index, j, at, :]
            place(ping, j, b, value)

    def step(k, source, write):
        for b in blocks:
            piece, at = divmod(SUB * b, height)
            rows_at = pl.ds(SUB + SUB * b, SUB)
            here = [source[j % columns, rows_at, :] for j in (-1, 0, 1)]
            for j in range(columns):
                left, centre, right = here
                west = pltpu.roll(jnp.where(last, left, centre), 1, 1)
                east = pltpu.roll(jnp.where(first, right, centre), LANE - 1, 1)
                up = source[j, pl.ds(SUB + 1 + SUB * b, SUB), :]
                down = source[j, pl.ds(SUB - 1 + SUB * b, SUB), :]
                speed_x = velocity[piece][k, 0, j, pl.ds(at, SUB), :].astype(jnp.float32)
                speed_y = velocity[piece][k, 1, j, pl.ds(at, SUB), :].astype(jnp.float32)
                carried = speed_x * (west - east) + speed_y * (down - up)
                write(j, b, 0.9 * centre + ((west + east) + (up + down)) + 0.25 * carried)
                here = [centre, right, source[(j + 2) % columns, rows_at, :]]

    def pair(i, carry):
        step(2 * i, ping, functools.partial(place, pong))
        step(2 * i + 1, pong, functools.partial(place, ping))
        return carry

    lax.fori_loop(0, (depth - 1) // 2, pair, 0)
    source = ping
    if depth % 2 == 0:
        step(depth - 2, ping, functools.partial(place, pong))
        source = pong
    scale = 0.2**depth

    def finish(j, b, value):
        piece, at = divmod(SUB * b, height)
        if piece < keep:
            pick(moved, piece)[j, pl.ds(at, SUB), :] = scale * value

    step(depth - 1, source, finish)


def propagate(velocity, previous, index=0, arrived=None, keep=None, apart=False):
    pieces = len(velocity)
    keep = pieces if keep is None else keep
    _, _, columns, height, lane = velocity[0].shape

    def shapes(count):
        parts = [1] * count if apart else [count]
        return [jax.ShapeDtypeStruct((n, columns, height, lane), jnp.float32) for n in parts]

    subtract = arrived is not None
    outs = (shapes(pieces) if subtract else []) + shapes(keep)
    scratch = pltpu.VMEM((columns, pieces * height + 2 * SUB, lane), jnp.float32)
    args = [*velocity] + ([previous, arrived] if subtract else [*previous])
    out = pl.pallas_call(
        functools.partial(propagate_kernel, pieces, index, subtract, keep, apart),
        out_shape=outs,
        in_specs=[VMEM] * len(args),
        out_specs=[VMEM] * len(outs),
        scratch_shapes=[scratch, scratch],
        compiler_params=pltpu.CompilerParams(vmem_limit_bytes=16 << 20),
        name="propagate",
    )(*args)
    if apart:
        return out[:pieces], out[pieces:]
    return out if subtract else out[0]


def gram_kernel(arrived_count, *refs):
    base = refs[0]
    groups = [(refs[1 + i], refs[1 + arrived_count + i]) for i in range(arrived_count)]
    residual, gram = refs[1 + 2 * arrived_count :]
    count, columns, height, _ = residual.shape
    size = [a.shape[0] for a, _ in groups]
    shift = base[0]
    sums = {}
    for j in range(columns):
        for at in range(0, height, SUB):
            values = []
            for (a, s), n in zip(groups, size):
                for i in range(n):
                    values.append(a[i, j, pl.ds(at, SUB), :] - s[i, j, pl.ds(at, SUB), :])
            for p in range(count):
                residual[p, j, pl.ds(at, SUB), :] = values[p]
                for q in range(p + 1):
                    term = values[p] * values[q]
                    sums[p, q] = term if (p, q) not in sums else sums[p, q] + term
    for (p, q), total in sums.items():
        line = jnp.sum(total, axis=0, keepdims=True)
        a, b = lax.rem(shift + p, count), lax.rem(shift + q, count)
        gram[pl.ds(a * count + b, 1), :] = line
        if p != q:
            gram[pl.ds(b * count + a, 1), :] = line


def local_gram(shift, arrived, start):
    count = sum(a.shape[0] for a in arrived)
    shape = (count,) + arrived[0].shape[1:]
    return pl.pallas_call(
        functools.partial(gram_kernel, len(arrived)),
        out_shape=[jax.ShapeDtypeStruct(shape, jnp.float32), jax.ShapeDtypeStruct((count * count, LANE), jnp.float32)],
        in_specs=[pl.BlockSpec(memory_space=pltpu.SMEM)] + [VMEM] * (2 * len(arrived)),
        out_specs=[VMEM, VMEM],
        compiler_params=pltpu.CompilerParams(vmem_limit_bytes=16 << 20),
        name="gram",
    )(shift, *arrived, *start)


def solve_kernel(base, gram, residual, out):
    count, columns, height, lane = residual.shape
    total = jnp.sum(gram[...], axis=1, keepdims=True)
    entry = lambda a, b: total[a * count + b : a * count + b + 1, :]
    lower, inverse = {}, {}
    for a in range(count):
        for b in range(a + 1):
            value = entry(a, b)
            for k in range(b):
                value = value - lower[a, k] * lower[b, k]
            lower[a, b] = jnp.sqrt(value) if a == b else value / lower[b, b]
    for a in range(count):
        inverse[a, a] = 1.0 / lower[a, a]
        for b in range(a):
            value = lower[a, b] * inverse[b, b]
            for k in range(b + 1, a):
                value = value + lower[a, k] * inverse[k, b]
            inverse[a, b] = -value / lower[a, a]
    factors = {at: jnp.broadcast_to(value, (SUB, lane)) for at, value in inverse.items()}
    place = [lax.rem(a + count - base[0], count) for a in range(count)]
    for j in range(columns):
        for at in range(0, height, SUB):
            values = [residual[place[a], j, pl.ds(at, SUB), :] for a in range(count)]
            for a in range(count):
                value = factors[a, 0] * values[0]
                for b in range(1, a + 1):
                    value = value + factors[a, b] * values[b]
                out[a, j, pl.ds(at, SUB), :] = value


def solved(shift, gram, residual):
    return pl.pallas_call(
        solve_kernel,
        out_shape=jax.ShapeDtypeStruct(residual.shape, jnp.float32),
        in_specs=[pl.BlockSpec(memory_space=pltpu.SMEM), VMEM, VMEM],
        out_specs=VMEM,
        compiler_params=pltpu.CompilerParams(vmem_limit_bytes=16 << 20),
        name="solve",
    )(shift, gram, residual)


def summed(value, axes):
    count = 1
    for axis in axes:
        count *= lax.axis_size(axis)
    if count & (count - 1):
        return lax.psum(value, axes)
    distance = 1
    while distance < count:
        value = value + lax.ppermute(value, axes, [(i, i ^ distance) for i in range(count)])
        distance *= 2
    return value


def from_slab(value, distance):
    size = lax.axis_size("slab")
    return lax.ppermute(value, "slab", [((i + distance) % size, i) for i in range(size)])


def to_next(value, turn=0):
    segs, slabs = lax.axis_size("seg"), lax.axis_size("slab")
    route = []
    for s in range(segs):
        for c in range(slabs):
            route.append((s * slabs + c, (s + 1) % segs * slabs + (c + turn) % slabs))
    return lax.ppermute(value, ("seg", "slab"), route)


def split_vectors(vectors, velocity):
    slabs, mine = lax.axis_size("slab"), lax.axis_index("slab")
    share = vectors.shape[0] // slabs

    def part(distance):
        at = lax.rem(mine + distance, slabs) * share
        return lax.dynamic_slice_in_dim(vectors, at, share, 0)

    start, speeds = [part(0)], [velocity]
    for d in range(1, slabs):
        start.append(from_slab(part(slabs - d), d))
        speeds.append(from_slab(velocity, d))
    moved = [propagate(speeds, start, i) for i in range(share)]
    previous = [jnp.concatenate([part[i : i + 1] for part in start], 0) for i in range(share)]
    for hop in range(1, HOPS):
        for i in range(share):
            final = hop + 1 == HOPS
            previous[i], moved[i] = propagate(speeds, previous[i], 0, to_next(moved[i]), None, final)
    arrived, begun = [], []
    for d in range(slabs):
        for i in range(share):
            at = (slabs - d) % slabs
            arrived.append(to_next(moved[i][at], at))
            begun.append(from_slab(previous[i][at], d) if d else previous[i][0])
    shift = jnp.full((1,), mine * share, jnp.int32)
    return shift, arrived, begun


def split_rows(vectors, velocity):
    depth, height = velocity.shape[0], vectors.shape[2]

    def pieces(value):
        after = value[..., :depth, :]
        before = value[..., height - depth :, :]
        return [value, from_slab(after, 1), from_slab(before, -1)]

    speeds = pieces(velocity)
    begun = vectors
    for hop in range(HOPS):
        state = pieces(begun)
        arrived = [to_next(propagate(speeds, state, i, keep=1)) for i in range(vectors.shape[0])]
        if hop + 1 < HOPS:
            begun = jnp.concatenate(arrived, 0) - begun
    return jnp.zeros((1,), jnp.int32), arrived, [begun[i : i + 1] for i in range(vectors.shape[0])]


def shards(block, base_velocity):
    vectors, velocity = tiled(block[0]), tiled(base_velocity[0])
    even = vectors.shape[0] % lax.axis_size("slab") == 0
    shift, arrived, begun = (split_vectors if even else split_rows)(vectors, velocity)
    residual, gram = local_gram(shift, arrived, begun)
    gram = summed(gram, ("seg", "slab"))
    return untiled(solved(shift, gram, residual))[None]


def solution(mesh):
    placed = (P("seg", None, "slab", None), P("seg", None, None, "slab", None))
    return jax.shard_map(
        shards, mesh=mesh, in_specs=placed, out_specs=P("seg", None, "slab", None), check_vma=False
    )
```

time: 407 us -> 80.2 us (0.20); the launches traced: 403 us -> 80.1 us
  blocking collectives: 151 us -> 0 us
  other arithmetic: 65.1 us -> 0.07 us
  between operations: 52.8 us -> 0.16 us
  local copies, waits for them, and re-layouts: 33.8 us -> 1.1 us
  matrix products: 14.7 us -> 0 us
  Pallas kernels: 0 us -> 12.6 us
  waiting for transfers between devices: 71.7 us -> 59.2 us
  starting transfers between devices: 13.3 us -> 6.94 us
    psum x4 -> x0, blocking collectives: 151 us -> none  [shards(): gram = lax.psum(local_gram, ('seg', 'slab'))]
    sub x35 -> x0, other arithmetic: 54.2 us -> none  [the longest x32 53.8 us: advance(): centre + 0.2 * (up + down + east + west - 4.0 * centre)]
    slice x64 -> x2, local copies, waits for them, and re-layouts: 24.3 us -> 0.04 us  [split_vectors(): part[i:i + 1]]
    dot_general x8 -> x0, matrix products: 14.7 us -> none  [the longest x4 9.32 us: shards(): jnp.einsum('ayx,byx->ab', residual, residual, precision=lax.Precision.HIG...]
    pallas_call x0 -> x10, Pallas kernels: none -> 12.6 us  [the longest x8 11.4 us: propagate(): pl.pallas_call(functools.partial(propagate_kernel, pieces, index, subtrac...]
    ppermute x14 -> x19, waiting for transfers between devices: 71.7 us -> 59.2 us  [the longest x10 41.2 us: to_next(): return lax.ppermute(value, ('seg', 'slab'), route)]
    unnamed x59 -> x2, local copies, waits for them, and re-layouts: 7.76 us -> 0.01 us
    ppermute x14 -> x19, starting transfers between devices: 13.3 us -> 6.94 us  [the longest x10 4.91 us: to_next(): return lax.ppermute(value, ('seg', 'slab'), route)]
  transfers between devices with their start and end apart: 14 -> 19, of which waited for: 13 -> 14; matrix products, arithmetic and copies ran while one was open for 0% -> 1% of each run, Pallas kernels for 0% -> 13%
where the time goes in v1:
time: 80.2 us; the launch traced here: 80.1 us
  waiting for transfers between devices  59.2 us (74%)
  Pallas kernels  12.6 us (16%)
  starting transfers between devices  6.94 us (9%)
  local copies, waits for them, and re-layouts  1.1 us (1%)
    ppermute x10, waiting for transfers between devices, to_next(): return lax.ppermute(value, ('seg', 'slab'), route)  41.2 us
    ppermute x5, waiting for transfers between devices, summed(): lax.ppermute(value, axes, [(i, i ^ distance) for i in range(count)])  16.3 us
    pallas_call x8, Pallas kernels, propagate(): pl.pallas_call(functools.partial(propagate_kernel, pieces, index, subtrac...  11.4 us
    ppermute x10, starting transfers between devices, to_next(): return lax.ppermute(value, ('seg', 'slab'), route)  4.91 us
    ppermute x4, waiting for transfers between devices, from_slab(): lax.ppermute(value, 'slab', [((i + distance) % size, i) for i in range(si...  1.62 us
  transfers between devices with their start and end apart: 19, of which 14 were waited for; matrix products, arithmetic and copies ran while one was open for 1% of the time, Pallas kernels for 13%

profile of v1, /device:TPU:0, one launch (start us, length us, event | category | flops | bytes accessed | tf_op | source)
XLA Modules:
  0.0 80.1 jit_solution(97912962854413058)
XLA Ops:
  1.8 1.6 %collective-permute-done.1.refs_3_ = f32[2,32,8,128]{3,2,1,0:T(8,128)S(1)} collective-permute-done((f32[2,32,8,128]{3,2,1,0:T(8,128)S(1)}, f32[2,32,8,128]{3,2,1,0:T(8,128)S(1)}, u32[]{:S(2)}, u32[]{:S(2)}) %collective-permute-start.1) | collective-permute-done | bytes 262176 | tf_op jit(solution)/shard_map/ppermute | solution.py:228
  3.4 1.4 %propagate.8 = f32[2,32,8,128]{3,2,1,0:T(8,128)S(1)} custom-call(bf16[8,2,32,8,128]{4,3,2,1,0:T(8,128)(2,1)S(1)} %bitcast.13, bf16[8,2,32,8,128]{4,3,2,1,0:T(8,128)(2,1)S(1)} %collective-permute-done.refs_1_, f32[2,32,8,128]{3,2,1,0:T(8,128)S(1)} %get-tuple-element.41.refs_2_, f32[2,32,8,128]{3,2,1,0:T(8,128)S(1)} %collective-permute-done.1.refs_3_), custom_call_target="tpu_custom_call" | custom-call | tf_op jit(solution)/shard_map/propagate/pallas_call | solution.py:118
  4.8 2.9 %collective-permute-start.2 = (f32[2,32,8,128]{3,2,1,0:T(8,128)S(1)}, f32[2,32,8,128]{3,2,1,0:T(8,128)S(1)}, u32[]{:S(2)}, u32[]{:S(2)}) collective-permute-start(f32[2,32,8,128]{3,2,1,0:T(8,128)S(1)} %propagate.8), channel_id=1, source_target_pairs={{0,2},{1,3},{2,4},{3,5},{4,6},{5,7},{6,8},{7,9},{8,10},{9,11},{10,... | collective-permute-start | bytes 786440 | tf_op jit(solution)/shard_map/ppermute | solution.py:237
  7.7 1.4 %propagate.12 = f32[2,32,8,128]{3,2,1,0:T(8,128)S(1)} custom-call(bf16[8,2,32,8,128]{4,3,2,1,0:T(8,128)(2,1)S(1)} %bitcast.14, bf16[8,2,32,8,128]{4,3,2,1,0:T(8,128)(2,1)S(1)} %collective-permute-done.refs_1_, f32[2,32,8,128]{3,2,1,0:T(8,128)S(1)} %get-tuple-element.41.refs_2_, f32[2,32,8,128]{3,2,1,0:T(8,128)S(1)} %collective-permute-done.1.refs_3_), custom_call_target="tpu_custom_call" | custom-call | tf_op jit(solution)/shard_map/propagate/pallas_call | solution.py:118
  9.1 1.5 %collective-permute-start.6 = (f32[2,32,8,128]{3,2,1,0:T(8,128)S(1)}, f32[2,32,8,128]{3,2,1,0:T(8,128)S(1)}, u32[]{:S(2)}, u32[]{:S(2)}) collective-permute-start(f32[2,32,8,128]{3,2,1,0:T(8,128)S(1)} %propagate.12), channel_id=1, source_target_pairs={{0,2},{1,3},{2,4},{3,5},{4,6},{5,7},{6,8},{7,9},{8,10},{9,11},{10,... | collective-permute-start | bytes 786440 | tf_op jit(solution)/shard_map/ppermute | solution.py:237
  10.7 8.1 %collective-permute-done.2.refs_3_ = f32[2,32,8,128]{3,2,1,0:T(8,128)S(1)} collective-permute-done((f32[2,32,8,128]{3,2,1,0:T(8,128)S(1)}, f32[2,32,8,128]{3,2,1,0:T(8,128)S(1)}, u32[]{:S(2)}, u32[]{:S(2)}) %collective-permute-start.2) | collective-permute-done | bytes 262176 | tf_op jit(solution)/shard_map/ppermute | solution.py:237
  18.8 1.4 %propagate.9 = (f32[2,32,8,128]{3,2,1,0:T(8,128)S(1)}, f32[2,32,8,128]{3,2,1,0:T(8,128)S(1)}) custom-call(bf16[8,2,32,8,128]{4,3,2,1,0:T(8,128)(2,1)S(1)} %bitcast.15, bf16[8,2,32,8,128]{4,3,2,1,0:T(8,128)(2,1)S(1)} %collective-permute-done.refs_1_, f32[2,32,8,128]{3,2,1,0:T(8,128)S(1)} %pad_maximum_fusion.refs_2_, ...), custom_call_target="tpu_custom_call" | custom-call | tf_op jit(solution)/shard_map/propagate/pallas_call | solution.py:118
  20.4 3.5 %collective-permute-done.6.refs_3_ = f32[2,32,8,128]{3,2,1,0:T(8,128)S(1)} collective-permute-done((f32[2,32,8,128]{3,2,1,0:T(8,128)S(1)}, f32[2,32,8,128]{3,2,1,0:T(8,128)S(1)}, u32[]{:S(2)}, u32[]{:S(2)}) %collective-permute-start.6) | collective-permute-done | bytes 262176 | tf_op jit(solution)/shard_map/ppermute | solution.py:237
  23.9 1.4 %propagate.13 = (f32[2,32,8,128]{3,2,1,0:T(8,128)S(1)}, f32[2,32,8,128]{3,2,1,0:T(8,128)S(1)}) custom-call(bf16[8,2,32,8,128]{4,3,2,1,0:T(8,128)(2,1)S(1)} %bitcast.16, bf16[8,2,32,8,128]{4,3,2,1,0:T(8,128)(2,1)S(1)} %collective-permute-done.refs_1_, f32[2,32,8,128]{3,2,1,0:T(8,128)S(1)} %pad_maximum_fusion.1.refs_2_, ...), custom_call_target="tpu_custom_call" | custom-call | tf_op jit(solution)/shard_map/propagate/pallas_call | solution.py:118
  25.4 5.7 %collective-permute-done.3.refs_3_ = f32[2,32,8,128]{3,2,1,0:T(8,128)S(1)} collective-permute-done((f32[2,32,8,128]{3,2,1,0:T(8,128)S(1)}, f32[2,32,8,128]{3,2,1,0:T(8,128)S(1)}, u32[]{:S(2)}, u32[]{:S(2)}) %collective-permute-start.3) | collective-permute-done | bytes 262176 | tf_op jit(solution)/shard_map/ppermute | solution.py:237
  31.2 1.4 %propagate.10 = (f32[2,32,8,128]{3,2,1,0:T(8,128)S(1)}, f32[2,32,8,128]{3,2,1,0:T(8,128)S(1)}) custom-call(bf16[8,2,32,8,128]{4,3,2,1,0:T(8,128)(2,1)S(1)} %bitcast.17, bf16[8,2,32,8,128]{4,3,2,1,0:T(8,128)(2,1)S(1)} %collective-permute-done.refs_1_, f32[2,32,8,128]{3,2,1,0:T(8,128)S(1)} %get-tuple-element.23.refs_2_, ...), custom_call_target="tpu_custom_call" | custom-call | tf_op jit(solution)/shard_map/propagate/pallas_call | solution.py:118
  32.7 4.1 %collective-permute-done.7.refs_3_ = f32[2,32,8,128]{3,2,1,0:T(8,128)S(1)} collective-permute-done((f32[2,32,8,128]{3,2,1,0:T(8,128)S(1)}, f32[2,32,8,128]{3,2,1,0:T(8,128)S(1)}, u32[]{:S(2)}, u32[]{:S(2)}) %collective-permute-start.7) | collective-permute-done | bytes 262176 | tf_op jit(solution)/shard_map/ppermute | solution.py:237
  36.8 1.4 %propagate.14 = (f32[2,32,8,128]{3,2,1,0:T(8,128)S(1)}, f32[2,32,8,128]{3,2,1,0:T(8,128)S(1)}) custom-call(bf16[8,2,32,8,128]{4,3,2,1,0:T(8,128)(2,1)S(1)} %bitcast.18, bf16[8,2,32,8,128]{4,3,2,1,0:T(8,128)(2,1)S(1)} %collective-permute-done.refs_1_, f32[2,32,8,128]{3,2,1,0:T(8,128)S(1)} %get-tuple-element.28.refs_2_, ...), custom_call_target="tpu_custom_call" | custom-call | tf_op jit(solution)/shard_map/propagate/pallas_call | solution.py:118
  38.3 4.3 %collective-permute-done.4.refs_3_ = f32[2,32,8,128]{3,2,1,0:T(8,128)S(1)} collective-permute-done((f32[2,32,8,128]{3,2,1,0:T(8,128)S(1)}, f32[2,32,8,128]{3,2,1,0:T(8,128)S(1)}, u32[]{:S(2)}, u32[]{:S(2)}) %collective-permute-start.4) | collective-permute-done | bytes 262176 | tf_op jit(solution)/shard_map/ppermute | solution.py:237
  42.6 1.4 %propagate.11 = (f32[1,32,8,128]{3,2,1,0:T(8,128)S(1)}, f32[1,32,8,128]{3,2,1,0:T(8,128)S(1)}, f32[1,32,8,128]{3,2,1,0:T(8,128)S(1)}, f32[1,32,8,128]{3,2,1,0:T(8,128)S(1)}) custom-call(bf16[8,2,32,8,128]{4,3,2,1,0:T(8,128)(2,1)S(1)} %bitcast.19, bf16[8,2,32,8,128]{4,3,2,1,0:T(8,128)(2,1)S(1)} %collective-permute-done.refs_1_, ...), custom_call_target="tpu_custom_call" | custom-call | tf_op jit(solution)/shard_map/propagate/pallas_call | solution.py:118
  44.3 5.9 %collective-permute-done.8.refs_3_ = f32[2,32,8,128]{3,2,1,0:T(8,128)S(1)} collective-permute-done((f32[2,32,8,128]{3,2,1,0:T(8,128)S(1)}, f32[2,32,8,128]{3,2,1,0:T(8,128)S(1)}, u32[]{:S(2)}, u32[]{:S(2)}) %collective-permute-start.8) | collective-permute-done | bytes 262176 | tf_op jit(solution)/shard_map/ppermute | solution.py:237
  50.2 1.4 %propagate.15 = (f32[1,32,8,128]{3,2,1,0:T(8,128)S(1)}, f32[1,32,8,128]{3,2,1,0:T(8,128)S(1)}, f32[1,32,8,128]{3,2,1,0:T(8,128)S(1)}, f32[1,32,8,128]{3,2,1,0:T(8,128)S(1)}) custom-call(bf16[8,2,32,8,128]{4,3,2,1,0:T(8,128)(2,1)S(1)} %bitcast.20, bf16[8,2,32,8,128]{4,3,2,1,0:T(8,128)(2,1)S(1)} %collective-permute-done.refs_1_, ...), custom_call_target="tpu_custom_call" | custom-call | tf_op jit(solution)/shard_map/propagate/pallas_call | solution.py:118
  51.8 1.8 %collective-permute-done.5.refs_1_ = f32[1,32,8,128]{3,2,1,0:T(8,128)S(1)} collective-permute-done((f32[1,32,8,128]{3,2,1,0:T(8,128)S(1)}, f32[1,32,8,128]{3,2,1,0:T(8,128)S(1)}, u32[]{:S(2)}, u32[]{:S(2)}) %collective-permute-start.5) | collective-permute-done | bytes 131104 | tf_op jit(solution)/shard_map/ppermute | solution.py:237
  53.6 7.7 %collective-permute-done.9.refs_2_ = f32[1,32,8,128]{3,2,1,0:T(8,128)S(1)} collective-permute-done((f32[1,32,8,128]{3,2,1,0:T(8,128)S(1)}, f32[1,32,8,128]{3,2,1,0:T(8,128)S(1)}, u32[]{:S(2)}, u32[]{:S(2)}) %collective-permute-start.9) | collective-permute-done | bytes 131104 | tf_op jit(solution)/shard_map/ppermute | solution.py:237
  61.4 1.3 %collective-permute-start.14 = (f32[16,128]{1,0:T(8,128)S(1)}, f32[16,128]{1,0:T(8,128)S(1)}, u32[]{:S(2)}, u32[]{:S(2)}) collective-permute-start(f32[16,128]{1,0:T(8,128)S(1)} %get-tuple-element.39), channel_id=1, source_target_pairs={{0,1},{1,0},{2,3},{3,2},{4,5},{5,4},{6,7},{7,6},{8,9},{9,8},{10,11... | collective-permute-start | bytes 24584 | tf_op jit(solution)/shard_map/ppermute | solution.py:221
  63.5 3.6 %collective-permute-done.15 = f32[16,128]{1,0:T(8,128)S(1)} collective-permute-done((f32[16,128]{1,0:T(8,128)S(1)}, f32[16,128]{1,0:T(8,128)S(1)}, u32[]{:S(2)}, u32[]{:S(2)}) %collective-permute-start.15) | collective-permute-done | bytes 8224 | tf_op jit(solution)/shard_map/ppermute | solution.py:221
  67.2 3.6 %collective-permute-done.16 = f32[16,128]{1,0:T(8,128)S(1)} collective-permute-done((f32[16,128]{1,0:T(8,128)S(1)}, f32[16,128]{1,0:T(8,128)S(1)}, u32[]{:S(2)}, u32[]{:S(2)}) %collective-permute-start.16) | collective-permute-done | bytes 8224 | tf_op jit(solution)/shard_map/ppermute | solution.py:221
  70.8 3.6 %collective-permute-done.17 = f32[16,128]{1,0:T(8,128)S(1)} collective-permute-done((f32[16,128]{1,0:T(8,128)S(1)}, f32[16,128]{1,0:T(8,128)S(1)}, u32[]{:S(2)}, u32[]{:S(2)}) %collective-permute-start.17) | collective-permute-done | bytes 8224 | tf_op jit(solution)/shard_map/ppermute | solution.py:221
  74.5 4.5 %collective-permute-done.18 = f32[16,128]{1,0:T(8,128)S(1)} collective-permute-done((f32[16,128]{1,0:T(8,128)S(1)}, f32[16,128]{1,0:T(8,128)S(1)}, u32[]{:S(2)}, u32[]{:S(2)}) %collective-permute-start.18) | collective-permute-done | bytes 8224 | tf_op jit(solution)/shard_map/ppermute | solution.py:221
  (36 shorter events, 4.4 us)
Async XLA Ops:
  0.0 3.4 %copy-start = (bf16[1,8,2,8,4096]{4,3,2,1,0:T(8,128)(2,1)S(1)}, bf16[1,8,2,8,4096]{4,3,2,1,0:T(8,128)(2,1)}, u32[]{:S(2)}) copy-start(bf16[1,8,2,8,4096]{4,3,2,1,0:T(8,128)(2,1)} %param.3) | copy-start | bytes 3145732
  0.0 3.4 %collective-permute-start = (bf16[8,2,32,8,128]{4,3,2,1,0:T(8,128)(2,1)}, bf16[8,2,32,8,128]{4,3,2,1,0:T(8,128)(2,1)S(1)}, u32[]{:S(2)}, u32[]{:S(2)}) collective-permute-start(bf16[8,2,32,8,128]{4,3,2,1,0:T(8,128)(2,1)} %bitcast.12), channel_id=1, source_target_pairs={{1,0},{0,1},{3,2},{2,3},{5,4},{4,5},{7,6},{6,7},{9,8},{8,9},{11,10... | collective-permute-start | bytes 3145736 | tf_op jit(solution)/shard_map/ppermute | solution.py:228
  1.6 1.8 %collective-permute-start.1 = (f32[2,32,8,128]{3,2,1,0:T(8,128)S(1)}, f32[2,32,8,128]{3,2,1,0:T(8,128)S(1)}, u32[]{:S(2)}, u32[]{:S(2)}) collective-permute-start(f32[2,32,8,128]{3,2,1,0:T(8,128)S(1)} %get-tuple-element.42), channel_id=1, source_target_pairs={{1,0},{0,1},{3,2},{2,3},{5,4},{4,5},{7,6},{6,7},{9,8},{8,9},{11,10... | collective-permute-start | bytes 786440 | tf_op jit(solution)/shard_map/ppermute | solution.py:228
  4.8 14.0 %collective-permute-start.2 = (f32[2,32,8,128]{3,2,1,0:T(8,128)S(1)}, f32[2,32,8,128]{3,2,1,0:T(8,128)S(1)}, u32[]{:S(2)}, u32[]{:S(2)}) collective-permute-start(f32[2,32,8,128]{3,2,1,0:T(8,128)S(1)} %propagate.8), channel_id=1, source_target_pairs={{0,2},{1,3},{2,4},{3,5},{4,6},{5,7},{6,8},{7,9},{8,10},{9,11},{10,... | collective-permute-start | bytes 786440 | tf_op jit(solution)/shard_map/ppermute | solution.py:237
  9.1 14.8 %collective-permute-start.6 = (f32[2,32,8,128]{3,2,1,0:T(8,128)S(1)}, f32[2,32,8,128]{3,2,1,0:T(8,128)S(1)}, u32[]{:S(2)}, u32[]{:S(2)}) collective-permute-start(f32[2,32,8,128]{3,2,1,0:T(8,128)S(1)} %propagate.12), channel_id=1, source_target_pairs={{0,2},{1,3},{2,4},{3,5},{4,6},{5,7},{6,8},{7,9},{8,10},{9,11},{10,... | collective-permute-start | bytes 786440 | tf_op jit(solution)/shard_map/ppermute | solution.py:237
  20.3 10.9 %collective-permute-start.3 = (f32[2,32,8,128]{3,2,1,0:T(8,128)S(1)}, f32[2,32,8,128]{3,2,1,0:T(8,128)S(1)}, u32[]{:S(2)}, u32[]{:S(2)}) collective-permute-start(f32[2,32,8,128]{3,2,1,0:T(8,128)S(1)} %get-tuple-element.24), channel_id=1, source_target_pairs={{0,2},{1,3},{2,4},{3,5},{4,6},{5,7},{6,8},{7,9},{8,10},{9,11},{10,... | collective-permute-start | bytes 786440 | tf_op jit(solution)/shard_map/ppermute | solution.py:237
  25.4 11.4 %collective-permute-start.7 = (f32[2,32,8,128]{3,2,1,0:T(8,128)S(1)}, f32[2,32,8,128]{3,2,1,0:T(8,128)S(1)}, u32[]{:S(2)}, u32[]{:S(2)}) collective-permute-start(f32[2,32,8,128]{3,2,1,0:T(8,128)S(1)} %get-tuple-element.29), channel_id=1, source_target_pairs={{0,2},{1,3},{2,4},{3,5},{4,6},{5,7},{6,8},{7,9},{8,10},{9,11},{10,... | collective-permute-start | bytes 786440 | tf_op jit(solution)/shard_map/ppermute | solution.py:237
  32.6 10.0 %collective-permute-start.4 = (f32[2,32,8,128]{3,2,1,0:T(8,128)S(1)}, f32[2,32,8,128]{3,2,1,0:T(8,128)S(1)}, u32[]{:S(2)}, u32[]{:S(2)}) collective-permute-start(f32[2,32,8,128]{3,2,1,0:T(8,128)S(1)} %get-tuple-element.26), channel_id=1, source_target_pairs={{0,2},{1,3},{2,4},{3,5},{4,6},{5,7},{6,8},{7,9},{8,10},{9,11},{10,... | collective-permute-start | bytes 786440 | tf_op jit(solution)/shard_map/ppermute | solution.py:237
  38.2 12.0 %collective-permute-start.8 = (f32[2,32,8,128]{3,2,1,0:T(8,128)S(1)}, f32[2,32,8,128]{3,2,1,0:T(8,128)S(1)}, u32[]{:S(2)}, u32[]{:S(2)}) collective-permute-start(f32[2,32,8,128]{3,2,1,0:T(8,128)S(1)} %get-tuple-element.31), channel_id=1, source_target_pairs={{0,2},{1,3},{2,4},{3,5},{4,6},{5,7},{6,8},{7,9},{8,10},{9,11},{10,... | collective-permute-start | bytes 786440 | tf_op jit(solution)/shard_map/ppermute | solution.py:237
  44.1 9.5 %collective-permute-start.5 = (f32[1,32,8,128]{3,2,1,0:T(8,128)S(1)}, f32[1,32,8,128]{3,2,1,0:T(8,128)S(1)}, u32[]{:S(2)}, u32[]{:S(2)}) collective-permute-start(f32[1,32,8,128]{3,2,1,0:T(8,128)S(1)} %get-tuple-element.27), channel_id=1, source_target_pairs={{0,2},{1,3},{2,4},{3,5},{4,6},{5,7},{6,8},{7,9},{8,10},{9,11},{10,... | collective-permute-start | bytes 393224 | tf_op jit(solution)/shard_map/ppermute | solution.py:237
  44.1 9.5 %collective-permute-start.10 = (f32[1,32,8,128]{3,2,1,0:T(8,128)S(1)}, f32[1,32,8,128]{3,2,1,0:T(8,128)S(1)}, u32[]{:S(2)}, u32[]{:S(2)}) collective-permute-start(f32[1,32,8,128]{3,2,1,0:T(8,128)S(1)} %get-tuple-element.33), channel_id=1, source_target_pairs={{0,3},{1,2},{2,5},{3,4},{4,7},{5,6},{6,9},{7,8},{8,11},{9,10},{10,... | collective-permute-start | bytes 393224 | tf_op jit(solution)/shard_map/ppermute | solution.py:237
  44.2 9.4 %collective-permute-start.12 = (f32[1,32,8,128]{3,2,1,0:T(8,128)S(1)}, f32[1,32,8,128]{3,2,1,0:T(8,128)S(1)}, u32[]{:S(2)}, u32[]{:S(2)}) collective-permute-start(f32[1,32,8,128]{3,2,1,0:T(8,128)S(1)} %get-tuple-element.37), channel_id=1, source_target_pairs={{1,0},{0,1},{3,2},{2,3},{5,4},{4,5},{7,6},{6,7},{9,8},{8,9},{11,10... | collective-permute-start | bytes 393224 | tf_op jit(solution)/shard_map/ppermute | solution.py:228
  51.6 9.6 %collective-permute-start.9 = (f32[1,32,8,128]{3,2,1,0:T(8,128)S(1)}, f32[1,32,8,128]{3,2,1,0:T(8,128)S(1)}, u32[]{:S(2)}, u32[]{:S(2)}) collective-permute-start(f32[1,32,8,128]{3,2,1,0:T(8,128)S(1)} %get-tuple-element.32), channel_id=1, source_target_pairs={{0,2},{1,3},{2,4},{3,5},{4,6},{5,7},{6,8},{7,9},{8,10},{9,11},{10,... | collective-permute-start | bytes 393224 | tf_op jit(solution)/shard_map/ppermute | solution.py:237
  51.7 9.5 %collective-permute-start.11 = (f32[1,32,8,128]{3,2,1,0:T(8,128)S(1)}, f32[1,32,8,128]{3,2,1,0:T(8,128)S(1)}, u32[]{:S(2)}, u32[]{:S(2)}) collective-permute-start(f32[1,32,8,128]{3,2,1,0:T(8,128)S(1)} %get-tuple-element.34), channel_id=1, source_target_pairs={{0,3},{1,2},{2,5},{3,4},{4,7},{5,6},{6,9},{7,8},{8,11},{9,10},{10,... | collective-permute-start | bytes 393224 | tf_op jit(solution)/shard_map/ppermute | solution.py:237
  53.6 7.7 %collective-permute-start.13 = (f32[1,32,8,128]{3,2,1,0:T(8,128)S(1)}, f32[1,32,8,128]{3,2,1,0:T(8,128)S(1)}, u32[]{:S(2)}, u32[]{:S(2)}) collective-permute-start(f32[1,32,8,128]{3,2,1,0:T(8,128)S(1)} %get-tuple-element.38), channel_id=1, source_target_pairs={{1,0},{0,1},{3,2},{2,3},{5,4},{4,5},{7,6},{6,7},{9,8},{8,9},{11,10... | collective-permute-start | bytes 393224 | tf_op jit(solution)/shard_map/ppermute | solution.py:228
  61.4 2.1 %collective-permute-start.14 = (f32[16,128]{1,0:T(8,128)S(1)}, f32[16,128]{1,0:T(8,128)S(1)}, u32[]{:S(2)}, u32[]{:S(2)}) collective-permute-start(f32[16,128]{1,0:T(8,128)S(1)} %get-tuple-element.39), channel_id=1, source_target_pairs={{0,1},{1,0},{2,3},{3,2},{4,5},{5,4},{6,7},{7,6},{8,9},{9,8},{10,11... | collective-permute-start | bytes 24584 | tf_op jit(solution)/shard_map/ppermute | solution.py:221
  63.5 3.7 %collective-permute-start.15 = (f32[16,128]{1,0:T(8,128)S(1)}, f32[16,128]{1,0:T(8,128)S(1)}, u32[]{:S(2)}, u32[]{:S(2)}) collective-permute-start(f32[16,128]{1,0:T(8,128)S(1)} %add.27), channel_id=1, source_target_pairs={{0,2},{1,3},{2,0},{3,1},{4,6},{5,7},{6,4},{7,5},{8,10},{9,11},{10,... | collective-permute-start | bytes 24584 | tf_op jit(solution)/shard_map/ppermute | solution.py:221
  67.2 3.7 %collective-permute-start.16 = (f32[16,128]{1,0:T(8,128)S(1)}, f32[16,128]{1,0:T(8,128)S(1)}, u32[]{:S(2)}, u32[]{:S(2)}) collective-permute-start(f32[16,128]{1,0:T(8,128)S(1)} %add.28), channel_id=1, source_target_pairs={{0,4},{1,5},{2,6},{3,7},{4,0},{5,1},{6,2},{7,3},{8,12},{9,13},{10,... | collective-permute-start | bytes 24584 | tf_op jit(solution)/shard_map/ppermute | solution.py:221
  70.8 3.7 %collective-permute-start.17 = (f32[16,128]{1,0:T(8,128)S(1)}, f32[16,128]{1,0:T(8,128)S(1)}, u32[]{:S(2)}, u32[]{:S(2)}) collective-permute-start(f32[16,128]{1,0:T(8,128)S(1)} %add.29), channel_id=1, source_target_pairs={{0,8},{1,9},{2,10},{3,11},{4,12},{5,13},{6,14},{7,15},{8,0},{9,1},... | collective-permute-start | bytes 24584 | tf_op jit(solution)/shard_map/ppermute | solution.py:221
  74.5 4.5 %collective-permute-start.18 = (f32[16,128]{1,0:T(8,128)S(1)}, f32[16,128]{1,0:T(8,128)S(1)}, u32[]{:S(2)}, u32[]{:S(2)}) collective-permute-start(f32[16,128]{1,0:T(8,128)S(1)} %add.30), channel_id=1, source_target_pairs={{0,16},{1,17},{2,18},{3,19},{4,20},{5,21},{6,22},{7,23},{8,24},{9,... | collective-permute-start | bytes 24584 | tf_op jit(solution)/shard_map/ppermute | solution.py:221

commit v2 on v1

v2 whole, which is shorter than its diff:
```python
import functools

import jax
import jax.numpy as jnp
from jax import lax
from jax.experimental import pallas as pl
from jax.experimental.pallas import tpu as pltpu
from jax.sharding import PartitionSpec as P

HOPS = 4
SUB = 8
LANE = 128
VMEM = pl.BlockSpec(memory_space=pltpu.VMEM)


def tiled(rows):
    lead, (height, width) = rows.shape[:-2], rows.shape[-2:]
    cut = rows.reshape(lead + (height, width // LANE, LANE))
    return jnp.swapaxes(cut, -3, -2)


def untiled(tiles):
    lead, (count, height, lane) = tiles.shape[:-3], tiles.shape[-3:]
    return jnp.swapaxes(tiles, -3, -2).reshape(lead + (height, count * lane))


def advance(velocity, ping, pong, pieces):
    depth, _, columns, height, _ = velocity[0].shape
    rows = pieces * height
    lane = lax.broadcasted_iota(jnp.int32, (SUB, LANE), 1)
    first, last = lane == 0, lane == LANE - 1

    def step(k, source, target):
        for b in range(rows // SUB):
            piece, at = divmod(SUB * b, height)
            rows_at = pl.ds(SUB + SUB * b, SUB)
            here = [source[j % columns, rows_at, :] for j in (-1, 0, 1)]
            for j in range(columns):
                left, centre, right = here
                west = pltpu.roll(jnp.where(last, left, centre), 1, 1)
                east = pltpu.roll(jnp.where(first, right, centre), LANE - 1, 1)
                up = source[j, pl.ds(SUB + 1 + SUB * b, SUB), :]
                down = source[j, pl.ds(SUB - 1 + SUB * b, SUB), :]
                speed_x = velocity[piece][k, 0, j, pl.ds(at, SUB), :].astype(jnp.float32)
                speed_y = velocity[piece][k, 1, j, pl.ds(at, SUB), :].astype(jnp.float32)
                carried = speed_x * (west - east) + speed_y * (down - up)
                place(target, rows, j, b, 0.9 * centre + ((west + east) + (up + down)) + 0.25 * carried)
                here = [centre, right, source[(j + 2) % columns, rows_at, :]]

    def pair(i, carry):
        step(2 * i, ping, pong)
        step(2 * i + 1, pong, ping)
        return carry

    lax.fori_loop(0, depth // 2, pair, 0)
    if depth % 2:
        step(depth - 1, ping, pong)
        return pong
    return ping


def place(ref, rows, j, b, value):
    ref[j, pl.ds(SUB + SUB * b, SUB), :] = value
    if b == 0:
        ref[j, pl.ds(SUB + rows, 1), :] = value[:1]
    if b == rows // SUB - 1:
        ref[j, pl.ds(SUB - 1, 1), :] = value[SUB - 1 :]


def tiles_of(pieces, columns, height):
    for j in range(columns):
        for b in range(pieces * height // SUB):
            piece, at = divmod(SUB * b, height)
            yield piece, j, pl.ds(at, SUB), b, (piece * columns + j) * (height // SUB) + at // SUB


TOP = 13.0


def propagate_kernel(pieces, index, first, final, *refs):
    refs = list(refs)
    take = lambda count: [refs.pop(0) for _ in range(count)]
    velocity = take(pieces)
    depth, _, columns, height, _ = velocity[0].shape
    rows, count = pieces * height, pieces * columns * height // SUB
    if first:
        previous = take(pieces)
    else:
        previous, message, missed = take(3)
        start = take(pieces) if final else take(1)
    if final:
        moved = take(pieces)
    else:
        sent, error = take(2)
    ping, pong = refs

    if not first:
        back = jnp.exp2(message[count] - TOP)
    for piece, j, at, b, m in tiles_of(pieces, columns, height):
        if first:
            value = previous[piece][index, j, at, :]
        else:
            value = message[m] * back - previous[piece, j, at, :]
            if final:
                start[piece][0, j, at, :] = value
            else:
                start[0][piece, j, at, :] = value
        place(ping, rows, j, b, value)

    done = advance(velocity, ping, pong, pieces)
    largest = None
    for piece, j, at, b, m in tiles_of(pieces, columns, height):
        value = 0.2**depth * done[j, pl.ds(SUB + SUB * b, SUB), :]
        if not first:
            value = value + missed[m]
        if final:
            moved[piece][0, j, at, :] = value
        else:
            sent[m] = value
            size = jnp.abs(value)
            largest = size if largest is None else jnp.maximum(largest, size)
    if final:
        return
    largest = jnp.broadcast_to(jnp.max(largest, axis=(0, 1), keepdims=True), (SUB, LANE))
    power = jnp.clip(jnp.floor(jnp.log2(largest)), -100.0, 100.0)
    scale, back = jnp.exp2(TOP - power), jnp.exp2(power - TOP)
    sent[count] = power
    for m in range(count):
        value = sent[m]
        scaled = value * scale
        wide = scaled * 8193.0
        short = wide - (wide - scaled)
        sent[m] = short
        error[m] = short * back - value


@functools.partial(jax.jit, static_argnames=("index", "final"))
def propagate(velocity, state, index=0, final=False):
    pieces = len(velocity)
    _, _, columns, height, lane = velocity[0].shape
    count = pieces * columns * height // SUB
    first = isinstance(state, list)
    shape = lambda *s: jax.ShapeDtypeStruct(s + (lane,), jnp.float32)
    parts = [shape(1, columns, height)] * pieces
    outs = [] if first else (parts if final else [shape(pieces, columns, height)])
    outs = outs + (parts if final else [shape(count + 1, SUB), shape(count, SUB)])
    scratch = pltpu.VMEM((columns, pieces * height + 2 * SUB, lane), jnp.float32)
    args = [*velocity, *state]
    out = pl.pallas_call(
        functools.partial(propagate_kernel, pieces, index, first, final),
        out_shape=outs,
        in_specs=[VMEM] * len(args),
        out_specs=[VMEM] * len(outs),
        scratch_shapes=[scratch, scratch],
        compiler_params=pltpu.CompilerParams(vmem_limit_bytes=16 << 20),
        name="propagate",
    )(*args)
    return (out[:pieces], out[pieces:]) if final else out


def rows_kernel(pieces, index, *refs):
    velocity, previous, (moved, ping, pong) = refs[:pieces], refs[pieces : 2 * pieces], refs[2 * pieces :]
    depth, _, columns, height, _ = velocity[0].shape
    for piece, j, at, b, _ in tiles_of(pieces, columns, height):
        place(ping, pieces * height, j, b, previous[piece][index, j, at, :])
    done = advance(velocity, ping, pong, pieces)
    for piece, j, at, b, _ in tiles_of(1, columns, height):
        moved[0, j, at, :] = 0.2**depth * done[j, pl.ds(SUB + SUB * b, SUB), :]


@functools.partial(jax.jit, static_argnames=("index",))
def propagate_rows(velocity, state, index):
    pieces = len(velocity)
    _, _, columns, height, lane = velocity[0].shape
    scratch = pltpu.VMEM((columns, pieces * height + 2 * SUB, lane), jnp.float32)
    return pl.pallas_call(
        functools.partial(rows_kernel, pieces, index),
        out_shape=jax.ShapeDtypeStruct((1, columns, height, lane), jnp.float32),
        in_specs=[VMEM] * (2 * pieces),
        out_specs=VMEM,
        scratch_shapes=[scratch, scratch],
        compiler_params=pltpu.CompilerParams(vmem_limit_bytes=16 << 20),
        name="propagate_rows",
    )(*velocity, *state)


def gram_kernel(groups, *refs):
    base, refs = refs[0], refs[1:]
    arrived, start = refs[:groups], refs[groups : 2 * groups]
    residual, gram, lines = refs[2 * groups :]
    count, columns, height, _ = residual.shape
    sums = {}
    for j in range(columns):
        for at in range(0, height, SUB):
            values = []
            for a, s in zip(arrived, start):
                for i in range(a.shape[0]):
                    values.append(a[i, j, pl.ds(at, SUB), :] - s[i, j, pl.ds(at, SUB), :])
            for p in range(count):
                residual[p, j, pl.ds(at, SUB), :] = values[p]
                for q in range(p + 1):
                    term = values[p] * values[q]
                    sums[p, q] = term if (p, q) not in sums else sums[p, q] + term
    for (p, q), total in sums.items():
        line = jnp.sum(total, axis=0, keepdims=True)
        a, b = lax.rem(base[0] + p, count), lax.rem(base[0] + q, count)
        lines[pl.ds(a * count + b, 1), :] = line
        if p != q:
            lines[pl.ds(b * count + a, 1), :] = line
    totals = jnp.where(diagonal(count), jnp.sum(lines[...], axis=1, keepdims=True), 0.0)
    gram[...] = jnp.broadcast_to(jnp.sum(totals, axis=0, keepdims=True), gram.shape)


def diagonal(count):
    shape = (count * count, LANE)
    return lax.broadcasted_iota(jnp.int32, shape, 0) == lax.broadcasted_iota(jnp.int32, shape, 1)


def local_gram(shift, arrived, start, copies):
    count = sum(a.shape[0] for a in arrived)
    shape = (count,) + arrived[0].shape[1:]
    return pl.pallas_call(
        functools.partial(gram_kernel, len(arrived)),
        out_shape=[jax.ShapeDtypeStruct(shape, jnp.float32), jax.ShapeDtypeStruct((copies, LANE), jnp.float32)],
        in_specs=[pl.BlockSpec(memory_space=pltpu.SMEM)] + [VMEM] * (2 * len(arrived)),
        out_specs=[VMEM, VMEM],
        scratch_shapes=[pltpu.VMEM((count * count, LANE), jnp.float32)],
        compiler_params=pltpu.CompilerParams(vmem_limit_bytes=16 << 20),
        name="gram",
    )(shift, *arrived, *start)


def solve_kernel(base, gram, residual, out):
    count, columns, height, lane = residual.shape
    line = jnp.broadcast_to(jnp.sum(gram[...], axis=0, keepdims=True), (count * count, lane))
    total = jnp.sum(jnp.where(diagonal(count), line, 0.0), axis=1, keepdims=True)
    entry = lambda a, b: total[a * count + b : a * count + b + 1, :]
    lower, inverse = {}, {}
    for a in range(count):
        for b in range(a + 1):
            value = entry(a, b)
            for k in range(b):
                value = value - lower[a, k] * lower[b, k]
            lower[a, b] = jnp.sqrt(value) if a == b else value / lower[b, b]
    for a in range(count):
        inverse[a, a] = 1.0 / lower[a, a]
        for b in range(a):
            value = lower[a, b] * inverse[b, b]
            for k in range(b + 1, a):
                value = value + lower[a, k] * inverse[k, b]
            inverse[a, b] = -value / lower[a, a]
    factors = {at: jnp.broadcast_to(value, (SUB, lane)) for at, value in inverse.items()}
    place = [lax.rem(a + count - base[0], count) for a in range(count)]
    for j in range(columns):
        for at in range(0, height, SUB):
            values = [residual[place[a], j, pl.ds(at, SUB), :] for a in range(count)]
            for a in range(count):
                value = factors[a, 0] * values[0]
                for b in range(1, a + 1):
                    value = value + factors[a, b] * values[b]
                out[a, j, pl.ds(at, SUB), :] = value


def solved(shift, gram, residual):
    return pl.pallas_call(
        solve_kernel,
        out_shape=jax.ShapeDtypeStruct(residual.shape, jnp.float32),
        in_specs=[pl.BlockSpec(memory_space=pltpu.SMEM), VMEM, VMEM],
        out_specs=VMEM,
        compiler_params=pltpu.CompilerParams(vmem_limit_bytes=16 << 20),
        name="solve",
    )(shift, gram, residual)


def from_slab(value, distance):
    size = lax.axis_size("slab")
    return lax.ppermute(value, "slab", [((i + distance) % size, i) for i in range(size)])


def to_next(value, turn=0):
    segs, slabs = lax.axis_size("seg"), lax.axis_size("slab")
    route = []
    for s in range(segs):
        for c in range(slabs):
            route.append((s * slabs + c, (s + 1) % segs * slabs + (c + turn) % slabs))
    return lax.ppermute(value, ("seg", "slab"), route)


def split_vectors(vectors, velocity):
    slabs, mine = lax.axis_size("slab"), lax.axis_index("slab")
    share = vectors.shape[0] // slabs

    def part(distance):
        at = lax.rem(mine + distance, slabs) * share
        return lax.dynamic_slice_in_dim(vectors, at, share, 0)

    start, speeds = [part(0)], [velocity]
    for d in range(1, slabs):
        start.append(from_slab(part(slabs - d), d))
        speeds.append(from_slab(velocity, d))
    firsts = [propagate(speeds, start, i) for i in range(share)]
    previous = [jnp.concatenate([part[i : i + 1] for part in start], 0) for i in range(share)]
    moved, missed = [f[0] for f in firsts], [f[1] for f in firsts]
    for hop in range(1, HOPS):
        for i in range(share):
            message = to_next(moved[i].astype(jnp.float16)).astype(jnp.float32)
            state = (previous[i], message, missed[i])
            if hop + 1 < HOPS:
                previous[i], moved[i], missed[i] = propagate(speeds, state)
            else:
                previous[i], moved[i] = propagate(speeds, state, final=True)
    arrived, begun = [], []
    for d in range(slabs):
        for i in range(share):
            at = (slabs - d) % slabs
            arrived.append(to_next(moved[i][at], at))
            begun.append(from_slab(previous[i][at], d) if d else previous[i][0])
    shift = jnp.full((1,), mine * share, jnp.int32)
    return shift, arrived, begun


def split_rows(vectors, velocity):
    depth, height = velocity.shape[0], vectors.shape[2]

    def pieces(value):
        after = value[..., :depth, :]
        before = value[..., height - depth :, :]
        return [value, from_slab(after, 1), from_slab(before, -1)]

    speeds = pieces(velocity)
    begun = vectors
    for hop in range(HOPS):
        state = pieces(begun)
        arrived = [to_next(propagate_rows(speeds, state, i)) for i in range(vectors.shape[0])]
        if hop + 1 < HOPS:
            begun = jnp.concatenate(arrived, 0) - begun
    return jnp.zeros((1,), jnp.int32), arrived, [begun[i : i + 1] for i in range(vectors.shape[0])]


def shards(block, base_velocity):
    vectors, velocity = tiled(block[0]), tiled(base_velocity[0])
    even = vectors.shape[0] % lax.axis_size("slab") == 0
    shift, arrived, begun = (split_vectors if even else split_rows)(vectors, velocity)
    axes = ("seg", "slab")
    residual, gram = local_gram(shift, arrived, begun, lax.axis_size("seg") * lax.axis_size("slab"))
    gram = lax.all_to_all(gram, axes, 0, 0, tiled=True)
    return untiled(solved(shift, gram, residual))[None]


def solution(mesh):
    placed = (P("seg", None, "slab", None), P("seg", None, None, "slab", None))
    return jax.shard_map(
        shards, mesh=mesh, in_specs=placed, out_specs=P("seg", None, "slab", None), check_vma=False
    )
```

time: 80.2 us -> 65.3 us (0.81)
  waiting for transfers between devices: 59.2 us -> 34.9 us
  blocking collectives: 0 us -> 8.86 us
  Pallas kernels: 12.6 us -> 14.1 us
  starting transfers between devices: 6.94 us -> 5.64 us
    ppermute x5 -> x0, waiting for transfers between devices: 16.3 us -> none  [summed(): lax.ppermute(value, axes, [(i, i ^ distance) for i in range(count)])]
    all_to_all x0 -> x1, blocking collectives: none -> 8.86 us  [shards(): gram = lax.all_to_all(gram, axes, 0, 0, tiled=True)]
    ppermute x10, waiting for transfers between devices: 41.2 us -> 33.3 us  [to_next(): return lax.ppermute(value, ('seg', 'slab'), route)]
    pallas_call x8, Pallas kernels: 11.4 us -> 12.9 us  [propagate(): pl.pallas_call(functools.partial(propagate_kernel, pieces, index, first,...]
    ppermute x5 -> x0, starting transfers between devices: 1.3 us -> none  [summed(): lax.ppermute(value, axes, [(i, i ^ distance) for i in range(count)])]
  transfers between devices with their start and end apart: 19 -> 14, of which waited for: 14 -> 8; matrix products, arithmetic and copies ran while one was open for 1% -> 2% of each run, Pallas kernels for 13% -> 17%
where the time goes in v2:
time: 65.3 us; the launch traced here: 65.2 us
  waiting for transfers between devices  34.9 us (53%)
  Pallas kernels  14.1 us (22%)
  blocking collectives  8.86 us (14%)
  starting transfers between devices  5.64 us (9%)
  local copies, waits for them, and re-layouts  1.1 us (2%)
    ppermute x10, waiting for transfers between devices, to_next(): return lax.ppermute(value, ('seg', 'slab'), route)  33.3 us
    pallas_call x8, Pallas kernels, propagate(): pl.pallas_call(functools.partial(propagate_kernel, pieces, index, first,...  12.9 us
    all_to_all x1, blocking collectives, shards(): gram = lax.all_to_all(gram, axes, 0, 0, tiled=True)  8.86 us
    ppermute x10, starting transfers between devices, to_next(): return lax.ppermute(value, ('seg', 'slab'), route)  4.91 us
    ppermute x4, waiting for transfers between devices, from_slab(): lax.ppermute(value, 'slab', [((i + distance) % size, i) for i in range(si...  1.62 us
  transfers between devices with their start and end apart: 14, of which 8 were waited for; matrix products, arithmetic and copies ran while one was open for 2% of the time, Pallas kernels for 17%

profile of v2, /device:TPU:0, one launch (start us, length us, event | category | flops | bytes accessed | tf_op | source)
XLA Modules:
  0.0 65.2 jit_solution(7317285192541615314)
XLA Ops:
  0.0 0.5 collective-permute-start
  0.5 1.1 %dynamic-slice_bitcast_fusion.1 = (f32[2,32,8,128]{3,2,1,0:T(8,128)S(1)}, f32[2,32,8,128]{3,2,1,0:T(8,128)S(1)}) fusion(f32[4,8,32,128]{3,1,2,0:T(8,128)} %bitcast.27, s32[]{:T(128)S(6)} %select_n.6, s32[]{:T(128)S(6)} %select_n.7), kind=kLoop, calls=%fused_computation.3 | loop fusion | bytes 1048584 | tf_op jit(solution)/shard_map/dynamic_slice | solution.py:295
  1.6 0.2 collective-permute-start.1
  1.8 1.6 %collective-permute-done.1.refs_3_ = f32[2,32,8,128]{3,2,1,0:T(8,128)S(1)} collective-permute-done((f32[2,32,8,128]{3,2,1,0:T(8,128)S(1)}, f32[2,32,8,128]{3,2,1,0:T(8,128)S(1)}, u32[]{:S(2)}, u32[]{:S(2)}) %collective-permute-start.1) | collective-permute-done | bytes 262176 | tf_op jit(solution)/shard_map/ppermute | solution.py:277
  3.4 1.6 %propagate.8 = (f32[65,8,128]{2,1,0:T(8,128)S(1)}, f32[64,8,128]{2,1,0:T(8,128)S(1)}) custom-call(bf16[8,2,32,8,128]{4,3,2,1,0:T(8,128)(2,1)S(1)} %bitcast.17, bf16[8,2,32,8,128]{4,3,2,1,0:T(8,128)(2,1)S(1)} %collective-permute-done.refs_1_, f32[2,32,8,128]{3,2,1,0:T(8,128)S(1)} %get-tuple-element.57.refs_2_, ...), custom_call_target="tpu_custom_call" | custom-call | tf_op jit(solution)/shard_map/jit(propagate)/propagate/pallas_call | solution.py:149
  5.0 2.9 %collective-permute-start.2 = (f16[65,8,128]{2,1,0:T(8,128)(2,1)S(1)}, f16[65,8,128]{2,1,0:T(8,128)(2,1)S(1)}, u32[]{:S(2)}, u32[]{:S(2)}) collective-permute-start(f16[65,8,128]{2,1,0:T(8,128)(2,1)S(1)} %convert_element_type.36), channel_id=1, source_target_pairs={{0,2},{1,3},{2,4},{3,5},{4,6},{5,7},{6,8},{7,9},{8,10},{9,11},{10,... | collective-permute-start | bytes 399368 | tf_op jit(solution)/shard_map/ppermute | solution.py:286
  8.0 1.6 %propagate.12 = (f32[65,8,128]{2,1,0:T(8,128)S(1)}, f32[64,8,128]{2,1,0:T(8,128)S(1)}) custom-call(bf16[8,2,32,8,128]{4,3,2,1,0:T(8,128)(2,1)S(1)} %bitcast.18, bf16[8,2,32,8,128]{4,3,2,1,0:T(8,128)(2,1)S(1)} %collective-permute-done.refs_1_, f32[2,32,8,128]{3,2,1,0:T(8,128)S(1)} %get-tuple-element.57.refs_2_, ...), custom_call_target="tpu_custom_call" | custom-call | tf_op jit(solution)/shard_map/jit(propagate)/propagate/pallas_call | solution.py:149
  9.6 1.5 %collective-permute-start.6 = (f16[65,8,128]{2,1,0:T(8,128)(2,1)S(1)}, f16[65,8,128]{2,1,0:T(8,128)(2,1)S(1)}, u32[]{:S(2)}, u32[]{:S(2)}) collective-permute-start(f16[65,8,128]{2,1,0:T(8,128)(2,1)S(1)} %convert_element_type.42), channel_id=1, source_target_pairs={{0,2},{1,3},{2,4},{3,5},{4,6},{5,7},{6,8},{7,9},{8,10},{9,11},{10,... | collective-permute-start | bytes 399368 | tf_op jit(solution)/shard_map/ppermute | solution.py:286
  11.2 4.6 %collective-permute-done.2 = f16[65,8,128]{2,1,0:T(8,128)(2,1)S(1)} collective-permute-done((f16[65,8,128]{2,1,0:T(8,128)(2,1)S(1)}, f16[65,8,128]{2,1,0:T(8,128)(2,1)S(1)}, u32[]{:S(2)}, u32[]{:S(2)}) %collective-permute-start.2) | collective-permute-done | bytes 133152 | tf_op jit(solution)/shard_map/ppermute | solution.py:286
  15.8 1.7 %propagate.9 = (f32[2,32,8,128]{3,2,1,0:T(8,128)S(1)}, f32[65,8,128]{2,1,0:T(8,128)S(1)}, f32[64,8,128]{2,1,0:T(8,128)S(1)}) custom-call(bf16[8,2,32,8,128]{4,3,2,1,0:T(8,128)(2,1)S(1)} %bitcast.19, bf16[8,2,32,8,128]{4,3,2,1,0:T(8,128)(2,1)S(1)} %collective-permute-done.refs_1_, f32[2,32,8,128]{3,2,1,0:T(8,128)S(1)} %pad_maximum_fusion.refs_2_, ...), custom_call_target="tpu_custom_call" | custom-call | tf_op jit(solution)/shard_map/jit(propagate)/propagate/pallas_call | solution.py:149
  17.7 1.0 %collective-permute-done.6 = f16[65,8,128]{2,1,0:T(8,128)(2,1)S(1)} collective-permute-done((f16[65,8,128]{2,1,0:T(8,128)(2,1)S(1)}, f16[65,8,128]{2,1,0:T(8,128)(2,1)S(1)}, u32[]{:S(2)}, u32[]{:S(2)}) %collective-permute-start.6) | collective-permute-done | bytes 133152 | tf_op jit(solution)/shard_map/ppermute | solution.py:286
  18.7 1.7 %propagate.13 = (f32[2,32,8,128]{3,2,1,0:T(8,128)S(1)}, f32[65,8,128]{2,1,0:T(8,128)S(1)}, f32[64,8,128]{2,1,0:T(8,128)S(1)}) custom-call(bf16[8,2,32,8,128]{4,3,2,1,0:T(8,128)(2,1)S(1)} %bitcast.20, bf16[8,2,32,8,128]{4,3,2,1,0:T(8,128)(2,1)S(1)} %collective-permute-done.refs_1_, f32[2,32,8,128]{3,2,1,0:T(8,128)S(1)} %pad_maximum_fusion.1.refs_2_, ...), custom_call_target="tpu_custom_call" | custom-call | tf_op jit(solution)/shard_map/jit(propagate)/propagate/pallas_call | solution.py:149
  20.4 6.3 %collective-permute-done.3 = f16[65,8,128]{2,1,0:T(8,128)(2,1)S(1)} collective-permute-done((f16[65,8,128]{2,1,0:T(8,128)(2,1)S(1)}, f16[65,8,128]{2,1,0:T(8,128)(2,1)S(1)}, u32[]{:S(2)}, u32[]{:S(2)}) %collective-permute-start.3) | collective-permute-done | bytes 133152 | tf_op jit(solution)/shard_map/ppermute | solution.py:286
  26.8 1.7 %propagate.10 = (f32[2,32,8,128]{3,2,1,0:T(8,128)S(1)}, f32[65,8,128]{2,1,0:T(8,128)S(1)}, f32[64,8,128]{2,1,0:T(8,128)S(1)}) custom-call(bf16[8,2,32,8,128]{4,3,2,1,0:T(8,128)(2,1)S(1)} %bitcast.21, bf16[8,2,32,8,128]{4,3,2,1,0:T(8,128)(2,1)S(1)} %collective-permute-done.refs_1_, f32[2,32,8,128]{3,2,1,0:T(8,128)S(1)} %get-tuple-element.33.refs_2_, ...), custom_call_target="tpu_custom_call" | custom-call | tf_op jit(solution)/shard_map/jit(propagate)/propagate/pallas_call | solution.py:149
  28.5 0.5 collective-permute-done.7
  29.1 1.7 %propagate.14 = (f32[2,32,8,128]{3,2,1,0:T(8,128)S(1)}, f32[65,8,128]{2,1,0:T(8,128)S(1)}, f32[64,8,128]{2,1,0:T(8,128)S(1)}) custom-call(bf16[8,2,32,8,128]{4,3,2,1,0:T(8,128)(2,1)S(1)} %bitcast.22, bf16[8,2,32,8,128]{4,3,2,1,0:T(8,128)(2,1)S(1)} %collective-permute-done.refs_1_, f32[2,32,8,128]{3,2,1,0:T(8,128)S(1)} %get-tuple-element.42.refs_2_, ...), custom_call_target="tpu_custom_call" | custom-call | tf_op jit(solution)/shard_map/jit(propagate)/propagate/pallas_call | solution.py:149
  30.9 7.6 %collective-permute-done.4 = f16[65,8,128]{2,1,0:T(8,128)(2,1)S(1)} collective-permute-done((f16[65,8,128]{2,1,0:T(8,128)(2,1)S(1)}, f16[65,8,128]{2,1,0:T(8,128)(2,1)S(1)}, u32[]{:S(2)}, u32[]{:S(2)}) %collective-permute-start.4) | collective-permute-done | bytes 133152 | tf_op jit(solution)/shard_map/ppermute | solution.py:286
  38.4 1.5 %propagate.11 = (f32[1,32,8,128]{3,2,1,0:T(8,128)S(1)}, f32[1,32,8,128]{3,2,1,0:T(8,128)S(1)}, f32[1,32,8,128]{3,2,1,0:T(8,128)S(1)}, f32[1,32,8,128]{3,2,1,0:T(8,128)S(1)}) custom-call(bf16[8,2,32,8,128]{4,3,2,1,0:T(8,128)(2,1)S(1)} %bitcast.23, bf16[8,2,32,8,128]{4,3,2,1,0:T(8,128)(2,1)S(1)} %collective-permute-done.refs_1_, ...), custom_call_target="tpu_custom_call" | custom-call | tf_op jit(solution)/shard_map/jit(propagate)/propagate/pallas_call | solution.py:149
  40.2 1.5 %propagate.15 = (f32[1,32,8,128]{3,2,1,0:T(8,128)S(1)}, f32[1,32,8,128]{3,2,1,0:T(8,128)S(1)}, f32[1,32,8,128]{3,2,1,0:T(8,128)S(1)}, f32[1,32,8,128]{3,2,1,0:T(8,128)S(1)}) custom-call(bf16[8,2,32,8,128]{4,3,2,1,0:T(8,128)(2,1)S(1)} %bitcast.24, bf16[8,2,32,8,128]{4,3,2,1,0:T(8,128)(2,1)S(1)} %collective-permute-done.refs_1_, ...), custom_call_target="tpu_custom_call" | custom-call | tf_op jit(solution)/shard_map/jit(propagate)/propagate/pallas_call | solution.py:149
  41.8 8.2 %collective-permute-done.5.refs_1_ = f32[1,32,8,128]{3,2,1,0:T(8,128)S(1)} collective-permute-done((f32[1,32,8,128]{3,2,1,0:T(8,128)S(1)}, f32[1,32,8,128]{3,2,1,0:T(8,128)S(1)}, u32[]{:S(2)}, u32[]{:S(2)}) %collective-permute-start.5) | collective-permute-done | bytes 131104 | tf_op jit(solution)/shard_map/ppermute | solution.py:286
  50.0 5.1 %collective-permute-done.9.refs_2_ = f32[1,32,8,128]{3,2,1,0:T(8,128)S(1)} collective-permute-done((f32[1,32,8,128]{3,2,1,0:T(8,128)S(1)}, f32[1,32,8,128]{3,2,1,0:T(8,128)S(1)}, u32[]{:S(2)}, u32[]{:S(2)}) %collective-permute-start.9) | collective-permute-done | bytes 131104 | tf_op jit(solution)/shard_map/ppermute | solution.py:286
  55.1 0.2 gram.1
  55.3 8.9 %all_to_all.11 = f32[32,1,128]{2,1,0:T(1,128)S(1)} all-to-all(f32[32,1,128]{2,1,0:T(1,128)S(1)} %bitcast.26), channel_id=1, replica_groups=mesh['seg'=16,'slab'=2] {'seg','slab'}, dimensions={0} | all-to-all | bytes 32768 | tf_op jit(solution)/shard_map/all_to_all | solution.py:346
  64.1 1.0 %solve.1 = f32[4,32,8,128]{3,2,1,0:T(8,128)} custom-call(s32[1]{0:T(128)} %bitcast.refs_0_.base, f32[32,128]{1,0:T(8,128)S(1)} %bitcast.25, f32[4,32,8,128]{3,2,1,0:T(8,128)S(1)} %get-tuple-element.56.residual), custom_call_target="tpu_custom_call" | custom-call | tf_op jit(solution)/shard_map/solve/pallas_call | solution.py:265
  (34 shorter events, 0.9 us)
Async XLA Ops:
  0.0 3.4 %copy-start = (bf16[1,8,2,8,4096]{4,3,2,1,0:T(8,128)(2,1)S(1)}, bf16[1,8,2,8,4096]{4,3,2,1,0:T(8,128)(2,1)}, u32[]{:S(2)}) copy-start(bf16[1,8,2,8,4096]{4,3,2,1,0:T(8,128)(2,1)} %param.3) | copy-start | bytes 3145732
  0.0 3.4 %collective-permute-start = (bf16[8,2,32,8,128]{4,3,2,1,0:T(8,128)(2,1)}, bf16[8,2,32,8,128]{4,3,2,1,0:T(8,128)(2,1)S(1)}, u32[]{:S(2)}, u32[]{:S(2)}) collective-permute-start(bf16[8,2,32,8,128]{4,3,2,1,0:T(8,128)(2,1)} %bitcast.16), channel_id=1, source_target_pairs={{1,0},{0,1},{3,2},{2,3},{5,4},{4,5},{7,6},{6,7},{9,8},{8,9},{11,10... | collective-permute-start | bytes 3145736 | tf_op jit(solution)/shard_map/ppermute | solution.py:277
  1.6 1.8 %collective-permute-start.1 = (f32[2,32,8,128]{3,2,1,0:T(8,128)S(1)}, f32[2,32,8,128]{3,2,1,0:T(8,128)S(1)}, u32[]{:S(2)}, u32[]{:S(2)}) collective-permute-start(f32[2,32,8,128]{3,2,1,0:T(8,128)S(1)} %get-tuple-element.58), channel_id=1, source_target_pairs={{1,0},{0,1},{3,2},{2,3},{5,4},{4,5},{7,6},{6,7},{9,8},{8,9},{11,10... | collective-permute-start | bytes 786440 | tf_op jit(solution)/shard_map/ppermute | solution.py:277
  5.0 10.8 %collective-permute-start.2 = (f16[65,8,128]{2,1,0:T(8,128)(2,1)S(1)}, f16[65,8,128]{2,1,0:T(8,128)(2,1)S(1)}, u32[]{:S(2)}, u32[]{:S(2)}) collective-permute-start(f16[65,8,128]{2,1,0:T(8,128)(2,1)S(1)} %convert_element_type.36), channel_id=1, source_target_pairs={{0,2},{1,3},{2,4},{3,5},{4,6},{5,7},{6,8},{7,9},{8,10},{9,11},{10,... | collective-permute-start | bytes 399368 | tf_op jit(solution)/shard_map/ppermute | solution.py:286
  9.6 9.0 %collective-permute-start.6 = (f16[65,8,128]{2,1,0:T(8,128)(2,1)S(1)}, f16[65,8,128]{2,1,0:T(8,128)(2,1)S(1)}, u32[]{:S(2)}, u32[]{:S(2)}) collective-permute-start(f16[65,8,128]{2,1,0:T(8,128)(2,1)S(1)} %convert_element_type.42), channel_id=1, source_target_pairs={{0,2},{1,3},{2,4},{3,5},{4,6},{5,7},{6,8},{7,9},{8,10},{9,11},{10,... | collective-permute-start | bytes 399368 | tf_op jit(solution)/shard_map/ppermute | solution.py:286
  17.6 9.2 %collective-permute-start.3 = (f16[65,8,128]{2,1,0:T(8,128)(2,1)S(1)}, f16[65,8,128]{2,1,0:T(8,128)(2,1)S(1)}, u32[]{:S(2)}, u32[]{:S(2)}) collective-permute-start(f16[65,8,128]{2,1,0:T(8,128)(2,1)S(1)} %convert_element_type.38), channel_id=1, source_target_pairs={{0,2},{1,3},{2,4},{3,5},{4,6},{5,7},{6,8},{7,9},{8,10},{9,11},{10,... | collective-permute-start | bytes 399368 | tf_op jit(solution)/shard_map/ppermute | solution.py:286
  20.4 8.7 %collective-permute-start.7 = (f16[65,8,128]{2,1,0:T(8,128)(2,1)S(1)}, f16[65,8,128]{2,1,0:T(8,128)(2,1)S(1)}, u32[]{:S(2)}, u32[]{:S(2)}) collective-permute-start(f16[65,8,128]{2,1,0:T(8,128)(2,1)S(1)} %convert_element_type.44), channel_id=1, source_target_pairs={{0,2},{1,3},{2,4},{3,5},{4,6},{5,7},{6,8},{7,9},{8,10},{9,11},{10,... | collective-permute-start | bytes 399368 | tf_op jit(solution)/shard_map/ppermute | solution.py:286
  28.5 10.0 %collective-permute-start.4 = (f16[65,8,128]{2,1,0:T(8,128)(2,1)S(1)}, f16[65,8,128]{2,1,0:T(8,128)(2,1)S(1)}, u32[]{:S(2)}, u32[]{:S(2)}) collective-permute-start(f16[65,8,128]{2,1,0:T(8,128)(2,1)S(1)} %convert_element_type.40), channel_id=1, source_target_pairs={{0,2},{1,3},{2,4},{3,5},{4,6},{5,7},{6,8},{7,9},{8,10},{9,11},{10,... | collective-permute-start | bytes 399368 | tf_op jit(solution)/shard_map/ppermute | solution.py:286
  30.8 9.3 %collective-permute-start.8 = (f16[65,8,128]{2,1,0:T(8,128)(2,1)S(1)}, f16[65,8,128]{2,1,0:T(8,128)(2,1)S(1)}, u32[]{:S(2)}, u32[]{:S(2)}) collective-permute-start(f16[65,8,128]{2,1,0:T(8,128)(2,1)S(1)} %convert_element_type.46), channel_id=1, source_target_pairs={{0,2},{1,3},{2,4},{3,5},{4,6},{5,7},{6,8},{7,9},{8,10},{9,11},{10,... | collective-permute-start | bytes 399368 | tf_op jit(solution)/shard_map/ppermute | solution.py:286
  39.9 10.0 %collective-permute-start.5 = (f32[1,32,8,128]{3,2,1,0:T(8,128)S(1)}, f32[1,32,8,128]{3,2,1,0:T(8,128)S(1)}, u32[]{:S(2)}, u32[]{:S(2)}) collective-permute-start(f32[1,32,8,128]{3,2,1,0:T(8,128)S(1)} %get-tuple-element.39), channel_id=1, source_target_pairs={{0,2},{1,3},{2,4},{3,5},{4,6},{5,7},{6,8},{7,9},{8,10},{9,11},{10,... | collective-permute-start | bytes 393224 | tf_op jit(solution)/shard_map/ppermute | solution.py:286
  40.0 10.0 %collective-permute-start.10 = (f32[1,32,8,128]{3,2,1,0:T(8,128)S(1)}, f32[1,32,8,128]{3,2,1,0:T(8,128)S(1)}, u32[]{:S(2)}, u32[]{:S(2)}) collective-permute-start(f32[1,32,8,128]{3,2,1,0:T(8,128)S(1)} %get-tuple-element.49), channel_id=1, source_target_pairs={{0,3},{1,2},{2,5},{3,4},{4,7},{5,6},{6,9},{7,8},{8,11},{9,10},{10,... | collective-permute-start | bytes 393224 | tf_op jit(solution)/shard_map/ppermute | solution.py:286
  40.1 9.9 %collective-permute-start.12 = (f32[1,32,8,128]{3,2,1,0:T(8,128)S(1)}, f32[1,32,8,128]{3,2,1,0:T(8,128)S(1)}, u32[]{:S(2)}, u32[]{:S(2)}) collective-permute-start(f32[1,32,8,128]{3,2,1,0:T(8,128)S(1)} %get-tuple-element.53), channel_id=1, source_target_pairs={{1,0},{0,1},{3,2},{2,3},{5,4},{4,5},{7,6},{6,7},{9,8},{8,9},{11,10... | collective-permute-start | bytes 393224 | tf_op jit(solution)/shard_map/ppermute | solution.py:277
  41.7 13.4 %collective-permute-start.9 = (f32[1,32,8,128]{3,2,1,0:T(8,128)S(1)}, f32[1,32,8,128]{3,2,1,0:T(8,128)S(1)}, u32[]{:S(2)}, u32[]{:S(2)}) collective-permute-start(f32[1,32,8,128]{3,2,1,0:T(8,128)S(1)} %get-tuple-element.48), channel_id=1, source_target_pairs={{0,2},{1,3},{2,4},{3,5},{4,6},{5,7},{6,8},{7,9},{8,10},{9,11},{10,... | collective-permute-start | bytes 393224 | tf_op jit(solution)/shard_map/ppermute | solution.py:286
  41.7 13.3 %collective-permute-start.11 = (f32[1,32,8,128]{3,2,1,0:T(8,128)S(1)}, f32[1,32,8,128]{3,2,1,0:T(8,128)S(1)}, u32[]{:S(2)}, u32[]{:S(2)}) collective-permute-start(f32[1,32,8,128]{3,2,1,0:T(8,128)S(1)} %get-tuple-element.50), channel_id=1, source_target_pairs={{0,3},{1,2},{2,5},{3,4},{4,7},{5,6},{6,9},{7,8},{8,11},{9,10},{10,... | collective-permute-start | bytes 393224 | tf_op jit(solution)/shard_map/ppermute | solution.py:286
  49.9 5.1 %collective-permute-start.13 = (f32[1,32,8,128]{3,2,1,0:T(8,128)S(1)}, f32[1,32,8,128]{3,2,1,0:T(8,128)S(1)}, u32[]{:S(2)}, u32[]{:S(2)}) collective-permute-start(f32[1,32,8,128]{3,2,1,0:T(8,128)S(1)} %get-tuple-element.54), channel_id=1, source_target_pairs={{1,0},{0,1},{3,2},{2,3},{5,4},{4,5},{7,6},{6,7},{9,8},{8,9},{11,10... | collective-permute-start | bytes 393224 | tf_op jit(solution)/shard_map/ppermute | solution.py:277

commit v3 on v2

--- a/solution.py
+++ b/solution.py
@@ -88,11 +88,10 @@
     else:
         previous, message, missed = take(3)
         start = take(pieces) if final else take(1)
-    if final:
-        moved = take(pieces)
-    else:
-        sent, error = take(2)
+    sent = take(pieces) if final else take(1)
+    error = None if final else take(1)[0]
     ping, pong = refs
+    each = count // len(sent)
 
     if not first:
         back = jnp.exp2(message[count] - TOP)
@@ -113,25 +112,22 @@
         value = 0.2**depth * done[j, pl.ds(SUB + SUB * b, SUB), :]
         if not first:
             value = value + missed[m]
-        if final:
-            moved[piece][0, j, at, :] = value
-        else:
-            sent[m] = value
-            size = jnp.abs(value)
-            largest = size if largest is None else jnp.maximum(largest, size)
-    if final:
-        return
+        sent[m // each][m % each] = value
+        size = jnp.abs(value)
+        largest = size if largest is None else jnp.maximum(largest, size)
     largest = jnp.broadcast_to(jnp.max(largest, axis=(0, 1), keepdims=True), (SUB, LANE))
     power = jnp.clip(jnp.floor(jnp.log2(largest)), -100.0, 100.0)
     scale, back = jnp.exp2(TOP - power), jnp.exp2(power - TOP)
-    sent[count] = power
+    for message in sent:
+        message[each] = power
     for m in range(count):
-        value = sent[m]
+        value = sent[m // each][m % each]
         scaled = value * scale
         wide = scaled * 8193.0
         short = wide - (wide - scaled)
-        sent[m] = short
-        error[m] = short * back - value
+        sent[m // each][m % each] = short
+        if not final:
+            error[m] = short * back - value
 
 
 @functools.partial(jax.jit, static_argnames=("index", "final"))
@@ -141,9 +137,10 @@
     count = pieces * columns * height // SUB
     first = isinstance(state, list)
     shape = lambda *s: jax.ShapeDtypeStruct(s + (lane,), jnp.float32)
-    parts = [shape(1, columns, height)] * pieces
-    outs = [] if first else (parts if final else [shape(pieces, columns, height)])
-    outs = outs + (parts if final else [shape(count + 1, SUB), shape(count, SUB)])
+    if final:
+        outs = [shape(1, columns, height)] * pieces + [shape(count // pieces + 1, SUB)] * pieces
+    else:
+        outs = ([] if first else [shape(pieces, columns, height)]) + [shape(count + 1, SUB), shape(count, SUB)]
     scratch = pltpu.VMEM((columns, pieces * height + 2 * SUB, lane), jnp.float32)
     args = [*velocity, *state]
     out = pl.pallas_call(
@@ -190,12 +187,16 @@
     residual, gram, lines = refs[2 * groups :]
     count, columns, height, _ = residual.shape
     sums = {}
+    coded = len(arrived[0].shape) == 3
+    backs = [jnp.exp2(a[a.shape[0] - 1] - TOP) for a in arrived] if coded else []
     for j in range(columns):
         for at in range(0, height, SUB):
-            values = []
-            for a, s in zip(arrived, start):
-                for i in range(a.shape[0]):
-                    values.append(a[i, j, pl.ds(at, SUB), :] - s[i, j, pl.ds(at, SUB), :])
+            values = [-s[0, j, pl.ds(at, SUB), :] for s in start]
+            for p, a in enumerate(arrived):
+                if coded:
+                    values[p] = a[(j * height + at) // SUB] * backs[p] + values[p]
+                else:
+                    values[p] = a[0, j, pl.ds(at, SUB), :] + values[p]
             for p in range(count):
                 residual[p, j, pl.ds(at, SUB), :] = values[p]
                 for q in range(p + 1):
@@ -217,8 +218,8 @@
 
 
 def local_gram(shift, arrived, start, copies):
-    count = sum(a.shape[0] for a in arrived)
-    shape = (count,) + arrived[0].shape[1:]
+    count = len(arrived)
+    shape = (count,) + start[0].shape[1:]
     return pl.pallas_call(
         functools.partial(gram_kernel, len(arrived)),
         out_shape=[jax.ShapeDtypeStruct(shape, jnp.float32), jax.ShapeDtypeStruct((copies, LANE), jnp.float32)],
@@ -277,6 +278,10 @@
     return lax.ppermute(value, "slab", [((i + distance) % size, i) for i in range(size)])
 
 
+def sent_short(message, turn=0):
+    return to_next(message.astype(jnp.float16), turn).astype(jnp.float32)
+
+
 def to_next(value, turn=0):
     segs, slabs = lax.axis_size("seg"), lax.axis_size("slab")
     route = []
@@ -303,8 +308,7 @@
     moved, missed = [f[0] for f in firsts], [f[1] for f in firsts]
     for hop in range(1, HOPS):
         for i in range(share):
-            message = to_next(moved[i].astype(jnp.float16)).astype(jnp.float32)
-            state = (previous[i], message, missed[i])
+            state = (previous[i], sent_short(moved[i]), missed[i])
             if hop + 1 < HOPS:
                 previous[i], moved[i], missed[i] = propagate(speeds, state)
             else:
@@ -313,7 +317,7 @@
     for d in range(slabs):
         for i in range(share):
             at = (slabs - d) % slabs
-            arrived.append(to_next(moved[i][at], at))
+            arrived.append(sent_short(moved[i][at], at))
             begun.append(from_slab(previous[i][at], d) if d else previous[i][0])
     shift = jnp.full((1,), mine * share, jnp.int32)
     return shift, arrived, begun

time: 65.3 us -> 65.7 us (level)
  transfers between devices with their start and end apart: 14 -> 14, of which waited for: 8 -> 10; matrix products, arithmetic and copies ran while one was open for 2% -> 2% of each run, Pallas kernels for 17% -> 18%
where the time goes in v3:
time: 65.7 us; the launch traced here: 65.6 us
  waiting for transfers between devices  34.3 us (52%)
  Pallas kernels  14.5 us (22%)
  blocking collectives  8.86 us (13%)
  starting transfers between devices  6.14 us (9%)
  local copies, waits for them, and re-layouts  1.1 us (2%)
    ppermute x10, waiting for transfers between devices, to_next(): return lax.ppermute(value, ('seg', 'slab'), route)  32.6 us
    pallas_call x8, Pallas kernels, propagate(): pl.pallas_call(functools.partial(propagate_kernel, pieces, index, first,...  13.2 us
    all_to_all x1, blocking collectives, shards(): gram = lax.all_to_all(gram, axes, 0, 0, tiled=True)  8.86 us
    ppermute x10, starting transfers between devices, to_next(): return lax.ppermute(value, ('seg', 'slab'), route)  4.85 us
    ppermute x4, waiting for transfers between devices, from_slab(): lax.ppermute(value, 'slab', [((i + distance) % size, i) for i in range(si...  1.62 us
  transfers between devices with their start and end apart: 14, of which 10 were waited for; matrix products, arithmetic and copies ran while one was open for 2% of the time, Pallas kernels for 18%

profile of v3, /device:TPU:0, one launch (start us, length us, event | category | flops | bytes accessed | tf_op | source)
XLA Modules:
  0.0 65.6 jit_solution(680607266943871358)
XLA Ops:
  0.0 0.5 collective-permute-start
  0.5 1.1 %dynamic-slice_bitcast_fusion.1 = (f32[2,32,8,128]{3,2,1,0:T(8,128)S(1)}, f32[2,32,8,128]{3,2,1,0:T(8,128)S(1)}) fusion(f32[4,8,32,128]{3,1,2,0:T(8,128)} %bitcast.27, s32[]{:T(128)S(6)} %select_n.6, s32[]{:T(128)S(6)} %select_n.7), kind=kLoop, calls=%fused_computation.3 | loop fusion | bytes 1048584 | tf_op jit(solution)/shard_map/dynamic_slice | solution.py:300
  1.8 1.6 %collective-permute-done.1.refs_3_ = f32[2,32,8,128]{3,2,1,0:T(8,128)S(1)} collective-permute-done((f32[2,32,8,128]{3,2,1,0:T(8,128)S(1)}, f32[2,32,8,128]{3,2,1,0:T(8,128)S(1)}, u32[]{:S(2)}, u32[]{:S(2)}) %collective-permute-start.1) | collective-permute-done | bytes 262176 | tf_op jit(solution)/shard_map/ppermute | solution.py:278
  3.4 1.6 %propagate.8 = (f32[65,8,128]{2,1,0:T(8,128)S(1)}, f32[64,8,128]{2,1,0:T(8,128)S(1)}) custom-call(bf16[8,2,32,8,128]{4,3,2,1,0:T(8,128)(2,1)S(1)} %bitcast.17, bf16[8,2,32,8,128]{4,3,2,1,0:T(8,128)(2,1)S(1)} %collective-permute-done.refs_1_, f32[2,32,8,128]{3,2,1,0:T(8,128)S(1)} %get-tuple-element.57.refs_2_, ...), custom_call_target="tpu_custom_call" | custom-call | tf_op jit(solution)/shard_map/jit(propagate)/propagate/pallas_call | solution.py:146
  5.0 2.9 %collective-permute-start.2 = (f16[65,8,128]{2,1,0:T(8,128)(2,1)S(1)}, f16[65,8,128]{2,1,0:T(8,128)(2,1)S(1)}, u32[]{:S(2)}, u32[]{:S(2)}) collective-permute-start(f16[65,8,128]{2,1,0:T(8,128)(2,1)S(1)} %convert_element_type.60), channel_id=1, source_target_pairs={{0,2},{1,3},{2,4},{3,5},{4,6},{5,7},{6,8},{7,9},{8,10},{9,11},{10,... | collective-permute-start | bytes 399368 | tf_op jit(solution)/shard_map/ppermute | solution.py:291
  8.0 1.6 %propagate.12 = (f32[65,8,128]{2,1,0:T(8,128)S(1)}, f32[64,8,128]{2,1,0:T(8,128)S(1)}) custom-call(bf16[8,2,32,8,128]{4,3,2,1,0:T(8,128)(2,1)S(1)} %bitcast.18, bf16[8,2,32,8,128]{4,3,2,1,0:T(8,128)(2,1)S(1)} %collective-permute-done.refs_1_, f32[2,32,8,128]{3,2,1,0:T(8,128)S(1)} %get-tuple-element.57.refs_2_, ...), custom_call_target="tpu_custom_call" | custom-call | tf_op jit(solution)/shard_map/jit(propagate)/propagate/pallas_call | solution.py:146
  9.6 1.5 %collective-permute-start.6 = (f16[65,8,128]{2,1,0:T(8,128)(2,1)S(1)}, f16[65,8,128]{2,1,0:T(8,128)(2,1)S(1)}, u32[]{:S(2)}, u32[]{:S(2)}) collective-permute-start(f16[65,8,128]{2,1,0:T(8,128)(2,1)S(1)} %convert_element_type.68), channel_id=1, source_target_pairs={{0,2},{1,3},{2,4},{3,5},{4,6},{5,7},{6,8},{7,9},{8,10},{9,11},{10,... | collective-permute-start | bytes 399368 | tf_op jit(solution)/shard_map/ppermute | solution.py:291
  11.2 4.6 %collective-permute-done.2 = f16[65,8,128]{2,1,0:T(8,128)(2,1)S(1)} collective-permute-done((f16[65,8,128]{2,1,0:T(8,128)(2,1)S(1)}, f16[65,8,128]{2,1,0:T(8,128)(2,1)S(1)}, u32[]{:S(2)}, u32[]{:S(2)}) %collective-permute-start.2) | collective-permute-done | bytes 133152 | tf_op jit(solution)/shard_map/ppermute | solution.py:291
  15.8 1.7 %propagate.9 = (f32[2,32,8,128]{3,2,1,0:T(8,128)S(1)}, f32[65,8,128]{2,1,0:T(8,128)S(1)}, f32[64,8,128]{2,1,0:T(8,128)S(1)}) custom-call(bf16[8,2,32,8,128]{4,3,2,1,0:T(8,128)(2,1)S(1)} %bitcast.19, bf16[8,2,32,8,128]{4,3,2,1,0:T(8,128)(2,1)S(1)} %collective-permute-done.refs_1_, f32[2,32,8,128]{3,2,1,0:T(8,128)S(1)} %pad_maximum_fusion.refs_2_, ...), custom_call_target="tpu_custom_call" | custom-call | tf_op jit(solution)/shard_map/jit(propagate)/propagate/pallas_call | solution.py:146
  17.7 1.0 %collective-permute-done.6 = f16[65,8,128]{2,1,0:T(8,128)(2,1)S(1)} collective-permute-done((f16[65,8,128]{2,1,0:T(8,128)(2,1)S(1)}, f16[65,8,128]{2,1,0:T(8,128)(2,1)S(1)}, u32[]{:S(2)}, u32[]{:S(2)}) %collective-permute-start.6) | collective-permute-done | bytes 133152 | tf_op jit(solution)/shard_map/ppermute | solution.py:291
  18.7 1.7 %propagate.13 = (f32[2,32,8,128]{3,2,1,0:T(8,128)S(1)}, f32[65,8,128]{2,1,0:T(8,128)S(1)}, f32[64,8,128]{2,1,0:T(8,128)S(1)}) custom-call(bf16[8,2,32,8,128]{4,3,2,1,0:T(8,128)(2,1)S(1)} %bitcast.20, bf16[8,2,32,8,128]{4,3,2,1,0:T(8,128)(2,1)S(1)} %collective-permute-done.refs_1_, f32[2,32,8,128]{3,2,1,0:T(8,128)S(1)} %pad_maximum_fusion.1.refs_2_, ...), custom_call_target="tpu_custom_call" | custom-call | tf_op jit(solution)/shard_map/jit(propagate)/propagate/pallas_call | solution.py:146
  20.4 6.3 %collective-permute-done.3 = f16[65,8,128]{2,1,0:T(8,128)(2,1)S(1)} collective-permute-done((f16[65,8,128]{2,1,0:T(8,128)(2,1)S(1)}, f16[65,8,128]{2,1,0:T(8,128)(2,1)S(1)}, u32[]{:S(2)}, u32[]{:S(2)}) %collective-permute-start.3) | collective-permute-done | bytes 133152 | tf_op jit(solution)/shard_map/ppermute | solution.py:291
  26.8 1.7 %propagate.10 = (f32[2,32,8,128]{3,2,1,0:T(8,128)S(1)}, f32[65,8,128]{2,1,0:T(8,128)S(1)}, f32[64,8,128]{2,1,0:T(8,128)S(1)}) custom-call(bf16[8,2,32,8,128]{4,3,2,1,0:T(8,128)(2,1)S(1)} %bitcast.21, bf16[8,2,32,8,128]{4,3,2,1,0:T(8,128)(2,1)S(1)} %collective-permute-done.refs_1_, f32[2,32,8,128]{3,2,1,0:T(8,128)S(1)} %get-tuple-element.33.refs_2_, ...), custom_call_target="tpu_custom_call" | custom-call | tf_op jit(solution)/shard_map/jit(propagate)/propagate/pallas_call | solution.py:146
  28.5 0.5 collective-permute-done.7
  29.1 1.7 %propagate.14 = (f32[2,32,8,128]{3,2,1,0:T(8,128)S(1)}, f32[65,8,128]{2,1,0:T(8,128)S(1)}, f32[64,8,128]{2,1,0:T(8,128)S(1)}) custom-call(bf16[8,2,32,8,128]{4,3,2,1,0:T(8,128)(2,1)S(1)} %bitcast.22, bf16[8,2,32,8,128]{4,3,2,1,0:T(8,128)(2,1)S(1)} %collective-permute-done.refs_1_, f32[2,32,8,128]{3,2,1,0:T(8,128)S(1)} %get-tuple-element.42.refs_2_, ...), custom_call_target="tpu_custom_call" | custom-call | tf_op jit(solution)/shard_map/jit(propagate)/propagate/pallas_call | solution.py:146
  30.9 7.6 %collective-permute-done.4 = f16[65,8,128]{2,1,0:T(8,128)(2,1)S(1)} collective-permute-done((f16[65,8,128]{2,1,0:T(8,128)(2,1)S(1)}, f16[65,8,128]{2,1,0:T(8,128)(2,1)S(1)}, u32[]{:S(2)}, u32[]{:S(2)}) %collective-permute-start.4) | collective-permute-done | bytes 133152 | tf_op jit(solution)/shard_map/ppermute | solution.py:291
  38.4 1.6 %propagate.11 = (f32[1,32,8,128]{3,2,1,0:T(8,128)S(1)}, f32[1,32,8,128]{3,2,1,0:T(8,128)S(1)}, f32[33,8,128]{2,1,0:T(8,128)S(1)}, f32[33,8,128]{2,1,0:T(8,128)S(1)}) custom-call(bf16[8,2,32,8,128]{4,3,2,1,0:T(8,128)(2,1)S(1)} %bitcast.23, bf16[8,2,32,8,128]{4,3,2,1,0:T(8,128)(2,1)S(1)} %collective-permute-done.refs_1_, ...), custom_call_target="tpu_custom_call" | custom-call | tf_op jit(solution)/shard_map/jit(propagate)/propagate/pallas_call | solution.py:146
  40.3 1.6 %propagate.15 = (f32[1,32,8,128]{3,2,1,0:T(8,128)S(1)}, f32[1,32,8,128]{3,2,1,0:T(8,128)S(1)}, f32[33,8,128]{2,1,0:T(8,128)S(1)}, f32[33,8,128]{2,1,0:T(8,128)S(1)}) custom-call(bf16[8,2,32,8,128]{4,3,2,1,0:T(8,128)(2,1)S(1)} %bitcast.24, bf16[8,2,32,8,128]{4,3,2,1,0:T(8,128)(2,1)S(1)} %collective-permute-done.refs_1_, ...), custom_call_target="tpu_custom_call" | custom-call | tf_op jit(solution)/shard_map/jit(propagate)/propagate/pallas_call | solution.py:146
  41.9 0.6 collective-permute-start.13
  42.7 4.8 %collective-permute-done.10 = f16[33,8,128]{2,1,0:T(8,128)(2,1)S(1)} collective-permute-done((f16[33,8,128]{2,1,0:T(8,128)(2,1)S(1)}, f16[33,8,128]{2,1,0:T(8,128)(2,1)S(1)}, u32[]{:S(2)}, u32[]{:S(2)}) %collective-permute-start.10) | collective-permute-done | bytes 67616 | tf_op jit(solution)/shard_map/ppermute | solution.py:291
  47.5 3.7 %collective-permute-done.5 = f16[33,8,128]{2,1,0:T(8,128)(2,1)S(1)} collective-permute-done((f16[33,8,128]{2,1,0:T(8,128)(2,1)S(1)}, f16[33,8,128]{2,1,0:T(8,128)(2,1)S(1)}, u32[]{:S(2)}, u32[]{:S(2)}) %collective-permute-start.5) | collective-permute-done | bytes 67616 | tf_op jit(solution)/shard_map/ppermute | solution.py:291
  51.3 4.0 %collective-permute-done.9 = f16[33,8,128]{2,1,0:T(8,128)(2,1)S(1)} collective-permute-done((f16[33,8,128]{2,1,0:T(8,128)(2,1)S(1)}, f16[33,8,128]{2,1,0:T(8,128)(2,1)S(1)}, u32[]{:S(2)}, u32[]{:S(2)}) %collective-permute-start.9) | collective-permute-done | bytes 67616 | tf_op jit(solution)/shard_map/ppermute | solution.py:291
  55.7 8.9 %all_to_all.11 = f32[32,1,128]{2,1,0:T(1,128)S(1)} all-to-all(f32[32,1,128]{2,1,0:T(1,128)S(1)} %bitcast.26), channel_id=1, replica_groups=mesh['seg'=16,'slab'=2] {'seg','slab'}, dimensions={0} | all-to-all | bytes 32768 | tf_op jit(solution)/shard_map/all_to_all | solution.py:350
  64.5 1.0 %solve.1 = f32[4,32,8,128]{3,2,1,0:T(8,128)} custom-call(s32[1]{0:T(128)} %bitcast.refs_0_.base, f32[32,128]{1,0:T(8,128)S(1)} %bitcast.25, f32[4,32,8,128]{3,2,1,0:T(8,128)S(1)} %get-tuple-element.56.residual), custom_call_target="tpu_custom_call" | custom-call | tf_op jit(solution)/shard_map/solve/pallas_call | solution.py:266
  (42 shorter events, 1.5 us)
Async XLA Ops:
  0.0 3.4 %copy-start = (bf16[1,8,2,8,4096]{4,3,2,1,0:T(8,128)(2,1)S(1)}, bf16[1,8,2,8,4096]{4,3,2,1,0:T(8,128)(2,1)}, u32[]{:S(2)}) copy-start(bf16[1,8,2,8,4096]{4,3,2,1,0:T(8,128)(2,1)} %param.3) | copy-start | bytes 3145732
  0.0 3.4 %collective-permute-start = (bf16[8,2,32,8,128]{4,3,2,1,0:T(8,128)(2,1)}, bf16[8,2,32,8,128]{4,3,2,1,0:T(8,128)(2,1)S(1)}, u32[]{:S(2)}, u32[]{:S(2)}) collective-permute-start(bf16[8,2,32,8,128]{4,3,2,1,0:T(8,128)(2,1)} %bitcast.16), channel_id=1, source_target_pairs={{1,0},{0,1},{3,2},{2,3},{5,4},{4,5},{7,6},{6,7},{9,8},{8,9},{11,10... | collective-permute-start | bytes 3145736 | tf_op jit(solution)/shard_map/ppermute | solution.py:278
  1.6 1.8 %collective-permute-start.1 = (f32[2,32,8,128]{3,2,1,0:T(8,128)S(1)}, f32[2,32,8,128]{3,2,1,0:T(8,128)S(1)}, u32[]{:S(2)}, u32[]{:S(2)}) collective-permute-start(f32[2,32,8,128]{3,2,1,0:T(8,128)S(1)} %get-tuple-element.58), channel_id=1, source_target_pairs={{1,0},{0,1},{3,2},{2,3},{5,4},{4,5},{7,6},{6,7},{9,8},{8,9},{11,10... | collective-permute-start | bytes 786440 | tf_op jit(solution)/shard_map/ppermute | solution.py:278
  5.0 10.8 %collective-permute-start.2 = (f16[65,8,128]{2,1,0:T(8,128)(2,1)S(1)}, f16[65,8,128]{2,1,0:T(8,128)(2,1)S(1)}, u32[]{:S(2)}, u32[]{:S(2)}) collective-permute-start(f16[65,8,128]{2,1,0:T(8,128)(2,1)S(1)} %convert_element_type.60), channel_id=1, source_target_pairs={{0,2},{1,3},{2,4},{3,5},{4,6},{5,7},{6,8},{7,9},{8,10},{9,11},{10,... | collective-permute-start | bytes 399368 | tf_op jit(solution)/shard_map/ppermute | solution.py:291
  9.6 9.0 %collective-permute-start.6 = (f16[65,8,128]{2,1,0:T(8,128)(2,1)S(1)}, f16[65,8,128]{2,1,0:T(8,128)(2,1)S(1)}, u32[]{:S(2)}, u32[]{:S(2)}) collective-permute-start(f16[65,8,128]{2,1,0:T(8,128)(2,1)S(1)} %convert_element_type.68), channel_id=1, source_target_pairs={{0,2},{1,3},{2,4},{3,5},{4,6},{5,7},{6,8},{7,9},{8,10},{9,11},{10,... | collective-permute-start | bytes 399368 | tf_op jit(solution)/shard_map/ppermute | solution.py:291
  17.6 9.2 %collective-permute-start.3 = (f16[65,8,128]{2,1,0:T(8,128)(2,1)S(1)}, f16[65,8,128]{2,1,0:T(8,128)(2,1)S(1)}, u32[]{:S(2)}, u32[]{:S(2)}) collective-permute-start(f16[65,8,128]{2,1,0:T(8,128)(2,1)S(1)} %convert_element_type.62), channel_id=1, source_target_pairs={{0,2},{1,3},{2,4},{3,5},{4,6},{5,7},{6,8},{7,9},{8,10},{9,11},{10,... | collective-permute-start | bytes 399368 | tf_op jit(solution)/shard_map/ppermute | solution.py:291
  20.4 8.7 %collective-permute-start.7 = (f16[65,8,128]{2,1,0:T(8,128)(2,1)S(1)}, f16[65,8,128]{2,1,0:T(8,128)(2,1)S(1)}, u32[]{:S(2)}, u32[]{:S(2)}) collective-permute-start(f16[65,8,128]{2,1,0:T(8,128)(2,1)S(1)} %convert_element_type.70), channel_id=1, source_target_pairs={{0,2},{1,3},{2,4},{3,5},{4,6},{5,7},{6,8},{7,9},{8,10},{9,11},{10,... | collective-permute-start | bytes 399368 | tf_op jit(solution)/shard_map/ppermute | solution.py:291
  28.5 10.0 %collective-permute-start.4 = (f16[65,8,128]{2,1,0:T(8,128)(2,1)S(1)}, f16[65,8,128]{2,1,0:T(8,128)(2,1)S(1)}, u32[]{:S(2)}, u32[]{:S(2)}) collective-permute-start(f16[65,8,128]{2,1,0:T(8,128)(2,1)S(1)} %convert_element_type.64), channel_id=1, source_target_pairs={{0,2},{1,3},{2,4},{3,5},{4,6},{5,7},{6,8},{7,9},{8,10},{9,11},{10,... | collective-permute-start | bytes 399368 | tf_op jit(solution)/shard_map/ppermute | solution.py:291
  30.8 9.5 %collective-permute-start.8 = (f16[65,8,128]{2,1,0:T(8,128)(2,1)S(1)}, f16[65,8,128]{2,1,0:T(8,128)(2,1)S(1)}, u32[]{:S(2)}, u32[]{:S(2)}) collective-permute-start(f16[65,8,128]{2,1,0:T(8,128)(2,1)S(1)} %convert_element_type.72), channel_id=1, source_target_pairs={{0,2},{1,3},{2,4},{3,5},{4,6},{5,7},{6,8},{7,9},{8,10},{9,11},{10,... | collective-permute-start | bytes 399368 | tf_op jit(solution)/shard_map/ppermute | solution.py:291
  40.1 7.4 %collective-permute-start.10 = (f16[33,8,128]{2,1,0:T(8,128)(2,1)S(1)}, f16[33,8,128]{2,1,0:T(8,128)(2,1)S(1)}, u32[]{:S(2)}, u32[]{:S(2)}) collective-permute-start(f16[33,8,128]{2,1,0:T(8,128)(2,1)S(1)} %convert_element_type.76), channel_id=1, source_target_pairs={{0,3},{1,2},{2,5},{3,4},{4,7},{5,6},{6,9},{7,8},{8,11},{9,10},{10,... | collective-permute-start | bytes 202760 | tf_op jit(solution)/shard_map/ppermute | solution.py:291
  40.2 15.2 %collective-permute-start.12 = (f32[1,32,8,128]{3,2,1,0:T(8,128)S(1)}, f32[1,32,8,128]{3,2,1,0:T(8,128)S(1)}, u32[]{:S(2)}, u32[]{:S(2)}) collective-permute-start(f32[1,32,8,128]{3,2,1,0:T(8,128)S(1)} %get-tuple-element.53), channel_id=1, source_target_pairs={{1,0},{0,1},{3,2},{2,3},{5,4},{4,5},{7,6},{6,7},{9,8},{8,9},{11,10... | collective-permute-start | bytes 393224 | tf_op jit(solution)/shard_map/ppermute | solution.py:278
  41.9 13.4 %collective-permute-start.13 = (f32[1,32,8,128]{3,2,1,0:T(8,128)S(1)}, f32[1,32,8,128]{3,2,1,0:T(8,128)S(1)}, u32[]{:S(2)}, u32[]{:S(2)}) collective-permute-start(f32[1,32,8,128]{3,2,1,0:T(8,128)S(1)} %get-tuple-element.54), channel_id=1, source_target_pairs={{1,0},{0,1},{3,2},{2,3},{5,4},{4,5},{7,6},{6,7},{9,8},{8,9},{11,10... | collective-permute-start | bytes 393224 | tf_op jit(solution)/shard_map/ppermute | solution.py:278
  42.5 8.7 %collective-permute-start.5 = (f16[33,8,128]{2,1,0:T(8,128)(2,1)S(1)}, f16[33,8,128]{2,1,0:T(8,128)(2,1)S(1)}, u32[]{:S(2)}, u32[]{:S(2)}) collective-permute-start(f16[33,8,128]{2,1,0:T(8,128)(2,1)S(1)} %convert_element_type.66), channel_id=1, source_target_pairs={{0,2},{1,3},{2,4},{3,5},{4,6},{5,7},{6,8},{7,9},{8,10},{9,11},{10,... | collective-permute-start | bytes 202760 | tf_op jit(solution)/shard_map/ppermute | solution.py:291
  42.6 8.7 %collective-permute-start.11 = (f16[33,8,128]{2,1,0:T(8,128)(2,1)S(1)}, f16[33,8,128]{2,1,0:T(8,128)(2,1)S(1)}, u32[]{:S(2)}, u32[]{:S(2)}) collective-permute-start(f16[33,8,128]{2,1,0:T(8,128)(2,1)S(1)} %convert_element_type.78), channel_id=1, source_target_pairs={{0,3},{1,2},{2,5},{3,4},{4,7},{5,6},{6,9},{7,8},{8,11},{9,10},{10,... | collective-permute-start | bytes 202760 | tf_op jit(solution)/shard_map/ppermute | solution.py:291
  47.5 7.9 %collective-permute-start.9 = (f16[33,8,128]{2,1,0:T(8,128)(2,1)S(1)}, f16[33,8,128]{2,1,0:T(8,128)(2,1)S(1)}, u32[]{:S(2)}, u32[]{:S(2)}) collective-permute-start(f16[33,8,128]{2,1,0:T(8,128)(2,1)S(1)} %convert_element_type.74), channel_id=1, source_target_pairs={{0,2},{1,3},{2,4},{3,5},{4,6},{5,7},{6,8},{7,9},{8,10},{9,11},{10,... | collective-permute-start | bytes 202760 | tf_op jit(solution)/shard_map/ppermute | solution.py:291

commit v4 on v2

v4 whole, which is shorter than its diff:
```python
import functools

import jax
import jax.numpy as jnp
from jax import lax
from jax.experimental import pallas as pl
from jax.experimental.pallas import tpu as pltpu
from jax.sharding import PartitionSpec as P

HOPS = 4
SUB = 8
LANE = 128
VMEM = pl.BlockSpec(memory_space=pltpu.VMEM)
SMEM = pl.BlockSpec(memory_space=pltpu.SMEM)


def tiled(rows):
    lead, (height, width) = rows.shape[:-2], rows.shape[-2:]
    cut = rows.reshape(lead + (height, width // LANE, LANE))
    return jnp.swapaxes(cut, -3, -2)


def untiled(tiles):
    lead, (count, height, lane) = tiles.shape[:-3], tiles.shape[-3:]
    return jnp.swapaxes(tiles, -3, -2).reshape(lead + (height, count * lane))


def advance(velocity, ping, pong, pieces):
    depth, _, columns, height, _ = velocity[0].shape
    rows = pieces * height
    lane = lax.broadcasted_iota(jnp.int32, (SUB, LANE), 1)
    first, last = lane == 0, lane == LANE - 1

    def step(k, source, target):
        for b in range(rows // SUB):
            piece, at = divmod(SUB * b, height)
            rows_at = pl.ds(SUB + SUB * b, SUB)
            here = [source[j % columns, rows_at, :] for j in (-1, 0, 1)]
            for j in range(columns):
                left, centre, right = here
                west = pltpu.roll(jnp.where(last, left, centre), 1, 1)
                east = pltpu.roll(jnp.where(first, right, centre), LANE - 1, 1)
                up = source[j, pl.ds(SUB + 1 + SUB * b, SUB), :]
                down = source[j, pl.ds(SUB - 1 + SUB * b, SUB), :]
                speed_x = velocity[piece][k, 0, j, pl.ds(at, SUB), :].astype(jnp.float32)
                speed_y = velocity[piece][k, 1, j, pl.ds(at, SUB), :].astype(jnp.float32)
                carried = speed_x * (west - east) + speed_y * (down - up)
                place(target, rows, j, b, 0.9 * centre + ((west + east) + (up + down)) + 0.25 * carried)
                here = [centre, right, source[(j + 2) % columns, rows_at, :]]

    def pair(i, carry):
        step(2 * i, ping, pong)
        step(2 * i + 1, pong, ping)
        return carry

    lax.fori_loop(0, depth // 2, pair, 0)
    if depth % 2:
        step(depth - 1, ping, pong)
        return pong
    return ping


def place(ref, rows, j, b, value):
    ref[j, pl.ds(SUB + SUB * b, SUB), :] = value
    if b == 0:
        ref[j, pl.ds(SUB + rows, 1), :] = value[:1]
    if b == rows // SUB - 1:
        ref[j, pl.ds(SUB - 1, 1), :] = value[SUB - 1 :]


def tiles_of(pieces, columns, height):
    for j in range(columns):
        for b in range(pieces * height // SUB):
            piece, at = divmod(SUB * b, height)
            yield piece, j, pl.ds(at, SUB), b, (piece * columns + j) * (height // SUB) + at // SUB


TOP = 13.0


def take_in(cases, use):
    def run(message, previous):
        count = message.shape[0] - 1
        back = jnp.exp2(message[count] - TOP)
        pieces, columns, height, _ = previous.shape
        for piece, j, at, b, m in tiles_of(pieces, columns, height):
            use(piece, j, at, b, message[m] * back - previous[piece, j, at, :])

    for chosen, message, previous in cases:
        pl.when(chosen)(functools.partial(run, message, previous))


def propagate_kernel(pieces, index, first, last, *refs):
    refs = list(refs)
    take = lambda count: [refs.pop(0) for _ in range(count)]
    (flags,) = take(1)
    velocity = take(pieces)
    depth, _, columns, height, _ = velocity[0].shape
    rows, count = pieces * height, pieces * columns * height // SUB
    if first:
        previous = take(pieces)
    else:
        previous, missed, message = take(3)
        wrapped = None if last else take(1)[0]
        (start,) = take(1)
    sent, error, ping, pong = refs

    @pl.when(flags[0] == (1 if last else 0))
    def _():
        def use(piece, j, at, b, value):
            start[piece, j, at, :] = value
            place(ping, rows, j, b, value)

        if first:
            for piece, j, at, b, m in tiles_of(pieces, columns, height):
                place(ping, rows, j, b, previous[piece][index, j, at, :])
        elif last:
            take_in([(flags[0] == 1, message, previous)], use)
        else:
            at_first = flags[1] == 1
            take_in([(at_first, wrapped, previous), (jnp.logical_not(at_first), message, previous)], use)

        done = advance(velocity, ping, pong, pieces)
        largest = None
        for piece, j, at, b, m in tiles_of(pieces, columns, height):
            value = 0.2**depth * done[j, pl.ds(SUB + SUB * b, SUB), :]
            if not first:
                value = value + missed[m]
            sent[m] = value
            size = jnp.abs(value)
            largest = size if largest is None else jnp.maximum(largest, size)
        largest = jnp.broadcast_to(jnp.max(largest, axis=(0, 1), keepdims=True), (SUB, LANE))
        power = jnp.clip(jnp.floor(jnp.log2(largest)), -100.0, 100.0)
        scale, back = jnp.exp2(TOP - power), jnp.exp2(power - TOP)
        sent[count] = power
        for m in range(count):
            value = sent[m]
            scaled = value * scale
            wide = scaled * 8193.0
            short = wide - (wide - scaled)
            sent[m] = short
            error[m] = short * back - value


@functools.partial(jax.jit, static_argnames=("index", "last"))
def propagate(flags, velocity, state, index=0, last=False):
    pieces = len(velocity)
    _, _, columns, height, lane = velocity[0].shape
    count = pieces * columns * height // SUB
    first = isinstance(state, list)
    shape = lambda *s: jax.ShapeDtypeStruct(s + (lane,), jnp.float32)
    outs = ([] if first else [shape(pieces, columns, height)]) + [shape(count + 1, SUB), shape(count, SUB)]
    scratch = pltpu.VMEM((columns, pieces * height + 2 * SUB, lane), jnp.float32)
    args = [*velocity, *state]
    return pl.pallas_call(
        functools.partial(propagate_kernel, pieces, index, first, last),
        out_shape=outs,
        in_specs=[SMEM] + [VMEM] * len(args),
        out_specs=[VMEM] * len(outs),
        scratch_shapes=[scratch, scratch],
        compiler_params=pltpu.CompilerParams(vmem_limit_bytes=16 << 20),
        name="propagate_last" if last else "propagate",
    )(flags, *args)


def residual_kernel(flags, message, wrapped, previous, previous_last, *outs):
    def use(piece, j, at, b, value):
        outs[piece][0, j, at, :] = value

    at_last, at_first = flags[0] == 1, flags[1] == 1
    rest = jnp.logical_not(jnp.logical_or(at_last, at_first))
    cases = [(at_last, message, previous_last), (at_first, wrapped, previous), (rest, message, previous)]
    take_in(cases, use)


@jax.jit
def last_residual(flags, *state):
    pieces, columns, height, lane = state[2].shape
    return pl.pallas_call(
        residual_kernel,
        out_shape=[jax.ShapeDtypeStruct((1, columns, height, lane), jnp.float32)] * pieces,
        in_specs=[SMEM] + [VMEM] * len(state),
        out_specs=[VMEM] * pieces,
        compiler_params=pltpu.CompilerParams(vmem_limit_bytes=16 << 20),
        name="residual",
    )(flags, *state)


def rows_kernel(pieces, index, *refs):
    velocity, previous, (moved, ping, pong) = refs[:pieces], refs[pieces : 2 * pieces], refs[2 * pieces :]
    depth, _, columns, height, _ = velocity[0].shape
    for piece, j, at, b, _ in tiles_of(pieces, columns, height):
        place(ping, pieces * height, j, b, previous[piece][index, j, at, :])
    done = advance(velocity, ping, pong, pieces)
    for piece, j, at, b, _ in tiles_of(1, columns, height):
        moved[0, j, at, :] = 0.2**depth * done[j, pl.ds(SUB + SUB * b, SUB), :]


@functools.partial(jax.jit, static_argnames=("index",))
def propagate_rows(velocity, state, index):
    pieces = len(velocity)
    _, _, columns, height, lane = velocity[0].shape
    scratch = pltpu.VMEM((columns, pieces * height + 2 * SUB, lane), jnp.float32)
    return pl.pallas_call(
        functools.partial(rows_kernel, pieces, index),
        out_shape=jax.ShapeDtypeStruct((1, columns, height, lane), jnp.float32),
        in_specs=[VMEM] * (2 * pieces),
        out_specs=VMEM,
        scratch_shapes=[scratch, scratch],
        compiler_params=pltpu.CompilerParams(vmem_limit_bytes=16 << 20),
        name="propagate_rows",
    )(*velocity, *state)


def gram_kernel(base, *refs):
    residual, (gram, lines) = refs[:-2], refs[-2:]
    count = len(residual)
    _, columns, height, _ = residual[0].shape
    sums = {}
    for j in range(columns):
        for at in range(0, height, SUB):
            values = [r[0, j, pl.ds(at, SUB), :] for r in residual]
            for p in range(count):
                for q in range(p + 1):
                    term = values[p] * values[q]
                    sums[p, q] = term if (p, q) not in sums else sums[p, q] + term
    for (p, q), total in sums.items():
        line = jnp.sum(total, axis=0, keepdims=True)
        a, b = lax.rem(base[0] + p, count), lax.rem(base[0] + q, count)
        lines[pl.ds(a * count + b, 1), :] = line
        if p != q:
            lines[pl.ds(b * count + a, 1), :] = line
    totals = jnp.where(diagonal(count), jnp.sum(lines[...], axis=1, keepdims=True), 0.0)
    gram[...] = jnp.broadcast_to(jnp.sum(totals, axis=0, keepdims=True), gram.shape)


def diagonal(count):
    shape = (count * count, LANE)
    return lax.broadcasted_iota(jnp.int32, shape, 0) == lax.broadcasted_iota(jnp.int32, shape, 1)


def local_gram(shift, residual, copies):
    count = len(residual)
    return pl.pallas_call(
        gram_kernel,
        out_shape=jax.ShapeDtypeStruct((copies, LANE), jnp.float32),
        in_specs=[SMEM] + [VMEM] * count,
        out_specs=VMEM,
        scratch_shapes=[pltpu.VMEM((count * count, LANE), jnp.float32)],
        compiler_params=pltpu.CompilerParams(vmem_limit_bytes=16 << 20),
        name="gram",
    )(shift, *residual)


def solve_kernel(base, gram, *refs):
    residual, out = refs[:-1], refs[-1]
    count, columns, height, lane = out.shape
    line = jnp.broadcast_to(jnp.sum(gram[...], axis=0, keepdims=True), (count * count, lane))
    total = jnp.sum(jnp.where(diagonal(count), line, 0.0), axis=1, keepdims=True)
    entry = lambda a, b: total[a * count + b : a * count + b + 1, :]
    lower, inverse = {}, {}
    for a in range(count):
        for b in range(a + 1):
            value = entry(a, b)
            for k in range(b):
                value = value - lower[a, k] * lower[b, k]
            lower[a, b] = jnp.sqrt(value) if a == b else value / lower[b, b]
    for a in range(count):
        inverse[a, a] = 1.0 / lower[a, a]
        for b in range(a):
            value = lower[a, b] * inverse[b, b]
            for k in range(b + 1, a):
                value = value + lower[a, k] * inverse[k, b]
            inverse[a, b] = -value / lower[a, a]
    factors = {at: jnp.broadcast_to(value, (SUB, lane)) for at, value in inverse.items()}

    def finish(place):
        for j in range(columns):
            for at in range(0, height, SUB):
                values = [residual[place[a]][0, j, pl.ds(at, SUB), :] for a in range(count)]
                for a in range(count):
                    value = factors[a, 0] * values[0]
                    for b in range(1, a + 1):
                        value = value + factors[a, b] * values[b]
                    out[a, j, pl.ds(at, SUB), :] = value

    for turn in range(count):
        pl.when(base[0] == turn)(functools.partial(finish, [(a - turn) % count for a in range(count)]))


def solved(shift, gram, residual):
    count, (_, columns, height, lane) = len(residual), residual[0].shape
    return pl.pallas_call(
        solve_kernel,
        out_shape=jax.ShapeDtypeStruct((count, columns, height, lane), jnp.float32),
        in_specs=[SMEM, VMEM] + [VMEM] * count,
        out_specs=VMEM,
        compiler_params=pltpu.CompilerParams(vmem_limit_bytes=16 << 20),
        name="solve",
    )(shift, gram, *residual)


def from_slab(value, distance):
    size = lax.axis_size("slab")
    return lax.ppermute(value, "slab", [((i + distance) % size, i) for i in range(size)])


def to_next(value, segments=None):
    size = lax.axis_size("seg")
    return lax.ppermute(value, "seg", [(i, (i + 1) % size) for i in segments or range(size)])


def sent_short(message, segments=None):
    return to_next(message.astype(jnp.float16), segments).astype(jnp.float32)


def split_vectors(vectors, velocity):
    slabs, mine = lax.axis_size("slab"), lax.axis_index("slab")
    share = vectors.shape[0] // slabs

    def part(distance):
        at = lax.rem(mine + distance, slabs) * share
        return lax.dynamic_slice_in_dim(vectors, at, share, 0)

    start, speeds = [part(0)], [velocity]
    for d in range(1, slabs):
        start.append(from_slab(part(slabs - d), d))
        speeds.append(from_slab(velocity, d))
    here, end = lax.axis_index("seg"), lax.axis_size("seg") - 1
    flags = jnp.stack([here == end, here == 0]).astype(jnp.int32)
    previous = [jnp.concatenate([part[i : i + 1] for part in start], 0) for i in range(share)]
    own, ends = list(previous), list(previous)
    arrived, wrapped, missed, missed_end = [[None] * share for _ in range(4)]
    for hop in range(HOPS):
        for i in range(share):
            if hop == 0:
                sent_end, missed_end[i] = propagate(flags, speeds, start, i, last=True)
                sent, missed[i] = propagate(flags, speeds, start, i)
            else:
                state = (ends[i], missed_end[i], arrived[i])
                ends[i], sent_end, missed_end[i] = propagate(flags, speeds, state, last=True)
                state = (own[i], missed[i], arrived[i], wrapped[i])
                own[i], sent, missed[i] = propagate(flags, speeds, state)
            wrapped[i] = sent_short(sent_end, [end])
            arrived[i] = sent_short(sent)
    parts = [last_residual(flags, arrived[i], wrapped[i], own[i], ends[i]) for i in range(share)]
    residual = []
    for d in range(slabs):
        for i in range(share):
            part_i = parts[i][(slabs - d) % slabs]
            residual.append(from_slab(part_i, d) if d else part_i)
    return jnp.full((1,), mine * share, jnp.int32), residual


def split_rows(vectors, velocity):
    depth, height = velocity.shape[0], vectors.shape[2]

    def pieces(value):
        after = value[..., :depth, :]
        before = value[..., height - depth :, :]
        return [value, from_slab(after, 1), from_slab(before, -1)]

    speeds = pieces(velocity)
    begun = vectors
    for hop in range(HOPS):
        state = pieces(begun)
        arrived = [to_next(propagate_rows(speeds, state, i)) for i in range(vectors.shape[0])]
        begun = jnp.concatenate(arrived, 0) - begun
    return jnp.zeros((1,), jnp.int32), [begun[i : i + 1] for i in range(vectors.shape[0])]


def shards(block, base_velocity):
    vectors, velocity = tiled(block[0]), tiled(base_velocity[0])
    even = vectors.shape[0] % lax.axis_size("slab") == 0
    shift, residual = (split_vectors if even else split_rows)(vectors, velocity)
    axes = ("seg", "slab")
    gram = local_gram(shift, residual, lax.axis_size("seg") * lax.axis_size("slab"))
    gram = lax.all_to_all(gram, axes, 0, 0, tiled=True)
    return untiled(solved(shift, gram, residual))[None]


def solution(mesh):
    placed = (P("seg", None, "slab", None), P("seg", None, None, "slab", None))
    return jax.shard_map(
        shards, mesh=mesh, in_specs=placed, out_specs=P("seg", None, "slab", None), check_vma=False
    )
```

time: 65.3 us -> 85.6 us (1.31)
  Pallas kernels: 14.1 us -> 27.4 us
  starting transfers between devices: 5.64 us -> 15.3 us
  waiting for transfers between devices: 34.9 us -> 31.4 us
    pallas_call x8 -> x16, Pallas kernels: 12.9 us -> 24.9 us  [propagate(): pl.pallas_call(functools.partial(propagate_kernel, pieces, index, first,...]
    ppermute x10 -> x16, starting transfers between devices: 4.91 us -> 14.5 us  [to_next(): lax.ppermute(value, 'seg', [(i, (i + 1) % size) for i in segments or rang...]
    ppermute x10 -> x16, waiting for transfers between devices: 33.3 us -> 28.5 us  [to_next(): lax.ppermute(value, 'seg', [(i, (i + 1) % size) for i in segments or rang...]
    ppermute x4, waiting for transfers between devices: 1.62 us -> 2.87 us  [from_slab(): lax.ppermute(value, 'slab', [((i + distance) % size, i) for i in range(si...]
    pallas_call x2 -> x4, Pallas kernels: 1.26 us -> 2.45 us  [the longest x2 1.18 us: last_residual(): pl.pallas_call(residual_kernel, out_shape=[jax.ShapeDtypeStruct((1, colum...]
  transfers between devices with their start and end apart: 14 -> 20, of which waited for: 8 -> 13; matrix products, arithmetic and copies ran while one was open for 2% -> 2% of each run, Pallas kernels for 17% -> 30%
where the time goes in v4:
time: 85.6 us; the launch traced here: 85.3 us
  waiting for transfers between devices  31.4 us (37%)
  Pallas kernels  27.4 us (32%)
  starting transfers between devices  15.3 us (18%)
  blocking collectives  8.86 us (10%)
  local copies, waits for them, and re-layouts  1.1 us (1%)
    ppermute x16, waiting for transfers between devices, to_next(): lax.ppermute(value, 'seg', [(i, (i + 1) % size) for i in segments or rang...  28.5 us
    pallas_call x16, Pallas kernels, propagate(): pl.pallas_call(functools.partial(propagate_kernel, pieces, index, first,...  24.9 us
    ppermute x16, starting transfers between devices, to_next(): lax.ppermute(value, 'seg', [(i, (i + 1) % size) for i in segments or rang...  14.5 us
    all_to_all x1, blocking collectives, shards(): gram = lax.all_to_all(gram, axes, 0, 0, tiled=True)  8.86 us
    ppermute x4, waiting for transfers between devices, from_slab(): lax.ppermute(value, 'slab', [((i + distance) % size, i) for i in range(si...  2.87 us
  transfers between devices with their start and end apart: 20, of which 13 were waited for; matrix products, arithmetic and copies ran while one was open for 2% of the time, Pallas kernels for 30%

profile of v4, /device:TPU:0, one launch (start us, length us, event | category | flops | bytes accessed | tf_op | source)
XLA Modules:
  0.0 85.3 jit_solution(7664933077290427515)
XLA Ops:
  1.8 1.5 %collective-permute-done.1.refs_4_ = f32[2,32,8,128]{3,2,1,0:T(8,128)S(1)} collective-permute-done((f32[2,32,8,128]{3,2,1,0:T(8,128)S(1)}, f32[2,32,8,128]{3,2,1,0:T(8,128)S(1)}, u32[]{:S(2)}, u32[]{:S(2)}) %collective-permute-start.1) | collective-permute-done | bytes 262176 | tf_op jit(solution)/shard_map/ppermute | solution.py:305
  5.3 2.2 %propagate.12 = (f32[65,8,128]{2,1,0:T(8,128)S(1)}, f32[64,8,128]{2,1,0:T(8,128)S(1)}) custom-call(s32[2]{0:T(128)S(1)} %add_convert_fusion.refs_0_.flags, bf16[8,2,32,8,128]{4,3,2,1,0:T(8,128)(2,1)S(1)} %bitcast.20, bf16[8,2,32,8,128]{4,3,2,1,0:T(8,128)(2,1)S(1)} %collective-permute-done.refs_2_, f32[2,32,8,128]{3,2,1,0:T(8,128)S(1)} %get-tuple-element.93.refs_3_, ...), custom_call_target="tpu_custom_call" | custom-call | tf_op jit(solution)/shard_map/jit(propagate)/propagate/pallas_call | solution.py:155
  7.5 2.3 %collective-permute-start.10 = (f16[65,8,128]{2,1,0:T(8,128)(2,1)S(1)}, f16[65,8,128]{2,1,0:T(8,128)(2,1)S(1)}, u32[]{:S(2)}, u32[]{:S(2)}) collective-permute-start(f16[65,8,128]{2,1,0:T(8,128)(2,1)S(1)} %convert_element_type.116), channel_id=1, source_target_pairs={{0,2},{2,4},{4,6},{6,8},{8,10},{10,12},{12,14},{14,16},{16,18},{18... | collective-permute-start | bytes 399368 | tf_op jit(solution)/shard_map/ppermute | solution.py:310
  10.4 2.2 %propagate.8 = (f32[65,8,128]{2,1,0:T(8,128)S(1)}, f32[64,8,128]{2,1,0:T(8,128)S(1)}) custom-call(s32[2]{0:T(128)S(1)} %add_convert_fusion.refs_0_.flags, bf16[8,2,32,8,128]{4,3,2,1,0:T(8,128)(2,1)S(1)} %bitcast.22, bf16[8,2,32,8,128]{4,3,2,1,0:T(8,128)(2,1)S(1)} %collective-permute-done.refs_2_, f32[2,32,8,128]{3,2,1,0:T(8,128)S(1)} %get-tuple-element.93.refs_3_, ...), custom_call_target="tpu_custom_call" | custom-call | tf_op jit(solution)/shard_map/jit(propagate)/propagate/pallas_call | solution.py:155
  12.6 1.5 %collective-permute-start.2 = (f16[65,8,128]{2,1,0:T(8,128)(2,1)S(1)}, f16[65,8,128]{2,1,0:T(8,128)(2,1)S(1)}, u32[]{:S(2)}, u32[]{:S(2)}) collective-permute-start(f16[65,8,128]{2,1,0:T(8,128)(2,1)S(1)} %convert_element_type.100), channel_id=1, source_target_pairs={{0,2},{2,4},{4,6},{6,8},{8,10},{10,12},{12,14},{14,16},{16,18},{18... | collective-permute-start | bytes 399368 | tf_op jit(solution)/shard_map/ppermute | solution.py:310
  15.4 5.5 %collective-permute-done.10 = f16[65,8,128]{2,1,0:T(8,128)(2,1)S(1)} collective-permute-done((f16[65,8,128]{2,1,0:T(8,128)(2,1)S(1)}, f16[65,8,128]{2,1,0:T(8,128)(2,1)S(1)}, u32[]{:S(2)}, u32[]{:S(2)}) %collective-permute-start.10) | collective-permute-done | bytes 133152 | tf_op jit(solution)/shard_map/ppermute | solution.py:310
  21.6 2.2 %propagate.13 = (f32[2,32,8,128]{3,2,1,0:T(8,128)S(1)}, f32[65,8,128]{2,1,0:T(8,128)S(1)}, f32[64,8,128]{2,1,0:T(8,128)S(1)}) custom-call(s32[2]{0:T(128)S(1)} %add_convert_fusion.refs_0_.flags, bf16[8,2,32,8,128]{4,3,2,1,0:T(8,128)(2,1)S(1)} %bitcast.24, bf16[8,2,32,8,128]{4,3,2,1,0:T(8,128)(2,1)S(1)} %collective-permute-done.refs_2_, ...), custom_call_target="tpu_custom_call" | custom-call | tf_op jit(solution)/shard_map/jit(propagate)/propagate/pallas_call | solution.py:155
  26.1 2.2 %propagate.9 = (f32[2,32,8,128]{3,2,1,0:T(8,128)S(1)}, f32[65,8,128]{2,1,0:T(8,128)S(1)}, f32[64,8,128]{2,1,0:T(8,128)S(1)}) custom-call(s32[2]{0:T(128)S(1)} %add_convert_fusion.refs_0_.flags, bf16[8,2,32,8,128]{4,3,2,1,0:T(8,128)(2,1)S(1)} %bitcast.25, bf16[8,2,32,8,128]{4,3,2,1,0:T(8,128)(2,1)S(1)} %collective-permute-done.refs_2_, ...), custom_call_target="tpu_custom_call" | custom-call | tf_op jit(solution)/shard_map/jit(propagate)/propagate/pallas_call | solution.py:155
  30.3 3.5 %collective-permute-done.12 = f16[65,8,128]{2,1,0:T(8,128)(2,1)S(1)} collective-permute-done((f16[65,8,128]{2,1,0:T(8,128)(2,1)S(1)}, f16[65,8,128]{2,1,0:T(8,128)(2,1)S(1)}, u32[]{:S(2)}, u32[]{:S(2)}) %collective-permute-start.12) | collective-permute-done | bytes 133152 | tf_op jit(solution)/shard_map/ppermute | solution.py:310
  33.9 2.5 %collective-permute-done.13 = f16[65,8,128]{2,1,0:T(8,128)(2,1)S(1)} collective-permute-done((f16[65,8,128]{2,1,0:T(8,128)(2,1)S(1)}, f16[65,8,128]{2,1,0:T(8,128)(2,1)S(1)}, u32[]{:S(2)}, u32[]{:S(2)}) %collective-permute-start.13) | collective-permute-done | bytes 133152 | tf_op jit(solution)/shard_map/ppermute | solution.py:310
  36.4 2.2 %propagate.14 = (f32[2,32,8,128]{3,2,1,0:T(8,128)S(1)}, f32[65,8,128]{2,1,0:T(8,128)S(1)}, f32[64,8,128]{2,1,0:T(8,128)S(1)}) custom-call(s32[2]{0:T(128)S(1)} %add_convert_fusion.refs_0_.flags, bf16[8,2,32,8,128]{4,3,2,1,0:T(8,128)(2,1)S(1)} %bitcast.27, bf16[8,2,32,8,128]{4,3,2,1,0:T(8,128)(2,1)S(1)} %collective-permute-done.refs_2_, ...), custom_call_target="tpu_custom_call" | custom-call | tf_op jit(solution)/shard_map/jit(propagate)/propagate/pallas_call | solution.py:155
  39.3 1.3 %collective-permute-start.15 = (f16[65,8,128]{2,1,0:T(8,128)(2,1)S(1)}, f16[65,8,128]{2,1,0:T(8,128)(2,1)S(1)}, u32[]{:S(2)}, u32[]{:S(2)}) collective-permute-start(f16[65,8,128]{2,1,0:T(8,128)(2,1)S(1)} %convert_element_type.126), channel_id=1, source_target_pairs={{30,0},{31,1}} | collective-permute-start | bytes 399368 | tf_op jit(solution)/shard_map/ppermute | solution.py:310
  41.0 2.2 %propagate.10 = (f32[2,32,8,128]{3,2,1,0:T(8,128)S(1)}, f32[65,8,128]{2,1,0:T(8,128)S(1)}, f32[64,8,128]{2,1,0:T(8,128)S(1)}) custom-call(s32[2]{0:T(128)S(1)} %add_convert_fusion.refs_0_.flags, bf16[8,2,32,8,128]{4,3,2,1,0:T(8,128)(2,1)S(1)} %bitcast.29, bf16[8,2,32,8,128]{4,3,2,1,0:T(8,128)(2,1)S(1)} %collective-permute-done.refs_2_, ...), custom_call_target="tpu_custom_call" | custom-call | tf_op jit(solution)/shard_map/jit(propagate)/propagate/pallas_call | solution.py:155
  45.2 3.4 %collective-permute-done.14 = f16[65,8,128]{2,1,0:T(8,128)(2,1)S(1)} collective-permute-done((f16[65,8,128]{2,1,0:T(8,128)(2,1)S(1)}, f16[65,8,128]{2,1,0:T(8,128)(2,1)S(1)}, u32[]{:S(2)}, u32[]{:S(2)}) %collective-permute-start.14) | collective-permute-done | bytes 133152 | tf_op jit(solution)/shard_map/ppermute | solution.py:310
  48.7 2.9 %collective-permute-done.15 = f16[65,8,128]{2,1,0:T(8,128)(2,1)S(1)} collective-permute-done((f16[65,8,128]{2,1,0:T(8,128)(2,1)S(1)}, f16[65,8,128]{2,1,0:T(8,128)(2,1)S(1)}, u32[]{:S(2)}, u32[]{:S(2)}) %collective-permute-start.15) | collective-permute-done | bytes 133152 | tf_op jit(solution)/shard_map/ppermute | solution.py:310
  51.6 2.9 %propagate.15 = (f32[2,32,8,128]{3,2,1,0:T(8,128)S(1)}, f32[65,8,128]{2,1,0:T(8,128)S(1)}, f32[64,8,128]{2,1,0:T(8,128)}) custom-call(s32[2]{0:T(128)S(1)} %add_convert_fusion.refs_0_.flags, bf16[8,2,32,8,128]{4,3,2,1,0:T(8,128)(2,1)S(1)} %bitcast.31, bf16[8,2,32,8,128]{4,3,2,1,0:T(8,128)(2,1)S(1)} %collective-permute-done.refs_2_, ...), custom_call_target="tpu_custom_call" | custom-call | tf_op jit(solution)/shard_map/jit(propagate)/propagate/pallas_call | solution.py:155
  55.9 1.3 %collective-permute-start.17 = (f16[65,8,128]{2,1,0:T(8,128)(2,1)S(1)}, f16[65,8,128]{2,1,0:T(8,128)(2,1)S(1)}, u32[]{:S(2)}, u32[]{:S(2)}) collective-permute-start(f16[65,8,128]{2,1,0:T(8,128)(2,1)S(1)} %convert_element_type.130), channel_id=1, source_target_pairs={{30,0},{31,1}} | collective-permute-start | bytes 399368 | tf_op jit(solution)/shard_map/ppermute | solution.py:310
  57.3 2.9 %propagate.11 = (f32[2,32,8,128]{3,2,1,0:T(8,128)S(1)}, f32[65,8,128]{2,1,0:T(8,128)S(1)}, f32[64,8,128]{2,1,0:T(8,128)}) custom-call(s32[2]{0:T(128)S(1)} %add_convert_fusion.refs_0_.flags, bf16[8,2,32,8,128]{4,3,2,1,0:T(8,128)(2,1)S(1)} %bitcast.33, bf16[8,2,32,8,128]{4,3,2,1,0:T(8,128)(2,1)S(1)} %collective-permute-done.refs_2_, ...), custom_call_target="tpu_custom_call" | custom-call | tf_op jit(solution)/shard_map/jit(propagate)/propagate/pallas_call | solution.py:155
  62.9 4.2 %collective-permute-done.17 = f16[65,8,128]{2,1,0:T(8,128)(2,1)S(1)} collective-permute-done((f16[65,8,128]{2,1,0:T(8,128)(2,1)S(1)}, f16[65,8,128]{2,1,0:T(8,128)(2,1)S(1)}, u32[]{:S(2)}, u32[]{:S(2)}) %collective-permute-start.17) | collective-permute-done | bytes 133152 | tf_op jit(solution)/shard_map/ppermute | solution.py:310
  67.1 1.4 %collective-permute-done.16 = f16[65,8,128]{2,1,0:T(8,128)(2,1)S(1)} collective-permute-done((f16[65,8,128]{2,1,0:T(8,128)(2,1)S(1)}, f16[65,8,128]{2,1,0:T(8,128)(2,1)S(1)}, u32[]{:S(2)}, u32[]{:S(2)}) %collective-permute-start.16) | collective-permute-done | bytes 133152 | tf_op jit(solution)/shard_map/ppermute | solution.py:310
  69.2 2.1 %collective-permute-done.8 = f16[65,8,128]{2,1,0:T(8,128)(2,1)S(1)} collective-permute-done((f16[65,8,128]{2,1,0:T(8,128)(2,1)S(1)}, f16[65,8,128]{2,1,0:T(8,128)(2,1)S(1)}, u32[]{:S(2)}, u32[]{:S(2)}) %collective-permute-start.8) | collective-permute-done | bytes 133152 | tf_op jit(solution)/shard_map/ppermute | solution.py:310
  71.4 1.8 %collective-permute-done.9 = f16[65,8,128]{2,1,0:T(8,128)(2,1)S(1)} collective-permute-done((f16[65,8,128]{2,1,0:T(8,128)(2,1)S(1)}, f16[65,8,128]{2,1,0:T(8,128)(2,1)S(1)}, u32[]{:S(2)}, u32[]{:S(2)}) %collective-permute-start.9) | collective-permute-done | bytes 133152 | tf_op jit(solution)/shard_map/ppermute | solution.py:310
  73.8 1.3 %collective-permute-done.18.refs_2_ = f32[1,32,8,128]{3,2,1,0:T(8,128)S(1)} collective-permute-done((f32[1,32,8,128]{3,2,1,0:T(8,128)S(1)}, f32[1,32,8,128]{3,2,1,0:T(8,128)S(1)}, u32[]{:S(2)}, u32[]{:S(2)}) %collective-permute-start.18) | collective-permute-done | bytes 131104 | tf_op jit(solution)/shard_map/ppermute | solution.py:305
  75.4 8.9 %all_to_all.11 = f32[32,1,128]{2,1,0:T(1,128)S(1)} all-to-all(f32[32,1,128]{2,1,0:T(1,128)S(1)} %bitcast.36), channel_id=1, replica_groups=mesh['seg'=16,'slab'=2] {'seg','slab'}, dimensions={0} | all-to-all | bytes 32768 | tf_op jit(solution)/shard_map/all_to_all | solution.py:378
  (77 shorter events, 20.2 us)
Async XLA Ops:
  0.0 3.4 %copy-start = (bf16[1,8,2,8,4096]{4,3,2,1,0:T(8,128)(2,1)S(1)}, bf16[1,8,2,8,4096]{4,3,2,1,0:T(8,128)(2,1)}, u32[]{:S(2)}) copy-start(bf16[1,8,2,8,4096]{4,3,2,1,0:T(8,128)(2,1)} %param.3) | copy-start | bytes 3145732
  0.0 3.4 %collective-permute-start = (bf16[8,2,32,8,128]{4,3,2,1,0:T(8,128)(2,1)}, bf16[8,2,32,8,128]{4,3,2,1,0:T(8,128)(2,1)S(1)}, u32[]{:S(2)}, u32[]{:S(2)}) collective-permute-start(bf16[8,2,32,8,128]{4,3,2,1,0:T(8,128)(2,1)} %bitcast.18), channel_id=1, source_target_pairs={{1,0},{0,1},{3,2},{2,3},{5,4},{4,5},{7,6},{6,7},{9,8},{8,9},{11,10... | collective-permute-start | bytes 3145736 | tf_op jit(solution)/shard_map/ppermute | solution.py:305
  1.6 1.8 %collective-permute-start.1 = (f32[2,32,8,128]{3,2,1,0:T(8,128)S(1)}, f32[2,32,8,128]{3,2,1,0:T(8,128)S(1)}, u32[]{:S(2)}, u32[]{:S(2)}) collective-permute-start(f32[2,32,8,128]{3,2,1,0:T(8,128)S(1)} %get-tuple-element.94), channel_id=1, source_target_pairs={{1,0},{0,1},{3,2},{2,3},{5,4},{4,5},{7,6},{6,7},{9,8},{8,9},{11,10... | collective-permute-start | bytes 786440 | tf_op jit(solution)/shard_map/ppermute | solution.py:305
  4.0 17.6 %collective-permute-start.11 = (f16[65,8,128]{2,1,0:T(8,128)(2,1)S(1)}, f16[65,8,128]{2,1,0:T(8,128)(2,1)S(1)}, u32[]{:S(2)}, u32[]{:S(2)}) collective-permute-start(f16[65,8,128]{2,1,0:T(8,128)(2,1)S(1)} %convert_element_type.118), channel_id=1, source_target_pairs={{30,0},{31,1}} | collective-permute-start | bytes 399368 | tf_op jit(solution)/shard_map/ppermute | solution.py:310
  7.5 13.5 %collective-permute-start.10 = (f16[65,8,128]{2,1,0:T(8,128)(2,1)S(1)}, f16[65,8,128]{2,1,0:T(8,128)(2,1)S(1)}, u32[]{:S(2)}, u32[]{:S(2)}) collective-permute-start(f16[65,8,128]{2,1,0:T(8,128)(2,1)S(1)} %convert_element_type.116), channel_id=1, source_target_pairs={{0,2},{2,4},{4,6},{6,8},{8,10},{10,12},{12,14},{14,16},{16,18},{18... | collective-permute-start | bytes 399368 | tf_op jit(solution)/shard_map/ppermute | solution.py:310
  12.6 12.7 %collective-permute-start.2 = (f16[65,8,128]{2,1,0:T(8,128)(2,1)S(1)}, f16[65,8,128]{2,1,0:T(8,128)(2,1)S(1)}, u32[]{:S(2)}, u32[]{:S(2)}) collective-permute-start(f16[65,8,128]{2,1,0:T(8,128)(2,1)S(1)} %convert_element_type.100), channel_id=1, source_target_pairs={{0,2},{2,4},{4,6},{6,8},{8,10},{10,12},{12,14},{14,16},{16,18},{18... | collective-permute-start | bytes 399368 | tf_op jit(solution)/shard_map/ppermute | solution.py:310
  14.1 12.0 %collective-permute-start.3 = (f16[65,8,128]{2,1,0:T(8,128)(2,1)S(1)}, f16[65,8,128]{2,1,0:T(8,128)(2,1)S(1)}, u32[]{:S(2)}, u32[]{:S(2)}) collective-permute-start(f16[65,8,128]{2,1,0:T(8,128)(2,1)S(1)} %convert_element_type.102), channel_id=1, source_target_pairs={{30,0},{31,1}} | collective-permute-start | bytes 399368 | tf_op jit(solution)/shard_map/ppermute | solution.py:310
  23.9 10.0 %collective-permute-start.12 = (f16[65,8,128]{2,1,0:T(8,128)(2,1)S(1)}, f16[65,8,128]{2,1,0:T(8,128)(2,1)S(1)}, u32[]{:S(2)}, u32[]{:S(2)}) collective-permute-start(f16[65,8,128]{2,1,0:T(8,128)(2,1)S(1)} %convert_element_type.120), channel_id=1, source_target_pairs={{0,2},{2,4},{4,6},{6,8},{8,10},{10,12},{12,14},{14,16},{16,18},{18... | collective-permute-start | bytes 399368 | tf_op jit(solution)/shard_map/ppermute | solution.py:310
  23.9 12.5 %collective-permute-start.13 = (f16[65,8,128]{2,1,0:T(8,128)(2,1)S(1)}, f16[65,8,128]{2,1,0:T(8,128)(2,1)S(1)}, u32[]{:S(2)}, u32[]{:S(2)}) collective-permute-start(f16[65,8,128]{2,1,0:T(8,128)(2,1)S(1)} %convert_element_type.122), channel_id=1, source_target_pairs={{30,0},{31,1}} | collective-permute-start | bytes 399368 | tf_op jit(solution)/shard_map/ppermute | solution.py:310
  28.4 12.3 %collective-permute-start.4 = (f16[65,8,128]{2,1,0:T(8,128)(2,1)S(1)}, f16[65,8,128]{2,1,0:T(8,128)(2,1)S(1)}, u32[]{:S(2)}, u32[]{:S(2)}) collective-permute-start(f16[65,8,128]{2,1,0:T(8,128)(2,1)S(1)} %convert_element_type.104), channel_id=1, source_target_pairs={{0,2},{2,4},{4,6},{6,8},{8,10},{10,12},{12,14},{14,16},{16,18},{18... | collective-permute-start | bytes 399368 | tf_op jit(solution)/shard_map/ppermute | solution.py:310
  29.0 12.0 %collective-permute-start.5 = (f16[65,8,128]{2,1,0:T(8,128)(2,1)S(1)}, f16[65,8,128]{2,1,0:T(8,128)(2,1)S(1)}, u32[]{:S(2)}, u32[]{:S(2)}) collective-permute-start(f16[65,8,128]{2,1,0:T(8,128)(2,1)S(1)} %convert_element_type.106), channel_id=1, source_target_pairs={{30,0},{31,1}} | collective-permute-start | bytes 399368 | tf_op jit(solution)/shard_map/ppermute | solution.py:310
  38.7 10.0 %collective-permute-start.14 = (f16[65,8,128]{2,1,0:T(8,128)(2,1)S(1)}, f16[65,8,128]{2,1,0:T(8,128)(2,1)S(1)}, u32[]{:S(2)}, u32[]{:S(2)}) collective-permute-start(f16[65,8,128]{2,1,0:T(8,128)(2,1)S(1)} %convert_element_type.124), channel_id=1, source_target_pairs={{0,2},{2,4},{4,6},{6,8},{8,10},{10,12},{12,14},{14,16},{16,18},{18... | collective-permute-start | bytes 399368 | tf_op jit(solution)/shard_map/ppermute | solution.py:310
  39.3 12.3 %collective-permute-start.15 = (f16[65,8,128]{2,1,0:T(8,128)(2,1)S(1)}, f16[65,8,128]{2,1,0:T(8,128)(2,1)S(1)}, u32[]{:S(2)}, u32[]{:S(2)}) collective-permute-start(f16[65,8,128]{2,1,0:T(8,128)(2,1)S(1)} %convert_element_type.126), channel_id=1, source_target_pairs={{30,0},{31,1}} | collective-permute-start | bytes 399368 | tf_op jit(solution)/shard_map/ppermute | solution.py:310
  43.3 14.0 %collective-permute-start.6 = (f16[65,8,128]{2,1,0:T(8,128)(2,1)S(1)}, f16[65,8,128]{2,1,0:T(8,128)(2,1)S(1)}, u32[]{:S(2)}, u32[]{:S(2)}) collective-permute-start(f16[65,8,128]{2,1,0:T(8,128)(2,1)S(1)} %convert_element_type.108), channel_id=1, source_target_pairs={{0,2},{2,4},{4,6},{6,8},{8,10},{10,12},{12,14},{14,16},{16,18},{18... | collective-permute-start | bytes 399368 | tf_op jit(solution)/shard_map/ppermute | solution.py:310
  43.9 13.3 %collective-permute-start.7 = (f16[65,8,128]{2,1,0:T(8,128)(2,1)S(1)}, f16[65,8,128]{2,1,0:T(8,128)(2,1)S(1)}, u32[]{:S(2)}, u32[]{:S(2)}) collective-permute-start(f16[65,8,128]{2,1,0:T(8,128)(2,1)S(1)} %convert_element_type.110), channel_id=1, source_target_pairs={{30,0},{31,1}} | collective-permute-start | bytes 399368 | tf_op jit(solution)/shard_map/ppermute | solution.py:310
  55.9 11.2 %collective-permute-start.17 = (f16[65,8,128]{2,1,0:T(8,128)(2,1)S(1)}, f16[65,8,128]{2,1,0:T(8,128)(2,1)S(1)}, u32[]{:S(2)}, u32[]{:S(2)}) collective-permute-start(f16[65,8,128]{2,1,0:T(8,128)(2,1)S(1)} %convert_element_type.130), channel_id=1, source_target_pairs={{30,0},{31,1}} | collective-permute-start | bytes 399368 | tf_op jit(solution)/shard_map/ppermute | solution.py:310
  57.2 11.4 %collective-permute-start.16 = (f16[65,8,128]{2,1,0:T(8,128)(2,1)S(1)}, f16[65,8,128]{2,1,0:T(8,128)(2,1)S(1)}, u32[]{:S(2)}, u32[]{:S(2)}) collective-permute-start(f16[65,8,128]{2,1,0:T(8,128)(2,1)S(1)} %convert_element_type.128), channel_id=1, source_target_pairs={{0,2},{2,4},{4,6},{6,8},{8,10},{10,12},{12,14},{14,16},{16,18},{18... | collective-permute-start | bytes 399368 | tf_op jit(solution)/shard_map/ppermute | solution.py:310
  60.3 11.1 %collective-permute-start.8 = (f16[65,8,128]{2,1,0:T(8,128)(2,1)S(1)}, f16[65,8,128]{2,1,0:T(8,128)(2,1)S(1)}, u32[]{:S(2)}, u32[]{:S(2)}) collective-permute-start(f16[65,8,128]{2,1,0:T(8,128)(2,1)S(1)} %convert_element_type.112), channel_id=1, source_target_pairs={{0,2},{2,4},{4,6},{6,8},{8,10},{10,12},{12,14},{14,16},{16,18},{18... | collective-permute-start | bytes 399368 | tf_op jit(solution)/shard_map/ppermute | solution.py:310
  61.6 11.5 %collective-permute-start.9 = (f16[65,8,128]{2,1,0:T(8,128)(2,1)S(1)}, f16[65,8,128]{2,1,0:T(8,128)(2,1)S(1)}, u32[]{:S(2)}, u32[]{:S(2)}) collective-permute-start(f16[65,8,128]{2,1,0:T(8,128)(2,1)S(1)} %convert_element_type.114), channel_id=1, source_target_pairs={{30,0},{31,1}} | collective-permute-start | bytes 399368 | tf_op jit(solution)/shard_map/ppermute | solution.py:310
  69.1 4.7 %collective-permute-start.19 = (f32[1,32,8,128]{3,2,1,0:T(8,128)S(1)}, f32[1,32,8,128]{3,2,1,0:T(8,128)S(1)}, u32[]{:S(2)}, u32[]{:S(2)}) collective-permute-start(f32[1,32,8,128]{3,2,1,0:T(8,128)S(1)} %get-tuple-element.92), channel_id=1, source_target_pairs={{1,0},{0,1},{3,2},{2,3},{5,4},{4,5},{7,6},{6,7},{9,8},{8,9},{11,10... | collective-permute-start | bytes 393224 | tf_op jit(solution)/shard_map/ppermute | solution.py:305
  73.8 1.4 %collective-permute-start.18 = (f32[1,32,8,128]{3,2,1,0:T(8,128)S(1)}, f32[1,32,8,128]{3,2,1,0:T(8,128)S(1)}, u32[]{:S(2)}, u32[]{:S(2)}) collective-permute-start(f32[1,32,8,128]{3,2,1,0:T(8,128)S(1)} %get-tuple-element.91), channel_id=1, source_target_pairs={{1,0},{0,1},{3,2},{2,3},{5,4},{4,5},{7,6},{6,7},{9,8},{8,9},{11,10... | collective-permute-start | bytes 393224 | tf_op jit(solution)/shard_map/ppermute | solution.py:305

commit v5 on v4

--- a/solution.py
+++ b/solution.py
@@ -6,6 +6,7 @@
 from jax.experimental import pallas as pl
 from jax.experimental.pallas import tpu as pltpu
 from jax.sharding import PartitionSpec as P
+
 
 HOPS = 4
 SUB = 8
@@ -334,13 +335,14 @@
     for hop in range(HOPS):
         for i in range(share):
             if hop == 0:
-                sent_end, missed_end[i] = propagate(flags, speeds, start, i, last=True)
-                sent, missed[i] = propagate(flags, speeds, start, i)
+                state_end, state = start, start
             else:
-                state = (ends[i], missed_end[i], arrived[i])
-                ends[i], sent_end, missed_end[i] = propagate(flags, speeds, state, last=True)
+                state_end = (ends[i], missed_end[i], arrived[i])
                 state = (own[i], missed[i], arrived[i], wrapped[i])
-                own[i], sent, missed[i] = propagate(flags, speeds, state)
+            *began_end, sent_end, missed_end[i] = propagate(flags, speeds, state_end, i if hop == 0 else 0, last=True)
+            *began, sent, missed[i] = propagate(flags, speeds, state, i if hop == 0 else 0)
+            if hop:
+                ends[i], own[i] = began_end[0], began[0]
             wrapped[i] = sent_short(sent_end, [end])
             arrived[i] = sent_short(sent)
     parts = [last_residual(flags, arrived[i], wrapped[i], own[i], ends[i]) for i in range(share)]
@@ -362,7 +364,7 @@
 
     speeds = pieces(velocity)
     begun = vectors
-    for hop in range(HOPS):
+    for _ in range(HOPS):
         state = pieces(begun)
         arrived = [to_next(propagate_rows(speeds, state, i)) for i in range(vectors.shape[0])]
         begun = jnp.concatenate(arrived, 0) - begun

time: 85.6 us -> 85.6 us (level)
  no operation moved by 1% of the time
where the time goes in v5:
time: 85.6 us; the launch traced here: 85.3 us
  waiting for transfers between devices  31.4 us (37%)
  Pallas kernels  27.4 us (32%)
  starting transfers between devices  15.3 us (18%)
  blocking collectives  8.86 us (10%)
  local copies, waits for them, and re-layouts  1.1 us (1%)
    ppermute x16, waiting for transfers between devices, to_next(): lax.ppermute(value, 'seg', [(i, (i + 1) % size) for i in segments or rang...  28.5 us
    pallas_call x16, Pallas kernels, propagate(): pl.pallas_call(functools.partial(propagate_kernel, pieces, index, first,...  24.9 us
    ppermute x16, starting transfers between devices, to_next(): lax.ppermute(value, 'seg', [(i, (i + 1) % size) for i in segments or rang...  14.5 us
    all_to_all x1, blocking collectives, shards(): gram = lax.all_to_all(gram, axes, 0, 0, tiled=True)  8.86 us
    ppermute x4, waiting for transfers between devices, from_slab(): lax.ppermute(value, 'slab', [((i + distance) % size, i) for i in range(si...  2.87 us
  transfers between devices with their start and end apart: 20, of which 13 were waited for; matrix products, arithmetic and copies ran while one was open for 2% of the time, Pallas kernels for 30%

profile of v5, /device:TPU:0, one launch (start us, length us, event | category | flops | bytes accessed | tf_op | source)
XLA Modules:
  0.0 85.3 jit_solution(7664933077290427515)
XLA Ops:
  1.8 1.5 %collective-permute-done.1.refs_4_ = f32[2,32,8,128]{3,2,1,0:T(8,128)S(1)} collective-permute-done((f32[2,32,8,128]{3,2,1,0:T(8,128)S(1)}, f32[2,32,8,128]{3,2,1,0:T(8,128)S(1)}, u32[]{:S(2)}, u32[]{:S(2)}) %collective-permute-start.1) | collective-permute-done | bytes 262176 | tf_op jit(solution)/shard_map/ppermute | solution.py:306
  4.0 1.3 %collective-permute-start.11 = (f16[65,8,128]{2,1,0:T(8,128)(2,1)S(1)}, f16[65,8,128]{2,1,0:T(8,128)(2,1)S(1)}, u32[]{:S(2)}, u32[]{:S(2)}) collective-permute-start(f16[65,8,128]{2,1,0:T(8,128)(2,1)S(1)} %convert_element_type.118), channel_id=1, source_target_pairs={{30,0},{31,1}} | collective-permute-start | bytes 399368 | tf_op jit(solution)/shard_map/ppermute | solution.py:311
  5.3 2.2 %propagate.12 = (f32[65,8,128]{2,1,0:T(8,128)S(1)}, f32[64,8,128]{2,1,0:T(8,128)S(1)}) custom-call(s32[2]{0:T(128)S(1)} %add_convert_fusion.refs_0_.flags, bf16[8,2,32,8,128]{4,3,2,1,0:T(8,128)(2,1)S(1)} %bitcast.20, bf16[8,2,32,8,128]{4,3,2,1,0:T(8,128)(2,1)S(1)} %collective-permute-done.refs_2_, f32[2,32,8,128]{3,2,1,0:T(8,128)S(1)} %get-tuple-element.93.refs_3_, ...), custom_call_target="tpu_custom_call" | custom-call | tf_op jit(solution)/shard_map/jit(propagate)/propagate/pallas_call | solution.py:156
  7.5 2.3 %collective-permute-start.10 = (f16[65,8,128]{2,1,0:T(8,128)(2,1)S(1)}, f16[65,8,128]{2,1,0:T(8,128)(2,1)S(1)}, u32[]{:S(2)}, u32[]{:S(2)}) collective-permute-start(f16[65,8,128]{2,1,0:T(8,128)(2,1)S(1)} %convert_element_type.116), channel_id=1, source_target_pairs={{0,2},{2,4},{4,6},{6,8},{8,10},{10,12},{12,14},{14,16},{16,18},{18... | collective-permute-start | bytes 399368 | tf_op jit(solution)/shard_map/ppermute | solution.py:311
  10.4 2.2 %propagate.8 = (f32[65,8,128]{2,1,0:T(8,128)S(1)}, f32[64,8,128]{2,1,0:T(8,128)S(1)}) custom-call(s32[2]{0:T(128)S(1)} %add_convert_fusion.refs_0_.flags, bf16[8,2,32,8,128]{4,3,2,1,0:T(8,128)(2,1)S(1)} %bitcast.22, bf16[8,2,32,8,128]{4,3,2,1,0:T(8,128)(2,1)S(1)} %collective-permute-done.refs_2_, f32[2,32,8,128]{3,2,1,0:T(8,128)S(1)} %get-tuple-element.93.refs_3_, ...), custom_call_target="tpu_custom_call" | custom-call | tf_op jit(solution)/shard_map/jit(propagate)/propagate/pallas_call | solution.py:156
  12.6 1.5 %collective-permute-start.2 = (f16[65,8,128]{2,1,0:T(8,128)(2,1)S(1)}, f16[65,8,128]{2,1,0:T(8,128)(2,1)S(1)}, u32[]{:S(2)}, u32[]{:S(2)}) collective-permute-start(f16[65,8,128]{2,1,0:T(8,128)(2,1)S(1)} %convert_element_type.100), channel_id=1, source_target_pairs={{0,2},{2,4},{4,6},{6,8},{8,10},{10,12},{12,14},{14,16},{16,18},{18... | collective-permute-start | bytes 399368 | tf_op jit(solution)/shard_map/ppermute | solution.py:311
  15.4 5.5 %collective-permute-done.10 = f16[65,8,128]{2,1,0:T(8,128)(2,1)S(1)} collective-permute-done((f16[65,8,128]{2,1,0:T(8,128)(2,1)S(1)}, f16[65,8,128]{2,1,0:T(8,128)(2,1)S(1)}, u32[]{:S(2)}, u32[]{:S(2)}) %collective-permute-start.10) | collective-permute-done | bytes 133152 | tf_op jit(solution)/shard_map/ppermute | solution.py:311
  21.6 2.2 %propagate.13 = (f32[2,32,8,128]{3,2,1,0:T(8,128)S(1)}, f32[65,8,128]{2,1,0:T(8,128)S(1)}, f32[64,8,128]{2,1,0:T(8,128)S(1)}) custom-call(s32[2]{0:T(128)S(1)} %add_convert_fusion.refs_0_.flags, bf16[8,2,32,8,128]{4,3,2,1,0:T(8,128)(2,1)S(1)} %bitcast.24, bf16[8,2,32,8,128]{4,3,2,1,0:T(8,128)(2,1)S(1)} %collective-permute-done.refs_2_, ...), custom_call_target="tpu_custom_call" | custom-call | tf_op jit(solution)/shard_map/jit(propagate)/propagate/pallas_call | solution.py:156
  26.1 2.2 %propagate.9 = (f32[2,32,8,128]{3,2,1,0:T(8,128)S(1)}, f32[65,8,128]{2,1,0:T(8,128)S(1)}, f32[64,8,128]{2,1,0:T(8,128)S(1)}) custom-call(s32[2]{0:T(128)S(1)} %add_convert_fusion.refs_0_.flags, bf16[8,2,32,8,128]{4,3,2,1,0:T(8,128)(2,1)S(1)} %bitcast.25, bf16[8,2,32,8,128]{4,3,2,1,0:T(8,128)(2,1)S(1)} %collective-permute-done.refs_2_, ...), custom_call_target="tpu_custom_call" | custom-call | tf_op jit(solution)/shard_map/jit(propagate)/propagate/pallas_call | solution.py:156
  30.3 3.5 %collective-permute-done.12 = f16[65,8,128]{2,1,0:T(8,128)(2,1)S(1)} collective-permute-done((f16[65,8,128]{2,1,0:T(8,128)(2,1)S(1)}, f16[65,8,128]{2,1,0:T(8,128)(2,1)S(1)}, u32[]{:S(2)}, u32[]{:S(2)}) %collective-permute-start.12) | collective-permute-done | bytes 133152 | tf_op jit(solution)/shard_map/ppermute | solution.py:311
  33.9 2.5 %collective-permute-done.13 = f16[65,8,128]{2,1,0:T(8,128)(2,1)S(1)} collective-permute-done((f16[65,8,128]{2,1,0:T(8,128)(2,1)S(1)}, f16[65,8,128]{2,1,0:T(8,128)(2,1)S(1)}, u32[]{:S(2)}, u32[]{:S(2)}) %collective-permute-start.13) | collective-permute-done | bytes 133152 | tf_op jit(solution)/shard_map/ppermute | solution.py:311
  36.4 2.2 %propagate.14 = (f32[2,32,8,128]{3,2,1,0:T(8,128)S(1)}, f32[65,8,128]{2,1,0:T(8,128)S(1)}, f32[64,8,128]{2,1,0:T(8,128)S(1)}) custom-call(s32[2]{0:T(128)S(1)} %add_convert_fusion.refs_0_.flags, bf16[8,2,32,8,128]{4,3,2,1,0:T(8,128)(2,1)S(1)} %bitcast.27, bf16[8,2,32,8,128]{4,3,2,1,0:T(8,128)(2,1)S(1)} %collective-permute-done.refs_2_, ...), custom_call_target="tpu_custom_call" | custom-call | tf_op jit(solution)/shard_map/jit(propagate)/propagate/pallas_call | solution.py:156
  39.3 1.3 %collective-permute-start.15 = (f16[65,8,128]{2,1,0:T(8,128)(2,1)S(1)}, f16[65,8,128]{2,1,0:T(8,128)(2,1)S(1)}, u32[]{:S(2)}, u32[]{:S(2)}) collective-permute-start(f16[65,8,128]{2,1,0:T(8,128)(2,1)S(1)} %convert_element_type.126), channel_id=1, source_target_pairs={{30,0},{31,1}} | collective-permute-start | bytes 399368 | tf_op jit(solution)/shard_map/ppermute | solution.py:311
  41.0 2.2 %propagate.10 = (f32[2,32,8,128]{3,2,1,0:T(8,128)S(1)}, f32[65,8,128]{2,1,0:T(8,128)S(1)}, f32[64,8,128]{2,1,0:T(8,128)S(1)}) custom-call(s32[2]{0:T(128)S(1)} %add_convert_fusion.refs_0_.flags, bf16[8,2,32,8,128]{4,3,2,1,0:T(8,128)(2,1)S(1)} %bitcast.29, bf16[8,2,32,8,128]{4,3,2,1,0:T(8,128)(2,1)S(1)} %collective-permute-done.refs_2_, ...), custom_call_target="tpu_custom_call" | custom-call | tf_op jit(solution)/shard_map/jit(propagate)/propagate/pallas_call | solution.py:156
  45.2 3.4 %collective-permute-done.14 = f16[65,8,128]{2,1,0:T(8,128)(2,1)S(1)} collective-permute-done((f16[65,8,128]{2,1,0:T(8,128)(2,1)S(1)}, f16[65,8,128]{2,1,0:T(8,128)(2,1)S(1)}, u32[]{:S(2)}, u32[]{:S(2)}) %collective-permute-start.14) | collective-permute-done | bytes 133152 | tf_op jit(solution)/shard_map/ppermute | solution.py:311
  48.7 2.9 %collective-permute-done.15 = f16[65,8,128]{2,1,0:T(8,128)(2,1)S(1)} collective-permute-done((f16[65,8,128]{2,1,0:T(8,128)(2,1)S(1)}, f16[65,8,128]{2,1,0:T(8,128)(2,1)S(1)}, u32[]{:S(2)}, u32[]{:S(2)}) %collective-permute-start.15) | collective-permute-done | bytes 133152 | tf_op jit(solution)/shard_map/ppermute | solution.py:311
  51.6 2.9 %propagate.15 = (f32[2,32,8,128]{3,2,1,0:T(8,128)S(1)}, f32[65,8,128]{2,1,0:T(8,128)S(1)}, f32[64,8,128]{2,1,0:T(8,128)}) custom-call(s32[2]{0:T(128)S(1)} %add_convert_fusion.refs_0_.flags, bf16[8,2,32,8,128]{4,3,2,1,0:T(8,128)(2,1)S(1)} %bitcast.31, bf16[8,2,32,8,128]{4,3,2,1,0:T(8,128)(2,1)S(1)} %collective-permute-done.refs_2_, ...), custom_call_target="tpu_custom_call" | custom-call | tf_op jit(solution)/shard_map/jit(propagate)/propagate/pallas_call | solution.py:156
  57.3 2.9 %propagate.11 = (f32[2,32,8,128]{3,2,1,0:T(8,128)S(1)}, f32[65,8,128]{2,1,0:T(8,128)S(1)}, f32[64,8,128]{2,1,0:T(8,128)}) custom-call(s32[2]{0:T(128)S(1)} %add_convert_fusion.refs_0_.flags, bf16[8,2,32,8,128]{4,3,2,1,0:T(8,128)(2,1)S(1)} %bitcast.33, bf16[8,2,32,8,128]{4,3,2,1,0:T(8,128)(2,1)S(1)} %collective-permute-done.refs_2_, ...), custom_call_target="tpu_custom_call" | custom-call | tf_op jit(solution)/shard_map/jit(propagate)/propagate/pallas_call | solution.py:156
  62.9 4.2 %collective-permute-done.17 = f16[65,8,128]{2,1,0:T(8,128)(2,1)S(1)} collective-permute-done((f16[65,8,128]{2,1,0:T(8,128)(2,1)S(1)}, f16[65,8,128]{2,1,0:T(8,128)(2,1)S(1)}, u32[]{:S(2)}, u32[]{:S(2)}) %collective-permute-start.17) | collective-permute-done | bytes 133152 | tf_op jit(solution)/shard_map/ppermute | solution.py:311
  67.1 1.4 %collective-permute-done.16 = f16[65,8,128]{2,1,0:T(8,128)(2,1)S(1)} collective-permute-done((f16[65,8,128]{2,1,0:T(8,128)(2,1)S(1)}, f16[65,8,128]{2,1,0:T(8,128)(2,1)S(1)}, u32[]{:S(2)}, u32[]{:S(2)}) %collective-permute-start.16) | collective-permute-done | bytes 133152 | tf_op jit(solution)/shard_map/ppermute | solution.py:311
  69.2 2.1 %collective-permute-done.8 = f16[65,8,128]{2,1,0:T(8,128)(2,1)S(1)} collective-permute-done((f16[65,8,128]{2,1,0:T(8,128)(2,1)S(1)}, f16[65,8,128]{2,1,0:T(8,128)(2,1)S(1)}, u32[]{:S(2)}, u32[]{:S(2)}) %collective-permute-start.8) | collective-permute-done | bytes 133152 | tf_op jit(solution)/shard_map/ppermute | solution.py:311
  71.4 1.8 %collective-permute-done.9 = f16[65,8,128]{2,1,0:T(8,128)(2,1)S(1)} collective-permute-done((f16[65,8,128]{2,1,0:T(8,128)(2,1)S(1)}, f16[65,8,128]{2,1,0:T(8,128)(2,1)S(1)}, u32[]{:S(2)}, u32[]{:S(2)}) %collective-permute-start.9) | collective-permute-done | bytes 133152 | tf_op jit(solution)/shard_map/ppermute | solution.py:311
  73.8 1.3 %collective-permute-done.18.refs_2_ = f32[1,32,8,128]{3,2,1,0:T(8,128)S(1)} collective-permute-done((f32[1,32,8,128]{3,2,1,0:T(8,128)S(1)}, f32[1,32,8,128]{3,2,1,0:T(8,128)S(1)}, u32[]{:S(2)}, u32[]{:S(2)}) %collective-permute-start.18) | collective-permute-done | bytes 131104 | tf_op jit(solution)/shard_map/ppermute | solution.py:306
  75.4 8.9 %all_to_all.11 = f32[32,1,128]{2,1,0:T(1,128)S(1)} all-to-all(f32[32,1,128]{2,1,0:T(1,128)S(1)} %bitcast.36), channel_id=1, replica_groups=mesh['seg'=16,'slab'=2] {'seg','slab'}, dimensions={0} | all-to-all | bytes 32768 | tf_op jit(solution)/shard_map/all_to_all | solution.py:380
  (77 shorter events, 20.2 us)
Async XLA Ops:
  0.0 3.4 %copy-start = (bf16[1,8,2,8,4096]{4,3,2,1,0:T(8,128)(2,1)S(1)}, bf16[1,8,2,8,4096]{4,3,2,1,0:T(8,128)(2,1)}, u32[]{:S(2)}) copy-start(bf16[1,8,2,8,4096]{4,3,2,1,0:T(8,128)(2,1)} %param.3) | copy-start | bytes 3145732
  0.0 3.4 %collective-permute-start = (bf16[8,2,32,8,128]{4,3,2,1,0:T(8,128)(2,1)}, bf16[8,2,32,8,128]{4,3,2,1,0:T(8,128)(2,1)S(1)}, u32[]{:S(2)}, u32[]{:S(2)}) collective-permute-start(bf16[8,2,32,8,128]{4,3,2,1,0:T(8,128)(2,1)} %bitcast.18), channel_id=1, source_target_pairs={{1,0},{0,1},{3,2},{2,3},{5,4},{4,5},{7,6},{6,7},{9,8},{8,9},{11,10... | collective-permute-start | bytes 3145736 | tf_op jit(solution)/shard_map/ppermute | solution.py:306
  1.6 1.8 %collective-permute-start.1 = (f32[2,32,8,128]{3,2,1,0:T(8,128)S(1)}, f32[2,32,8,128]{3,2,1,0:T(8,128)S(1)}, u32[]{:S(2)}, u32[]{:S(2)}) collective-permute-start(f32[2,32,8,128]{3,2,1,0:T(8,128)S(1)} %get-tuple-element.94), channel_id=1, source_target_pairs={{1,0},{0,1},{3,2},{2,3},{5,4},{4,5},{7,6},{6,7},{9,8},{8,9},{11,10... | collective-permute-start | bytes 786440 | tf_op jit(solution)/shard_map/ppermute | solution.py:306
  4.0 17.6 %collective-permute-start.11 = (f16[65,8,128]{2,1,0:T(8,128)(2,1)S(1)}, f16[65,8,128]{2,1,0:T(8,128)(2,1)S(1)}, u32[]{:S(2)}, u32[]{:S(2)}) collective-permute-start(f16[65,8,128]{2,1,0:T(8,128)(2,1)S(1)} %convert_element_type.118), channel_id=1, source_target_pairs={{30,0},{31,1}} | collective-permute-start | bytes 399368 | tf_op jit(solution)/shard_map/ppermute | solution.py:311
  7.5 13.5 %collective-permute-start.10 = (f16[65,8,128]{2,1,0:T(8,128)(2,1)S(1)}, f16[65,8,128]{2,1,0:T(8,128)(2,1)S(1)}, u32[]{:S(2)}, u32[]{:S(2)}) collective-permute-start(f16[65,8,128]{2,1,0:T(8,128)(2,1)S(1)} %convert_element_type.116), channel_id=1, source_target_pairs={{0,2},{2,4},{4,6},{6,8},{8,10},{10,12},{12,14},{14,16},{16,18},{18... | collective-permute-start | bytes 399368 | tf_op jit(solution)/shard_map/ppermute | solution.py:311
  12.6 12.7 %collective-permute-start.2 = (f16[65,8,128]{2,1,0:T(8,128)(2,1)S(1)}, f16[65,8,128]{2,1,0:T(8,128)(2,1)S(1)}, u32[]{:S(2)}, u32[]{:S(2)}) collective-permute-start(f16[65,8,128]{2,1,0:T(8,128)(2,1)S(1)} %convert_element_type.100), channel_id=1, source_target_pairs={{0,2},{2,4},{4,6},{6,8},{8,10},{10,12},{12,14},{14,16},{16,18},{18... | collective-permute-start | bytes 399368 | tf_op jit(solution)/shard_map/ppermute | solution.py:311
  14.1 12.0 %collective-permute-start.3 = (f16[65,8,128]{2,1,0:T(8,128)(2,1)S(1)}, f16[65,8,128]{2,1,0:T(8,128)(2,1)S(1)}, u32[]{:S(2)}, u32[]{:S(2)}) collective-permute-start(f16[65,8,128]{2,1,0:T(8,128)(2,1)S(1)} %convert_element_type.102), channel_id=1, source_target_pairs={{30,0},{31,1}} | collective-permute-start | bytes 399368 | tf_op jit(solution)/shard_map/ppermute | solution.py:311
  23.9 10.0 %collective-permute-start.12 = (f16[65,8,128]{2,1,0:T(8,128)(2,1)S(1)}, f16[65,8,128]{2,1,0:T(8,128)(2,1)S(1)}, u32[]{:S(2)}, u32[]{:S(2)}) collective-permute-start(f16[65,8,128]{2,1,0:T(8,128)(2,1)S(1)} %convert_element_type.120), channel_id=1, source_target_pairs={{0,2},{2,4},{4,6},{6,8},{8,10},{10,12},{12,14},{14,16},{16,18},{18... | collective-permute-start | bytes 399368 | tf_op jit(solution)/shard_map/ppermute | solution.py:311
  23.9 12.5 %collective-permute-start.13 = (f16[65,8,128]{2,1,0:T(8,128)(2,1)S(1)}, f16[65,8,128]{2,1,0:T(8,128)(2,1)S(1)}, u32[]{:S(2)}, u32[]{:S(2)}) collective-permute-start(f16[65,8,128]{2,1,0:T(8,128)(2,1)S(1)} %convert_element_type.122), channel_id=1, source_target_pairs={{30,0},{31,1}} | collective-permute-start | bytes 399368 | tf_op jit(solution)/shard_map/ppermute | solution.py:311
  28.4 12.3 %collective-permute-start.4 = (f16[65,8,128]{2,1,0:T(8,128)(2,1)S(1)}, f16[65,8,128]{2,1,0:T(8,128)(2,1)S(1)}, u32[]{:S(2)}, u32[]{:S(2)}) collective-permute-start(f16[65,8,128]{2,1,0:T(8,128)(2,1)S(1)} %convert_element_type.104), channel_id=1, source_target_pairs={{0,2},{2,4},{4,6},{6,8},{8,10},{10,12},{12,14},{14,16},{16,18},{18... | collective-permute-start | bytes 399368 | tf_op jit(solution)/shard_map/ppermute | solution.py:311
  29.0 12.0 %collective-permute-start.5 = (f16[65,8,128]{2,1,0:T(8,128)(2,1)S(1)}, f16[65,8,128]{2,1,0:T(8,128)(2,1)S(1)}, u32[]{:S(2)}, u32[]{:S(2)}) collective-permute-start(f16[65,8,128]{2,1,0:T(8,128)(2,1)S(1)} %convert_element_type.106), channel_id=1, source_target_pairs={{30,0},{31,1}} | collective-permute-start | bytes 399368 | tf_op jit(solution)/shard_map/ppermute | solution.py:311
  38.7 10.0 %collective-permute-start.14 = (f16[65,8,128]{2,1,0:T(8,128)(2,1)S(1)}, f16[65,8,128]{2,1,0:T(8,128)(2,1)S(1)}, u32[]{:S(2)}, u32[]{:S(2)}) collective-permute-start(f16[65,8,128]{2,1,0:T(8,128)(2,1)S(1)} %convert_element_type.124), channel_id=1, source_target_pairs={{0,2},{2,4},{4,6},{6,8},{8,10},{10,12},{12,14},{14,16},{16,18},{18... | collective-permute-start | bytes 399368 | tf_op jit(solution)/shard_map/ppermute | solution.py:311
  39.3 12.3 %collective-permute-start.15 = (f16[65,8,128]{2,1,0:T(8,128)(2,1)S(1)}, f16[65,8,128]{2,1,0:T(8,128)(2,1)S(1)}, u32[]{:S(2)}, u32[]{:S(2)}) collective-permute-start(f16[65,8,128]{2,1,0:T(8,128)(2,1)S(1)} %convert_element_type.126), channel_id=1, source_target_pairs={{30,0},{31,1}} | collective-permute-start | bytes 399368 | tf_op jit(solution)/shard_map/ppermute | solution.py:311
  43.3 14.0 %collective-permute-start.6 = (f16[65,8,128]{2,1,0:T(8,128)(2,1)S(1)}, f16[65,8,128]{2,1,0:T(8,128)(2,1)S(1)}, u32[]{:S(2)}, u32[]{:S(2)}) collective-permute-start(f16[65,8,128]{2,1,0:T(8,128)(2,1)S(1)} %convert_element_type.108), channel_id=1, source_target_pairs={{0,2},{2,4},{4,6},{6,8},{8,10},{10,12},{12,14},{14,16},{16,18},{18... | collective-permute-start | bytes 399368 | tf_op jit(solution)/shard_map/ppermute | solution.py:311
  43.9 13.3 %collective-permute-start.7 = (f16[65,8,128]{2,1,0:T(8,128)(2,1)S(1)}, f16[65,8,128]{2,1,0:T(8,128)(2,1)S(1)}, u32[]{:S(2)}, u32[]{:S(2)}) collective-permute-start(f16[65,8,128]{2,1,0:T(8,128)(2,1)S(1)} %convert_element_type.110), channel_id=1, source_target_pairs={{30,0},{31,1}} | collective-permute-start | bytes 399368 | tf_op jit(solution)/shard_map/ppermute | solution.py:311
  55.9 11.2 %collective-permute-start.17 = (f16[65,8,128]{2,1,0:T(8,128)(2,1)S(1)}, f16[65,8,128]{2,1,0:T(8,128)(2,1)S(1)}, u32[]{:S(2)}, u32[]{:S(2)}) collective-permute-start(f16[65,8,128]{2,1,0:T(8,128)(2,1)S(1)} %convert_element_type.130), channel_id=1, source_target_pairs={{30,0},{31,1}} | collective-permute-start | bytes 399368 | tf_op jit(solution)/shard_map/ppermute | solution.py:311
  57.2 11.4 %collective-permute-start.16 = (f16[65,8,128]{2,1,0:T(8,128)(2,1)S(1)}, f16[65,8,128]{2,1,0:T(8,128)(2,1)S(1)}, u32[]{:S(2)}, u32[]{:S(2)}) collective-permute-start(f16[65,8,128]{2,1,0:T(8,128)(2,1)S(1)} %convert_element_type.128), channel_id=1, source_target_pairs={{0,2},{2,4},{4,6},{6,8},{8,10},{10,12},{12,14},{14,16},{16,18},{18... | collective-permute-start | bytes 399368 | tf_op jit(solution)/shard_map/ppermute | solution.py:311
  60.3 11.1 %collective-permute-start.8 = (f16[65,8,128]{2,1,0:T(8,128)(2,1)S(1)}, f16[65,8,128]{2,1,0:T(8,128)(2,1)S(1)}, u32[]{:S(2)}, u32[]{:S(2)}) collective-permute-start(f16[65,8,128]{2,1,0:T(8,128)(2,1)S(1)} %convert_element_type.112), channel_id=1, source_target_pairs={{0,2},{2,4},{4,6},{6,8},{8,10},{10,12},{12,14},{14,16},{16,18},{18... | collective-permute-start | bytes 399368 | tf_op jit(solution)/shard_map/ppermute | solution.py:311
  61.6 11.5 %collective-permute-start.9 = (f16[65,8,128]{2,1,0:T(8,128)(2,1)S(1)}, f16[65,8,128]{2,1,0:T(8,128)(2,1)S(1)}, u32[]{:S(2)}, u32[]{:S(2)}) collective-permute-start(f16[65,8,128]{2,1,0:T(8,128)(2,1)S(1)} %convert_element_type.114), channel_id=1, source_target_pairs={{30,0},{31,1}} | collective-permute-start | bytes 399368 | tf_op jit(solution)/shard_map/ppermute | solution.py:311
  69.1 4.7 %collective-permute-start.19 = (f32[1,32,8,128]{3,2,1,0:T(8,128)S(1)}, f32[1,32,8,128]{3,2,1,0:T(8,128)S(1)}, u32[]{:S(2)}, u32[]{:S(2)}) collective-permute-start(f32[1,32,8,128]{3,2,1,0:T(8,128)S(1)} %get-tuple-element.92), channel_id=1, source_target_pairs={{1,0},{0,1},{3,2},{2,3},{5,4},{4,5},{7,6},{6,7},{9,8},{8,9},{11,10... | collective-permute-start | bytes 393224 | tf_op jit(solution)/shard_map/ppermute | solution.py:306
  73.8 1.4 %collective-permute-start.18 = (f32[1,32,8,128]{3,2,1,0:T(8,128)S(1)}, f32[1,32,8,128]{3,2,1,0:T(8,128)S(1)}, u32[]{:S(2)}, u32[]{:S(2)}) collective-permute-start(f32[1,32,8,128]{3,2,1,0:T(8,128)S(1)} %get-tuple-element.91), channel_id=1, source_target_pairs={{1,0},{0,1},{3,2},{2,3},{5,4},{4,5},{7,6},{6,7},{9,8},{8,9},{11,10... | collective-permute-start | bytes 393224 | tf_op jit(solution)/shard_map/ppermute | solution.py:306
